TPU v7x, 32 devices: a whole 2x2x4 slice. The times are simulated.
32 devices in a mesh: groups: 2 (over x), gz: 16 (over z, y, core).
Axes of the slice: x: 2, y: 2, z: 4, core: 2. Of those that a mesh axis runs over, the one named last changes fastest.
Arguments:
- labels: int32 [128, 256, 256], P(('groups', 'gz')), parts along dimension 0, may hold values from 0 to 7
- tensor_table: float32 [16, 7], P('groups'), parts along dimension 0, may hold values from -0.3 to 3.5, as said below
- bounds: float32 [4], P('groups'), parts along dimension 0, may hold values from 0 to 51, as said below
- right_side: float32 [128, 256, 256], P(('groups', 'gz')), parts along dimension 0, may hold values from -18 to 18
Outputs:
- solution: float32 [128, 256, 256], P(('groups', 'gz')), parts along dimension 0
- residual: float32 [128, 256, 256], P(('groups', 'gz')), parts along dimension 0
- residual_norm: float32 [2], P('groups'), parts along dimension 0
There are 2 independent parts, one for each index of `groups`. A program takes and returns all parts, laid end to end along the dimension named above; each array names one. Nothing has to cross between parts.
Inputs may be any that keep to these rules, and one draw needn't show every extreme that they name: `tensor_table`: every tensor is diagonally dominant: each diagonal component exceeds the sum of the magnitudes of its row's off-diagonal components by 0.4 or more; reactions are positive. 0 < bounds[0] < bounds[1], and bounds[1] is at least the largest eigenvalue of the operator.
All inputs are finite; a program needn't handle non-finite values.
Results may differ from a plain program's by a relative error of at most 0.00002.
Values sent between devices are 32-bit elements; how exact they have to be, the bound alone decides.
No kernel may reach another device: no remote copies, remote signals or barrier semaphores. Data moves between devices by JAX's collectives and lax.ppermute only.
A program may use at most 256 MiB of HBM per device.

v0:
```python
import jax
import jax.numpy as jnp
from jax import lax
from jax.sharding import PartitionSpec as P

ITERS = 3


lattice_steps = (
    (1, 0, 0),
    (0, 1, 0),
    (0, 0, 1),
    (1, 1, 0),
    (1, -1, 0),
    (1, 0, 1),
    (1, 0, -1),
    (0, 1, 1),
    (0, 1, -1),
)
x_links = (0, 3, 4, 5, 6)


def extended_2(cells, sides, width):
    for axis, dim in sides:
        count = lax.axis_size(axis)
        ends = count - 1
        head = lax.slice_in_dim(cells, 0, width, axis=dim)
        tail = lax.slice_in_dim(cells, cells.shape[dim] - width, cells.shape[dim], axis=dim)
        cells = jnp.concatenate(
            [
                lax.ppermute(tail, axis, [(i, (i + 1) % count) for i in range(ends)]),
                cells,
                lax.ppermute(head, axis, [((i + 1) % count, i) for i in range(ends)]),
            ],
            axis=dim,
        )
    return cells


def phase_weights(tensor_table):
    k_xx = tensor_table[:, 0]
    k_yy = tensor_table[:, 1]
    k_zz = tensor_table[:, 2]
    k_xy = tensor_table[:, 3]
    k_xz = tensor_table[:, 4]
    k_yz = tensor_table[:, 5]
    weights = [
        k_xx - jnp.abs(k_xy) - jnp.abs(k_xz),
        k_yy - jnp.abs(k_xy) - jnp.abs(k_yz),
        k_zz - jnp.abs(k_xz) - jnp.abs(k_yz),
        jnp.maximum(k_xy, 0.0),
        jnp.maximum(-k_xy, 0.0),
        jnp.maximum(k_xz, 0.0),
        jnp.maximum(-k_xz, 0.0),
        jnp.maximum(k_yz, 0.0),
        jnp.maximum(-k_yz, 0.0),
    ]
    return (weights, tensor_table[:, 6])


def cell_values(per_phase, labels):
    result = jnp.zeros(labels.shape, jnp.float32)
    for phase in range(per_phase.shape[0]):
        result = jnp.where(labels == phase, per_phase[phase], result)
    return result


def shifted(field, shift_x, shift_y, shift_z):
    length, rows, columns = field.shape
    padded = jnp.pad(field, ((0, 0), (1, 1), (1, 1)))
    return padded[
        1 + shift_x : length - 1 + shift_x,
        1 + shift_y : 1 + shift_y + rows,
        1 + shift_z : 1 + shift_z + columns,
    ]


def apply_operator(field, weights, reaction):
    middle_field = field[1:-1]
    image = reaction[1:-1] * middle_field
    for which, offset in enumerate(lattice_steps):
        own_weight = weights[which][1:-1]
        for direction_sign in (1, -1):
            step_x = direction_sign * offset[0]
            step_y = direction_sign * offset[1]
            step_z = direction_sign * offset[2]
            neighbour = shifted(field, step_x, step_y, step_z)
            link = 0.5 * (own_weight + shifted(weights[which], step_x, step_y, step_z))
            image = image + link * (middle_field - neighbour)
    return image


def pad_planes(field):
    return jnp.pad(field, ((1, 1), (0, 0), (0, 0)))


def per_device(labels, tensor_table, bounds, right_side):
    per_phase, reaction_phase = phase_weights(tensor_table)
    per_cell = [cell_values(table_column, labels) for table_column in per_phase]
    reaction_cell = cell_values(reaction_phase, labels)
    lower_bound = bounds[0]
    upper_bound = bounds[1]
    centre = (upper_bound + lower_bound) / 2.0
    spread = (upper_bound - lower_bound) / 2.0
    sigma_ratio = centre / spread
    factor = 1.0 / sigma_ratio
    solution = jnp.zeros_like(right_side)
    x_weights = jnp.stack([per_cell[which] for which in x_links])
    extended = extended_2(x_weights, (("gz", 1),), 1)
    weights = []
    for which in range(len(lattice_steps)):
        if which in x_links:
            weights.append(extended[x_links.index(which)])
        else:
            weights.append(pad_planes(per_cell[which]))
    reaction = pad_planes(reaction_cell)
    residual = right_side
    direction = right_side / centre
    for iteration in range(ITERS):
        solution = solution + direction
        direction_rim = extended_2(direction, (("gz", 0),), 1)
        image = apply_operator(direction_rim, weights, reaction)
        residual = residual - image
        new_factor = 1.0 / (2.0 * sigma_ratio - factor)
        direction = new_factor * factor * direction + 2.0 * new_factor / spread * residual
        factor = new_factor
    squares = lax.psum(jnp.sum(residual * residual), "gz")
    residual_norm = jnp.sqrt(squares).reshape(1)
    return (solution, residual, residual_norm)


def solution(mesh):
    return jax.shard_map(
        per_device,
        mesh=mesh,
        in_specs=(
            P(("groups", "gz"), None, None),
            P("groups", None),
            P("groups"),
            P(("groups", "gz"), None, None),
        ),
        out_specs=(P(("groups", "gz"), None, None), P(("groups", "gz"), None, None), P("groups")),
        check_vma=False,
    )
```

profile of v0, /device:TPU:0, one launch (start us, length us, event | category | flops | bytes accessed | tf_op | source)
XLA Modules:
  0.0 196.1 jit_solution(2028619274310046077)
XLA Ops:
  0.7 1.4 fusion.179
  3.4 1.3 broadcast_divide_fusion
  4.7 0.9 fusion.168
  5.6 2.4 %collective-permute-start.3 = (f32[1,256,256]{2,1,0:T(8,128)}, f32[1,256,256]{2,1,0:T(8,128)S(1)}, u32[]{:S(2)}, u32[]{:S(2)}) collective-permute-start(f32[1,256,256]{2,1,0:T(8,128)} %get-tuple-element.41), channel_id=1, source_target_pairs={{0,1},{1,2},{2,3},{3,4},{4,5},{5,6},{6,7},{7,8},{8,9},{9,10},{10,1... | collective-permute-start | bytes 786440 | tf_op jit(solution)/shard_map/ppermute | solution.py:31
  8.0 1.3 collective-permute-start.1
  12.0 6.4 %select_select_fusion.3 = (f32[4,256,256]{2,1,0:T(8,128)S(1)}, pred[4,256,256]{2,1,0:T(8,128)(4,1)S(1)}, pred[4,256,256]{2,1,0:T(8,128)(4,1)S(1)}, pred[4,256,25...) fusion(f32[]{:T(128)} %bitcast.64, f32[]{:T(128)} %bitcast.63, ...), kind=kLoop, calls=%fused_computation.258 | loop fusion | flops 4194304 | bytes 4194336 | tf_op jit(solution)/shard_map/jit(_where)/select_n | solution.py:64
  18.4 6.7 %bitcast_dynamic-update-slice_fusion.4 = (f32[5,4,256,256]{3,2,1,0:T(8,128)S(1)}, f32[4,256,256]{2,1,0:T(8,128)}) fusion(pred[4,256,256]{2,1,0:T(8,128)(4,1)S(1)} %get-tuple-element.20, pred[4,256,256]{2,1,0:T(8,128)(4,1)S(1)} %get-tuple-element.19, pred[4,256,256]{2,1,0:T(8,128)(4,1)S(1)} %get-tuple-element.18, ...), kind=kLoop, calls=%fused_computation.250 | loop fusion | flops 2097151 | bytes 4194336
  25.1 6.8 %bitcast_dynamic-update-slice_fusion.3 = (f32[5,4,256,256]{3,2,1,0:T(8,128)S(1)}, f32[4,256,256]{2,1,0:T(8,128)}) fusion(f32[5,4,256,256]{3,2,1,0:T(8,128)S(1)} %get-tuple-element.29, pred[4,256,256]{2,1,0:T(8,128)(4,1)S(1)} %get-tuple-element.20, pred[4,256,256]{2,1,0:T(8,128)(4,1)S(1)} %get-tuple-element.19, ...), kind=kLoop, calls=%fused_computation.249 | loop fusion | flops 2097152 | bytes 4194336
  31.9 6.8 %bitcast_dynamic-update-slice_fusion.2 = (f32[5,4,256,256]{3,2,1,0:T(8,128)S(1)}, f32[4,256,256]{2,1,0:T(8,128)}) fusion(f32[5,4,256,256]{3,2,1,0:T(8,128)S(1)} %get-tuple-element.27, pred[4,256,256]{2,1,0:T(8,128)(4,1)S(1)} %get-tuple-element.20, pred[4,256,256]{2,1,0:T(8,128)(4,1)S(1)} %get-tuple-element.19, ...), kind=kLoop, calls=%fused_computation.248 | loop fusion | flops 2097152 | bytes 4194336
  38.7 6.8 %bitcast_dynamic-update-slice_fusion.1 = (f32[5,4,256,256]{3,2,1,0:T(8,128)S(1)}, f32[4,256,256]{2,1,0:T(8,128)}) fusion(f32[5,4,256,256]{3,2,1,0:T(8,128)S(1)} %get-tuple-element.25, pred[4,256,256]{2,1,0:T(8,128)(4,1)S(1)} %get-tuple-element.20, pred[4,256,256]{2,1,0:T(8,128)(4,1)S(1)} %get-tuple-element.19, ...), kind=kLoop, calls=%fused_computation.247 | loop fusion | flops 2097152 | bytes 4194336
  45.5 6.8 %bitcast_dynamic-update-slice_fusion = (f32[5,4,256,256]{3,2,1,0:T(8,128)S(1)}, f32[4,256,256]{2,1,0:T(8,128)}) fusion(f32[5,4,256,256]{3,2,1,0:T(8,128)S(1)} %get-tuple-element.23, pred[4,256,256]{2,1,0:T(8,128)(4,1)S(1)} %get-tuple-element.20, pred[4,256,256]{2,1,0:T(8,128)(4,1)S(1)} %get-tuple-element.19, pred[4,256,256]{2,1,0:T(8,128)(4,1)S(1)} %get-tuple-element.18, ...), kind=kLoop, calls=%fused_computation.246 | loop fusion | flops 2097152 | bytes 4194336 | tf_op jit(solution)/shard_map/stack | solution.py:108
  52.3 1.9 fusion.165
  54.2 1.2 copy-done
  55.4 6.3 %collective-permute-start.2 = (f32[5,1,256,256]{3,2,1,0:T(8,128)}, f32[5,1,256,256]{3,2,1,0:T(8,128)}, u32[]{:S(2)}, u32[]{:S(2)}) collective-permute-start(f32[5,1,256,256]{3,2,1,0:T(8,128)} %get-tuple-element.35), channel_id=1, source_target_pairs={{0,1},{1,2},{2,3},{3,4},{4,5},{5,6},{6,7},{7,8},{8,9},{9,10},{10,1... | collective-permute-start | bytes 3932168 | tf_op jit(solution)/shard_map/ppermute | solution.py:31
  61.7 1.5 collective-permute-start
  63.8 6.8 %select_select_fusion.1 = f32[4,256,256]{2,1,0:T(8,128)} fusion(pred[4,256,256]{2,1,0:T(8,128)(4,1)S(1)} %get-tuple-element.20, pred[4,256,256]{2,1,0:T(8,128)(4,1)S(1)} %get-tuple-element.19, pred[4,256,256]{2,1,0:T(8,128)(4,1)S(1)} %get-tuple-element.18, pred[4,256,256]{2,1,0:T(8,128)(4,1)S(1)} %get-tuple-element.17, ...), kind=kLoop, calls=%fused_computation.256 | loop fusion | flops 2097152 | bytes 3145760 | tf_op jit(solution)/shard_map/jit(_where)/select_n | solution.py:64
  72.8 7.0 %select_select_fusion.2 = f32[4,256,256]{2,1,0:T(8,128)} fusion(pred[4,256,256]{2,1,0:T(8,128)(4,1)S(1)} %get-tuple-element.20, pred[4,256,256]{2,1,0:T(8,128)(4,1)S(1)} %get-tuple-element.19, pred[4,256,256]{2,1,0:T(8,128)(4,1)S(1)} %get-tuple-element.18, pred[4,256,256]{2,1,0:T(8,128)(4,1)S(1)} %get-tuple-element.17, ...), kind=kLoop, calls=%fused_computation.257 | loop fusion | flops 2097152 | bytes 3145760 | tf_op jit(solution)/shard_map/jit(_where)/select_n | solution.py:64
  79.8 7.0 %select_select_fusion = f32[4,256,256]{2,1,0:T(8,128)} fusion(pred[4,256,256]{2,1,0:T(8,128)(4,1)S(1)} %get-tuple-element.20, pred[4,256,256]{2,1,0:T(8,128)(4,1)S(1)} %get-tuple-element.19, pred[4,256,256]{2,1,0:T(8,128)(4,1)S(1)} %get-tuple-element.18, pred[4,256,256]{2,1,0:T(8,128)(4,1)S(1)} %get-tuple-element.17, ...), kind=kLoop, calls=%fused_computation.255 | loop fusion | flops 2097152 | bytes 3145760 | tf_op jit(solution)/shard_map/jit(_where)/select_n | solution.py:64
  86.8 1.7 select_maximum_fusion.4
  88.5 2.1 %maximum_bitcast_fusion.2 = (f32[6,256,256]{2,1,0:T(8,128)S(1)}, f32[6,256,256]{2,1,0:T(8,128)S(1)}, f32[6,256,256]{2,1,0:T(8,128)S(1)}, f32[6,256,256]{2,1,0:T(8,128)S(1)}) fusion(f32[5,1,256,256]{3,2,1,0:T(8,128)} %collective-permute-done, f32[5,4,256,256]{3,2,1,0:T(8,128)S(1)} %copy-done.1, f32[5,1,256,256]{3,2,1,0:T(8,128)} %collective-permute-done.2), kind=kLoop, calls=%fused_computation.34 | loop fusion | flops 3145728 | bytes 14155776 | tf_op jit(solution)/shard_map/squeeze | solution.py:113
  90.7 18.2 %multiply_add_fusion.1 = (f32[4,256,256]{2,1,0:T(8,128)}, f32[4,256,256]{2,1,0:T(8,128)}, f32[4,256,256]{2,1,0:T(8,128)}, f32[4,256,256]{2,1,0:T(8,128)}, f32[4,256,256]{2,1,0:T(8,128)}) fusion(f32[4,256,256]{2,1,0:T(8,128)} %copy-done.20, f32[]{:T(128)S(6)} %div.43, f32[]{:T(128)S(6)} %mul.305, f32[4,256,256]{2,1,0:T(8,128)} %param.7, ...), kind=kLoop, calls=%fused_computation.254 | loop fusion | flops 28049408 | bytes 50331688 | tf_op jit(solution)/shard_map/add | solution.py:125
  108.9 2.0 %fusion.167 = (f32[1,256,256]{2,1,0:T(8,128)}, f32[1,256,256]{2,1,0:T(8,128)}) fusion(f32[4,256,256]{2,1,0:T(8,128)} %get-tuple-element.7), kind=kLoop, calls=%fused_computation.285 | loop fusion | bytes 1048576 | tf_op jit(solution)/shard_map/slice | solution.py:28
  110.9 4.6 %collective-permute-start.5 = (f32[1,256,256]{2,1,0:T(8,128)}, f32[1,256,256]{2,1,0:T(8,128)S(1)}, u32[]{:S(2)}, u32[]{:S(2)}) collective-permute-start(f32[1,256,256]{2,1,0:T(8,128)} %get-tuple-element.39), channel_id=1, source_target_pairs={{0,1},{1,2},{2,3},{3,4},{4,5},{5,6},{6,7},{7,8},{8,9},{9,10},{10,1... | collective-permute-start | bytes 786440 | tf_op jit(solution)/shard_map/ppermute | solution.py:31
  115.5 1.3 collective-permute-start.4
  116.9 4.3 %collective-permute-done.4 = f32[1,256,256]{2,1,0:T(8,128)} collective-permute-done((f32[1,256,256]{2,1,0:T(8,128)}, f32[1,256,256]{2,1,0:T(8,128)}, u32[]{:S(2)}, u32[]{:S(2)}) %collective-permute-start.4) | collective-permute-done | bytes 262176 | tf_op jit(solution)/shard_map/ppermute | solution.py:33
  121.2 2.1 %select_maximum_fusion.2 = f32[6,258,258]{2,1,0:T(8,128)S(1)} fusion(f32[1,256,256]{2,1,0:T(8,128)} %collective-permute-done.4, f32[4,256,256]{2,1,0:T(8,128)} %get-tuple-element.7, f32[1,256,256]{2,1,0:T(8,128)S(1)} %collective-permute-done.5), kind=kLoop, calls=%fused_computation.22 | loop fusion | flops 5990760 | bytes 3170400 | tf_op jit(solution)/shard_map/concatenate | solution.py:29
  123.4 14.1 %multiply_add_fusion = (f32[4,256,256]{2,1,0:T(8,128)S(1)}, f32[4,256,256]{2,1,0:T(8,128)S(1)}) fusion(f32[4,256,256]{2,1,0:T(8,128)} %get-tuple-element.7, f32[]{:T(128)S(6)} %div.45, f32[]{:T(128)S(6)} %mul.348, f32[4,256,256]{2,1,0:T(8,128)} %get-tuple-element.8, f32[6,258,258]{2,1,0:T(8,128)S(1)} %select_maximum_fusion.2, ...), kind=kLoop, calls=%fused_computation.252 | loop fusion | flops 24379392 | bytes 39321608 | tf_op jit(solution)/shard_map/add | solution.py:125
  137.6 6.8 %collective-permute-start.7 = (f32[1,256,256]{2,1,0:T(8,128)S(1)}, f32[1,256,256]{2,1,0:T(8,128)S(1)}, u32[]{:S(2)}, u32[]{:S(2)}) collective-permute-start(f32[1,256,256]{2,1,0:T(8,128)S(1)} %get-tuple-element.37), channel_id=1, source_target_pairs={{0,1},{1,2},{2,3},{3,4},{4,5},{5,6},{6,7},{7,8},{8,9},{9,10},{10,1... | collective-permute-start | bytes 786440 | tf_op jit(solution)/shard_map/ppermute | solution.py:31
  144.4 1.5 collective-permute-start.6
  146.0 1.3 fusion.159
  149.9 10.1 %multiply_reduce_fusion = (f32[]{:T(128)}, f32[4,256,256]{2,1,0:T(8,128)}) fusion(f32[4,256,256]{2,1,0:T(8,128)S(1)} %get-tuple-element.6, f32[4,256,256]{2,1,0:T(8,128)S(1)} %get-tuple-element.5, f32[6,258,258]{2,1,0:T(8,128)S(1)} %select_maximum_fusion, f32[4,256,256]{2,1,0:T(8,128)S(1)} %copy-done.19, f32[4,256,256]{2,1,0:T(8,128)S(1)} %copy-done.17, ...), kind=kLoop, calls=%fused_computation.251 | loop fusion | flops 24117248 | bytes 38273028 | tf_op jit(solution)/shard_map/reduce_sum | solution.py:127
  160.0 34.3 %psum.7 = f32[]{:T(128)} all-reduce(f32[]{:T(128)} %get-tuple-element.3), channel_id=1, replica_groups=mesh['groups'=2,'gz'=16] {'gz'}, use_global_device_ids=true, to_apply=%region_1.2 | all-reduce | flops 1 | bytes 8 | tf_op jit(solution)/shard_map/psum | solution.py:127
  (77 shorter events, 6.7 us)
Async XLA Ops:
  0.6 8.7 %copy-start.30 = (f32[8,7]{1,0:T(8,128)S(1)}, f32[8,7]{1,0:T(8,128)}, u32[]{:S(2)}) copy-start(f32[8,7]{1,0:T(8,128)} %param.5) | copy-start | bytes 676
  0.6 11.4 %copy-start.29 = (s32[4,256,256]{2,1,0:T(8,128)S(1)}, s32[4,256,256]{2,1,0:T(8,128)}, u32[]{:S(2)}) copy-start(s32[4,256,256]{2,1,0:T(8,128)} %param.4) | copy-start | bytes 3145732
  4.7 7.3 %copy-start.20 = (f32[4,256,256]{2,1,0:T(8,128)}, f32[4,256,256]{2,1,0:T(8,128)S(1)}, u32[]{:S(2)}) copy-start(f32[4,256,256]{2,1,0:T(8,128)S(1)} %broadcast_divide_fusion) | copy-start | bytes 3145732
  5.6 81.1 %collective-permute-start.3 = (f32[1,256,256]{2,1,0:T(8,128)}, f32[1,256,256]{2,1,0:T(8,128)S(1)}, u32[]{:S(2)}, u32[]{:S(2)}) collective-permute-start(f32[1,256,256]{2,1,0:T(8,128)} %get-tuple-element.41), channel_id=1, source_target_pairs={{0,1},{1,2},{2,3},{3,4},{4,5},{5,6},{6,7},{7,8},{8,9},{9,10},{10,1... | collective-permute-start | bytes 786440 | tf_op jit(solution)/shard_map/ppermute | solution.py:31
  8.0 78.7 %collective-permute-start.1 = (f32[1,256,256]{2,1,0:T(8,128)}, f32[1,256,256]{2,1,0:T(8,128)}, u32[]{:S(2)}, u32[]{:S(2)}) collective-permute-start(f32[1,256,256]{2,1,0:T(8,128)} %get-tuple-element.42), channel_id=1, source_target_pairs={{1,0},{2,1},{3,2},{4,3},{5,4},{6,5},{7,6},{8,7},{9,8},{10,9},{11,1... | collective-permute-start | bytes 786440 | tf_op jit(solution)/shard_map/ppermute | solution.py:33
  18.4 72.2 %copy-start.11 = (f32[4,256,256]{2,1,0:T(8,128)}, f32[4,256,256]{2,1,0:T(8,128)S(1)}, u32[]{:S(2)}) copy-start(f32[4,256,256]{2,1,0:T(8,128)S(1)} %get-tuple-element.12) | copy-start | bytes 3145732
  55.4 33.1 %collective-permute-start.2 = (f32[5,1,256,256]{3,2,1,0:T(8,128)}, f32[5,1,256,256]{3,2,1,0:T(8,128)}, u32[]{:S(2)}, u32[]{:S(2)}) collective-permute-start(f32[5,1,256,256]{3,2,1,0:T(8,128)} %get-tuple-element.35), channel_id=1, source_target_pairs={{0,1},{1,2},{2,3},{3,4},{4,5},{5,6},{6,7},{7,8},{8,9},{9,10},{10,1... | collective-permute-start | bytes 3932168 | tf_op jit(solution)/shard_map/ppermute | solution.py:31
  61.7 26.8 %collective-permute-start = (f32[5,1,256,256]{3,2,1,0:T(8,128)}, f32[5,1,256,256]{3,2,1,0:T(8,128)}, u32[]{:S(2)}, u32[]{:S(2)}) collective-permute-start(f32[5,1,256,256]{3,2,1,0:T(8,128)} %get-tuple-element.36), channel_id=1, source_target_pairs={{1,0},{2,1},{3,2},{4,3},{5,4},{6,5},{7,6},{8,7},{9,8},{10,9},{11,1... | collective-permute-start | bytes 3932168 | tf_op jit(solution)/shard_map/ppermute | solution.py:33
  72.8 14.0 %copy-start.21 = (f32[4,256,256]{2,1,0:T(8,128)S(1)}, f32[4,256,256]{2,1,0:T(8,128)}, u32[]{:S(2)}) copy-start(f32[4,256,256]{2,1,0:T(8,128)} %copy-done.20) | copy-start | bytes 3145732
  79.8 8.7 %copy-start.1 = (f32[5,4,256,256]{3,2,1,0:T(8,128)S(1)}, f32[5,4,256,256]{3,2,1,0:T(8,128)}, u32[]{:S(2)}) copy-start(f32[5,4,256,256]{3,2,1,0:T(8,128)} %copy-done) | copy-start | bytes 15728644
  90.6 18.3 %copy-start.2 = (f32[6,256,256]{2,1,0:T(8,128)}, f32[6,256,256]{2,1,0:T(8,128)S(1)}, u32[]{:S(2)}) copy-start(f32[6,256,256]{2,1,0:T(8,128)S(1)} %get-tuple-element.31) | copy-start | bytes 4718596
  90.6 18.3 %copy-start.4 = (f32[6,256,256]{2,1,0:T(8,128)}, f32[6,256,256]{2,1,0:T(8,128)S(1)}, u32[]{:S(2)}) copy-start(f32[6,256,256]{2,1,0:T(8,128)S(1)} %get-tuple-element.32) | copy-start | bytes 4718596
  90.7 18.3 %copy-start.6 = (f32[6,256,256]{2,1,0:T(8,128)}, f32[6,256,256]{2,1,0:T(8,128)S(1)}, u32[]{:S(2)}) copy-start(f32[6,256,256]{2,1,0:T(8,128)S(1)} %get-tuple-element.33) | copy-start | bytes 4718596
  90.7 18.3 %copy-start.8 = (f32[6,256,256]{2,1,0:T(8,128)}, f32[6,256,256]{2,1,0:T(8,128)S(1)}, u32[]{:S(2)}) copy-start(f32[6,256,256]{2,1,0:T(8,128)S(1)} %get-tuple-element.34) | copy-start | bytes 4718596
  108.9 14.4 %copy-start.3 = (f32[6,256,256]{2,1,0:T(8,128)S(1)}, f32[6,256,256]{2,1,0:T(8,128)}, u32[]{:S(2)}) copy-start(f32[6,256,256]{2,1,0:T(8,128)} %copy-done.2) | copy-start | bytes 4718596
  108.9 14.4 %copy-start.5 = (f32[6,256,256]{2,1,0:T(8,128)S(1)}, f32[6,256,256]{2,1,0:T(8,128)}, u32[]{:S(2)}) copy-start(f32[6,256,256]{2,1,0:T(8,128)} %copy-done.4) | copy-start | bytes 4718596
  110.9 6.0 %collective-permute-start.5 = (f32[1,256,256]{2,1,0:T(8,128)}, f32[1,256,256]{2,1,0:T(8,128)S(1)}, u32[]{:S(2)}, u32[]{:S(2)}) collective-permute-start(f32[1,256,256]{2,1,0:T(8,128)} %get-tuple-element.39), channel_id=1, source_target_pairs={{0,1},{1,2},{2,3},{3,4},{4,5},{5,6},{6,7},{7,8},{8,9},{9,10},{10,1... | collective-permute-start | bytes 786440 | tf_op jit(solution)/shard_map/ppermute | solution.py:31
  115.5 5.7 %collective-permute-start.4 = (f32[1,256,256]{2,1,0:T(8,128)}, f32[1,256,256]{2,1,0:T(8,128)}, u32[]{:S(2)}, u32[]{:S(2)}) collective-permute-start(f32[1,256,256]{2,1,0:T(8,128)} %get-tuple-element.40), channel_id=1, source_target_pairs={{1,0},{2,1},{3,2},{4,3},{5,4},{6,5},{7,6},{8,7},{9,8},{10,9},{11,1... | collective-permute-start | bytes 786440 | tf_op jit(solution)/shard_map/ppermute | solution.py:33
  116.9 6.4 %copy-start.7 = (f32[6,256,256]{2,1,0:T(8,128)S(1)}, f32[6,256,256]{2,1,0:T(8,128)}, u32[]{:S(2)}) copy-start(f32[6,256,256]{2,1,0:T(8,128)} %copy-done.6) | copy-start | bytes 4718596
  116.9 6.4 %copy-start.28 = (f32[1,256,256]{2,1,0:T(8,128)}, f32[1,256,256]{2,1,0:T(8,128)S(1)}, u32[]{:S(2)}) copy-start(f32[1,256,256]{2,1,0:T(8,128)S(1)} %collective-permute-done.5) | copy-start | bytes 786436
  123.3 22.6 %copy-start.10 = (f32[4,256,256]{2,1,0:T(8,128)S(1)}, f32[4,256,256]{2,1,0:T(8,128)}, u32[]{:S(2)}) copy-start(f32[4,256,256]{2,1,0:T(8,128)} %get-tuple-element.7) | copy-start | bytes 3145732
  123.4 22.6 %copy-start.22 = (f32[4,256,256]{2,1,0:T(8,128)S(1)}, f32[4,256,256]{2,1,0:T(8,128)}, u32[]{:S(2)}) copy-start(f32[4,256,256]{2,1,0:T(8,128)} %param.7) | copy-start | bytes 3145732
  123.4 26.0 %copy-start.19 = (f32[4,256,256]{2,1,0:T(8,128)S(1)}, f32[4,256,256]{2,1,0:T(8,128)}, u32[]{:S(2)}) copy-start(f32[4,256,256]{2,1,0:T(8,128)} %select_select_fusion) | copy-start | bytes 3145732
  123.4 26.0 %copy-start.23 = (f32[4,256,256]{2,1,0:T(8,128)S(1)}, f32[4,256,256]{2,1,0:T(8,128)}, u32[]{:S(2)}) copy-start(f32[4,256,256]{2,1,0:T(8,128)} %get-tuple-element.9) | copy-start | bytes 3145732
  123.4 26.0 %copy-start.24 = (f32[4,256,256]{2,1,0:T(8,128)S(1)}, f32[4,256,256]{2,1,0:T(8,128)}, u32[]{:S(2)}) copy-start(f32[4,256,256]{2,1,0:T(8,128)} %get-tuple-element.10) | copy-start | bytes 3145732
  123.4 26.0 %copy-start.25 = (f32[4,256,256]{2,1,0:T(8,128)S(1)}, f32[4,256,256]{2,1,0:T(8,128)}, u32[]{:S(2)}) copy-start(f32[4,256,256]{2,1,0:T(8,128)} %get-tuple-element.11) | copy-start | bytes 3145732
  137.6 11.9 %copy-start.18 = (f32[4,256,256]{2,1,0:T(8,128)S(1)}, f32[4,256,256]{2,1,0:T(8,128)}, u32[]{:S(2)}) copy-start(f32[4,256,256]{2,1,0:T(8,128)} %select_select_fusion.2) | copy-start | bytes 3145732
  137.6 9.7 %collective-permute-start.7 = (f32[1,256,256]{2,1,0:T(8,128)S(1)}, f32[1,256,256]{2,1,0:T(8,128)S(1)}, u32[]{:S(2)}, u32[]{:S(2)}) collective-permute-start(f32[1,256,256]{2,1,0:T(8,128)S(1)} %get-tuple-element.37), channel_id=1, source_target_pairs={{0,1},{1,2},{2,3},{3,4},{4,5},{5,6},{6,7},{7,8},{8,9},{9,10},{10,1... | collective-permute-start | bytes 786440 | tf_op jit(solution)/shard_map/ppermute | solution.py:31
  144.4 3.4 %collective-permute-start.6 = (f32[1,256,256]{2,1,0:T(8,128)S(1)}, f32[1,256,256]{2,1,0:T(8,128)S(1)}, u32[]{:S(2)}, u32[]{:S(2)}) collective-permute-start(f32[1,256,256]{2,1,0:T(8,128)S(1)} %get-tuple-element.38), channel_id=1, source_target_pairs={{1,0},{2,1},{3,2},{4,3},{5,4},{6,5},{7,6},{8,7},{9,8},{10,9},{11,1... | collective-permute-start | bytes 786440 | tf_op jit(solution)/shard_map/ppermute | solution.py:33
  145.9 3.5 %copy-start.14 = (f32[4,256,256]{2,1,0:T(8,128)S(1)}, f32[4,256,256]{2,1,0:T(8,128)}, u32[]{:S(2)}) copy-start(f32[4,256,256]{2,1,0:T(8,128)} %get-tuple-element.26) | copy-start | bytes 3145732
  146.0 3.5 %copy-start.15 = (f32[4,256,256]{2,1,0:T(8,128)S(1)}, f32[4,256,256]{2,1,0:T(8,128)}, u32[]{:S(2)}) copy-start(f32[4,256,256]{2,1,0:T(8,128)} %get-tuple-element.24) | copy-start | bytes 3145732
  146.0 3.5 %copy-start.16 = (f32[4,256,256]{2,1,0:T(8,128)S(1)}, f32[4,256,256]{2,1,0:T(8,128)}, u32[]{:S(2)}) copy-start(f32[4,256,256]{2,1,0:T(8,128)} %get-tuple-element.22) | copy-start | bytes 3145732
  (7 other events, 15.2 us)
where the time goes:
time: 197 us; the launch traced here: 196 us
  other arithmetic  113 us (57%)
  blocking collectives  34.3 us (17%)
  starting transfers between devices  25.6 us (13%)
  local copies, waits for them, and re-layouts  12.7 us (6%)
  between operations  5.93 us (3%)
  waiting for transfers between devices  4.89 us (2%)
    psum x1, blocking collectives, per_device(): squares = lax.psum(jnp.sum(residual * residual), 'gz')  34.3 us
    add x2, other arithmetic, per_device(): new_factor * factor * direction + 2.0 * new_factor / spread * residual  32.3 us
    select_n x4, other arithmetic, cell_values(): result = jnp.where(labels == phase, per_phase[phase], result)  27.2 us
    unnamed x4, other arithmetic  27 us
    ppermute x4, starting transfers between devices, extended_2(): lax.ppermute(tail, axis, [(i, (i + 1) % count) for i in range(ends)])  20 us
    reduce_sum x1, other arithmetic, per_device(): squares = lax.psum(jnp.sum(residual * residual), 'gz')  10.1 us
    another operation x1, other arithmetic, per_device(): x_weights = jnp.stack([per_cell[which] for which in x_links])  6.79 us
    ppermute x4, starting transfers between devices, extended_2(): lax.ppermute(head, axis, [((i + 1) % count, i) for i in range(ends)])  5.56 us
  transfers between devices with their start and end apart: 8, of which 2 were waited for; matrix products, arithmetic and copies ran while one was open for 36% of the time, Pallas kernels for 0%

commit v1 on v0

v1 whole, which is shorter than its diff:
```python
import functools

import jax
import jax.numpy as jnp
from jax import lax
from jax.experimental import pallas as pl
from jax.experimental.pallas import tpu as pltpu
from jax.sharding import PartitionSpec as P

ITERS = 3
PHASES = 8
OUTSIDE = 8
BASE = 9
LANES = 128
SUB = 8
PAD = 8
HALO = 2

steps = (
    (1, 0, 0),
    (0, 1, 0),
    (0, 0, 1),
    (1, 1, 0),
    (1, -1, 0),
    (1, 0, 1),
    (1, 0, -1),
    (0, 1, 1),
    (0, 1, -1),
)
links = tuple((which, sign) for which in range(len(steps)) for sign in (1, -1))


def splat(value):
    return jnp.full((SUB, LANES), value, jnp.float32)


def look_up(table, index):
    return jnp.take_along_axis(table, index, axis=1, mode="promise_in_bounds")


def chebyshev(bounds_ref):
    lower, upper = splat(bounds_ref[0]), splat(bounds_ref[1])
    centre = (upper + lower) / 2.0
    half = (upper - lower) / 2.0
    sigma = centre / half
    rho = 1.0 / sigma
    factors = []
    for _ in range(ITERS):
        rho_new = 1.0 / (2.0 * sigma - rho)
        factors.append((rho_new * rho, 2.0 * rho_new / half))
        rho = rho_new
    return 1.0 / centre, factors


def link_tables(table_ref, flip):
    lane = lax.broadcasted_iota(jnp.int32, (SUB, LANES), 1)
    own, other = lane // BASE, lane % BASE
    turn = jnp.where(splat(flip.astype(jnp.float32)) > 0.5, -1.0, 1.0)
    columns = []
    for column in range(7):
        first = jnp.zeros((SUB, LANES), jnp.float32)
        second = jnp.zeros((SUB, LANES), jnp.float32)
        single = jnp.zeros((SUB, LANES), jnp.float32)
        for phase in range(PHASES):
            value = splat(table_ref[phase, column])
            first = jnp.where(own == phase, value, first)
            second = jnp.where(other == phase, value, second)
            single = jnp.where(lane == phase, value, single)
        if column in (3, 4):
            first, second = first * turn, second * turn
        columns.append((first, second, single))

    def weights(k):
        k_xx, k_yy, k_zz, k_xy, k_xz, k_yz = k
        return [
            k_xx - jnp.abs(k_xy) - jnp.abs(k_xz),
            k_yy - jnp.abs(k_xy) - jnp.abs(k_yz),
            k_zz - jnp.abs(k_xz) - jnp.abs(k_yz),
            jnp.maximum(k_xy, 0.0),
            jnp.maximum(-k_xy, 0.0),
            jnp.maximum(k_xz, 0.0),
            jnp.maximum(-k_xz, 0.0),
            jnp.maximum(k_yz, 0.0),
            jnp.maximum(-k_yz, 0.0),
        ]

    pairs = zip(weights([c[0] for c in columns[:6]]), weights([c[1] for c in columns[:6]]))
    return [0.5 * (a + b) for a, b in pairs], columns[6][2]


def put_lane_shifted(trio, plane, row, values, fill):
    lane = lax.broadcasted_iota(jnp.int32, (SUB, LANES), 1)
    count = len(values)
    up = [pltpu.roll(value, LANES - 1, 1) for value in values]
    down = [pltpu.roll(value, 1, 1) for value in values]
    edge = jnp.full((SUB, LANES), fill, values[0].dtype)
    for c in range(count):
        right = up[c + 1] if c + 1 < count else edge
        left = down[c - 1] if c else edge
        trio[0][plane, c, pl.ds(row + PAD, SUB), :] = values[c]
        trio[1][plane, c, pl.ds(row + PAD, SUB), :] = jnp.where(lane == LANES - 1, right, up[c])
        trio[2][plane, c, pl.ds(row + PAD, SUB), :] = jnp.where(lane == 0, left, down[c])


def fill_rims(trio, plane, tiles, rows, fill):
    edge = jnp.full((PAD, LANES), fill, trio[0].dtype)
    for ref in trio:
        for c in range(tiles):
            ref[plane, c, pl.ds(0, PAD), :] = edge
            ref[plane, c, pl.ds(rows + PAD, PAD), :] = edge


def neighbour(trio, plane, c, row, step):
    dx, dy, dz = step
    return trio[dz % 3][plane + dx, c, pl.ds(row + PAD + dy, SUB), :]


def signed(link):
    which, sign = link
    return tuple(sign * part for part in steps[which])


def each_block(rows, body, unroll=2):
    def step(k, carry):
        return body(pl.multiple_of(k * SUB, SUB), carry)

    return functools.partial(lax.fori_loop, 0, rows // SUB, step, unroll=unroll)


def set_labels(trio, plane, tiles, rows, read):
    fill_rims(trio, plane, tiles, rows, OUTSIDE)

    def body(row, carry):
        put_lane_shifted(trio, plane, row, [read(c, row) for c in range(tiles)], OUTSIDE)
        return carry

    each_block(rows, body)(0)


def set_links(labels, link_ref, plane, out, tiles, rows, tables, reaction):
    for c in range(tiles):

        def body(row, carry):
            mine = labels[0][plane, c, pl.ds(row + PAD, SUB), :]
            base = mine * BASE
            total = look_up(reaction, mine)
            for k, link in enumerate(links):
                value = look_up(tables[link[0]], base + neighbour(labels, plane, c, row, signed(link)))
                link_ref[out, k, c, pl.ds(row, SUB), :] = value
                total = total + value
            link_ref[out, len(links), c, pl.ds(row, SUB), :] = total
            return carry

        each_block(rows, body)(0)


def operator(field, link_ref, plane, at, c, row):
    where = pl.ds(row, SUB)
    parts = [link_ref[at, len(links), c, where, :] * neighbour(field, plane, c, row, (0, 0, 0))]
    sums = [None] * 3
    for k, link in enumerate(links):
        term = link_ref[at, k, c, where, :] * neighbour(field, plane, c, row, signed(link))
        sums[k % 3] = term if sums[k % 3] is None else sums[k % 3] + term
    return parts[0] - ((sums[0] + sums[1]) + sums[2])


def tile(ref, plane, c, row):
    return ref[plane, pl.ds(row, SUB), pl.ds(c * LANES, LANES)]


def inner_kernel(depth, labels_ref, right_ref, table_ref, bounds_ref, near_ref, far_ref, *scratch):
    labels, field, link_ref = scratch[:3], scratch[3:6], scratch[6]
    rows, tiles = labels_ref.shape[1], labels_ref.shape[2] // LANES
    flip = lax.axis_index("gz") % 2
    inverse, factors = chebyshev(bounds_ref)
    tables, reaction = link_tables(table_ref, flip)
    first, second = factors[0]

    for q in range(depth):
        source = jnp.where(flip == 1, depth - 1 - q, q)
        set_labels(labels, q, tiles, rows, lambda c, row: tile(labels_ref, source, c, row))
        fill_rims(field, q, tiles, rows, 0.0)

        def body(row, carry):
            values = [tile(right_ref, source, c, row) * inverse for c in range(tiles)]
            put_lane_shifted(field, q, row, values, 0.0)
            return carry

        each_block(rows, body)(0)

    for q, out in ((1, near_ref), (depth - 2, far_ref)):
        set_links(labels, link_ref, q, 0, tiles, rows, tables, reaction)
        source = jnp.where(flip == 1, depth - 1 - q, q)
        for c in range(tiles):

            def body(row, carry):
                rest = tile(right_ref, source, c, row) - operator(field, link_ref, q, 0, c, row)
                here = neighbour(field, q, c, row, (0, 0, 0))
                out[0, pl.ds(row, SUB), pl.ds(c * LANES, LANES)] = first * here + second * rest
                return carry

            each_block(rows, body)(0)


def main_kernel(
    depth,
    labels_ref,
    right_ref,
    table_ref,
    bounds_ref,
    labels_near_ref,
    right_near_ref,
    direction_near_ref,
    labels_far_ref,
    right_far_ref,
    direction_far_ref,
    solution_ref,
    residual_ref,
    squares_ref,
    *scratch,
):
    labels, field, link_ref, rest_ref = scratch[:3], scratch[3:6], scratch[6], scratch[7]
    rows, tiles = labels_ref.shape[1], labels_ref.shape[2] // LANES
    place, count = lax.axis_index("gz"), lax.axis_size("gz")
    flip = place % 2
    joined = jnp.logical_and(place > 0, place < count - 1)
    joined_mask = splat(joined.astype(jnp.float32))
    inverse, factors = chebyshev(bounds_ref)
    tables, reaction = link_tables(table_ref, flip)

    own = range(depth)
    inner_halo = (-1, depth)
    outer_halo = (-HALO, depth + 1)

    def source(q):
        if q in own:
            return labels_ref, right_ref, jnp.where(flip == 1, depth - 1 - q, q)
        far = q >= depth
        distance = q - depth if far else -1 - q
        order = distance == 0
        index = jnp.where(flip == (1 if far else 0), 1 if order else 0, 0 if order else 1)
        if far:
            return labels_far_ref, right_far_ref, index
        return labels_near_ref, right_near_ref, index

    for q in range(-HALO, depth + HALO):
        labels_from, right_from, index = source(q)

        def read(c, row):
            value = tile(labels_from, index, c, row)
            return jnp.where(joined, value, OUTSIDE) if q < 0 else value

        set_labels(labels, q + HALO, tiles, rows, read)
        fill_rims(field, q + HALO, tiles, rows, 0.0)

        def body(row, carry):
            values = [tile(right_from, index, c, row) * inverse for c in range(tiles)]
            put_lane_shifted(field, q + HALO, row, values, 0.0)
            return carry

        each_block(rows, body)(0)

    for q in range(-1, depth + 1):
        set_links(labels, link_ref, q + HALO, q + 1, tiles, rows, tables, reaction)

    for iteration in range(ITERS):
        last = iteration == ITERS - 1
        planes = own if last else range(-1, depth + 1)
        total = jnp.zeros((SUB, LANES), jnp.float32)
        for q in planes:
            _, right_from, index = source(q)
            for c in range(tiles):

                def body(row, carry):
                    image = operator(field, link_ref, q + HALO, q + 1, c, row)
                    if iteration == 0:
                        rest = tile(right_from, index, c, row) - image
                    else:
                        rest = rest_ref[q + 1, c, pl.ds(row, SUB), :] - image
                    if q < 0:
                        rest = rest * joined_mask
                    if last:
                        residual_ref[index, pl.ds(row, SUB), pl.ds(c * LANES, LANES)] = rest
                        return carry + rest * rest
                    rest_ref[q + 1, c, pl.ds(row, SUB), :] = rest
                    return carry

                total = each_block(rows, body)(total)
        if last:
            squares_ref[0, 0] = jnp.sum(total)
            break
        first, second = factors[iteration]
        for q in planes:
            _, _, index = source(q)

            def body(row, carry):
                values = []
                for c in range(tiles):
                    here = neighbour(field, q + HALO, c, row, (0, 0, 0))
                    value = first * here + second * rest_ref[q + 1, c, pl.ds(row, SUB), :]
                    values.append(value)
                    if q in own:
                        at = (index, pl.ds(row, SUB), pl.ds(c * LANES, LANES))
                        before = here if iteration == 0 else solution_ref[at]
                        solution_ref[at] = before + value
                put_lane_shifted(field, q + HALO, row, values, 0.0)
                return carry

            each_block(rows, body)(0)
        if iteration == 0:
            for q, received in zip(outer_halo, (direction_near_ref, direction_far_ref)):

                def body(row, carry):
                    put_lane_shifted(field, q + HALO, row, [tile(received, 0, c, row) for c in range(tiles)], 0.0)
                    return carry

                each_block(rows, body)(0)


def per_device(labels, tensor_table, bounds, right_side):
    depth, rows, columns = labels.shape
    tiles = columns // LANES
    count = lax.axis_size("gz")
    place = lax.axis_index("gz")
    odd = place % 2

    vmem = pl.BlockSpec(memory_space=pltpu.VMEM)
    smem = pl.BlockSpec(memory_space=pltpu.SMEM)

    def scratch(planes, linked):
        padded = (planes, tiles, rows + 2 * PAD, LANES)
        return (
            [pltpu.VMEM(padded, jnp.int32)] * 3
            + [pltpu.VMEM(padded, jnp.float32)] * 3
            + [pltpu.VMEM((linked, len(links) + 1, tiles, rows, LANES), jnp.float32)]
        )

    inside = [(i, i ^ 1) for i in range(count)]
    across = [(i, i + 1) for i in range(1, count - 1, 2)]
    across += [(j, i) for i, j in across]
    near_start = odd * (depth - HALO)
    far_start = (1 - odd) * (depth - HALO)

    def send(array, start, pairs):
        return lax.ppermute(lax.dynamic_slice_in_dim(array, start, HALO, 0), "gz", pairs)

    labels_near = send(labels, near_start, across)
    right_near = send(right_side, near_start, across)
    labels_far = send(labels, far_start, inside)
    right_far = send(right_side, far_start, inside)

    plane = jax.ShapeDtypeStruct((1, rows, columns), jnp.float32)
    near, far = pl.pallas_call(
        functools.partial(inner_kernel, depth),
        out_shape=(plane, plane),
        in_specs=[vmem, vmem, smem, smem],
        out_specs=(vmem, vmem),
        scratch_shapes=scratch(depth, 1),
        name="inner",
    )(labels, right_side, tensor_table, bounds)
    direction_near = lax.ppermute(near, "gz", across)
    direction_far = lax.ppermute(far, "gz", inside)

    block = jax.ShapeDtypeStruct(right_side.shape, jnp.float32)
    solved, residual, squares = pl.pallas_call(
        functools.partial(main_kernel, depth),
        out_shape=(block, block, jax.ShapeDtypeStruct((1, 1), jnp.float32)),
        in_specs=[vmem, vmem, smem, smem] + [vmem] * 6,
        out_specs=(vmem, vmem, smem),
        scratch_shapes=scratch(depth + 2 * HALO, depth + 2)
        + [pltpu.VMEM((depth + 2, tiles, rows, LANES), jnp.float32)],
        compiler_params=pltpu.CompilerParams(vmem_limit_bytes=60 * 1024 * 1024),
        name="main",
    )(
        labels,
        right_side,
        tensor_table,
        bounds,
        labels_near,
        right_near,
        direction_near,
        labels_far,
        right_far,
        direction_far,
    )
    gathered = lax.all_to_all(jnp.broadcast_to(squares.reshape(1), (count,)), "gz", 0, 0, tiled=True)
    return solved, residual, jnp.sqrt(jnp.sum(gathered)).reshape(1)


def solution(mesh):
    whole = P(("groups", "gz"), None, None)
    return jax.shard_map(
        per_device,
        mesh=mesh,
        in_specs=(whole, P("groups", None), P("groups"), whole),
        out_specs=(whole, whole, P("groups")),
        check_vma=False,
    )
```

time: 197 us -> 166 us (0.84)
  Pallas kernels: 0 us -> 115 us
  other arithmetic: 113 us -> 0.62 us
  blocking collectives: 34.3 us -> 20.8 us
  local copies, waits for them, and re-layouts: 12.7 us -> 2.79 us
  waiting for transfers between devices: 4.89 us -> 1.18 us
  between operations: 5.93 us -> 2.63 us
  starting transfers between devices: 25.6 us -> 22.4 us
    pallas_call x0 -> x2, Pallas kernels: none -> 115 us  [the longest x1 89.6 us: per_device(): pl.pallas_call(functools.partial(main_kernel, depth), out_shape=(block, b...]
    psum x1 -> x0, blocking collectives: 34.3 us -> none  [per_device(): squares = lax.psum(jnp.sum(residual * residual), 'gz')]
    add x3 -> x0, other arithmetic: 33.6 us -> none  [the longest x2 32.3 us: per_device(): new_factor * factor * direction + 2.0 * new_factor / spread * residual]
    select_n x4 -> x0, other arithmetic: 27.2 us -> none  [cell_values(): result = jnp.where(labels == phase, per_phase[phase], result)]
    unnamed x4 -> x0, other arithmetic: 27 us -> none
    all_to_all x0 -> x1, blocking collectives: none -> 20.8 us  [per_device(): lax.all_to_all(jnp.broadcast_to(squares.reshape(1), (count,)), 'gz', 0, 0...]
    slice x11 -> x0, local copies, waits for them, and re-layouts: 10.2 us -> none  [the longest x4 4.85 us: extended_2(): lax.slice_in_dim(cells, cells.shape[dim] - width, cells.shape[dim], axis=...]
    reduce_sum x1, other arithmetic: 10.1 us -> 0.62 us  [per_device(): return (solved, residual, jnp.sqrt(jnp.sum(gathered)).reshape(1))]
  transfers between devices with their start and end apart: 8 -> 6, of which waited for: 2 -> 1; matrix products, arithmetic and copies ran while one was open for 36% -> 0% of each run, Pallas kernels for 0% -> 0%
where the time goes in v1:
time: 166 us
  Pallas kernels  115 us (69%)
  starting transfers between devices  22.4 us (13%)
  blocking collectives  20.8 us (13%)
  local copies, waits for them, and re-layouts  2.79 us (2%)
  between operations  2.63 us (2%)
    pallas_call x1, Pallas kernels, per_device(): pl.pallas_call(functools.partial(main_kernel, depth), out_shape=(block, b...  89.6 us
    pallas_call x1, Pallas kernels, per_device(): pl.pallas_call(functools.partial(inner_kernel, depth), out_shape=(plane,...  25.6 us
    all_to_all x1, blocking collectives, per_device(): lax.all_to_all(jnp.broadcast_to(squares.reshape(1), (count,)), 'gz', 0, 0...  20.8 us
    ppermute x1, starting transfers between devices, per_device(): direction_far = lax.ppermute(far, 'gz', inside)  12.9 us
    ppermute x4, starting transfers between devices, send(): lax.ppermute(lax.dynamic_slice_in_dim(array, start, HALO, 0), 'gz', pairs)  8.82 us
  transfers between devices with their start and end apart: 6, of which 1 were waited for; matrix products, arithmetic and copies ran while one was open for 0% of the time, Pallas kernels for 0%

profile of v1, /device:TPU:0, one launch (start us, length us, event | category | flops | bytes accessed | tf_op | source)
XLA Modules:
  0.0 165.6 jit_solution(14172329681599321273)
XLA Ops:
  0.6 0.0 copy-start
  0.6 25.6 %inner.1 = (f32[1,256,256]{2,1,0:T(8,128)}, f32[1,256,256]{2,1,0:T(8,128)}) custom-call(s32[4,256,256]{2,1,0:T(8,128)} %labels_ref.3, f32[4,256,256]{2,1,0:T(8,128)} %right_ref.3, f32[8,7]{1,0:T(8,128)} %table_ref.3, f32[2]{0:T(128)} %bounds_ref.3), custom_call_target="tpu_custom_call" | custom-call | tf_op jit(solution)/shard_map/inner/pallas_call | solution.py:353
  26.3 0.7 collective-permute-start.2
  27.0 0.0 copy-done
  27.0 0.0 copy-start.1
  27.0 0.1 constant_dynamic-slice_fusion.1
  27.1 4.4 %collective-permute-start.3 = (s32[2,256,256]{2,1,0:T(8,128)S(1)}, s32[2,256,256]{2,1,0:T(8,128)S(1)}, u32[]{:S(2)}, u32[]{:S(2)}) collective-permute-start(s32[2,256,256]{2,1,0:T(8,128)S(1)} %get-tuple-element.15), channel_id=1, source_target_pairs={{0,1},{1,0},{2,3},{3,2},{4,5},{5,4},{6,7},{7,6},{8,9},{9,8},{10,11... | collective-permute-start | bytes 1572872 | tf_op jit(solution)/shard_map/ppermute | solution.py:345
  31.5 0.8 collective-permute-start
  32.3 0.0 copy-done.1
  32.3 0.1 constant_dynamic-slice_fusion
  32.4 2.9 %collective-permute-start.4 = (f32[2,256,256]{2,1,0:T(8,128)S(1)}, f32[2,256,256]{2,1,0:T(8,128)S(1)}, u32[]{:S(2)}, u32[]{:S(2)}) collective-permute-start(f32[2,256,256]{2,1,0:T(8,128)S(1)} %get-tuple-element.13), channel_id=1, source_target_pairs={{0,1},{1,0},{2,3},{3,2},{4,5},{5,4},{6,7},{7,6},{8,9},{9,8},{10,11... | collective-permute-start | bytes 1572872 | tf_op jit(solution)/shard_map/ppermute | solution.py:345
  35.3 0.7 collective-permute-start.1
  36.0 0.0 collective-permute-done.2.direction_near_ref
  36.0 0.0 copy-start.6
  36.1 0.0 copy-done.8
  36.1 12.9 %collective-permute-start.5 = (f32[1,256,256]{2,1,0:T(8,128)S(1)}, f32[1,256,256]{2,1,0:T(8,128)S(1)}, u32[]{:S(2)}, u32[]{:S(2)}) collective-permute-start(f32[1,256,256]{2,1,0:T(8,128)S(1)} %copy-done.8), channel_id=1, source_target_pairs={{0,1},{1,0},{2,3},{3,2},{4,5},{5,4},{6,7},{7,6},{8,9},{9,8},{10,11... | collective-permute-start | bytes 786440 | tf_op jit(solution)/shard_map/ppermute | solution.py:362
  49.0 1.2 collective-permute-done.5.direction_far_ref
  50.1 0.0 collective-permute-done.3.labels_far_ref
  50.1 0.0 collective-permute-done.labels_near_ref
  50.1 0.0 copy-start.3
  50.2 0.0 collective-permute-done.4.right_far_ref
  50.2 0.0 collective-permute-done.1.right_near_ref
  50.2 0.0 copy-done.6
  50.2 0.6 copy-done.7
  50.8 0.2 copy-done.2
  51.1 0.2 copy-done.3
  51.2 0.1 copy-done.4
  51.3 0.8 copy-done.5
  52.1 89.6 %main.1 = (f32[4,256,256]{2,1,0:T(8,128)}, f32[4,256,256]{2,1,0:T(8,128)}, f32[1,1]{1,0:T(1,128)}) custom-call(s32[4,256,256]{2,1,0:T(8,128)} %labels_ref.3, f32[4,256,256]{2,1,0:T(8,128)} %right_ref.3, f32[8,7]{1,0:T(8,128)} %table_ref.3, f32[2]{0:T(128)} %bounds_ref.3, s32[2,256,256]{2,1,0:T(8,128)} %copy-done.3, f32[2,256,256]{2,1,0:T(8,128)} %copy-done.5, ...), custom_call_target="tpu_custom_call" | custom-call | tf_op jit(solution)/shard_map/main/pallas_call | solution.py:365
  141.7 0.7 broadcast_in_dim.8
  142.4 20.8 %all_to_all.6 = f32[16,1,1]{2,1,0:T(1,128)S(1)} all-to-all(f32[16,1,1]{2,1,0:T(1,128)S(1)} %broadcast_in_dim.8), channel_id=1, replica_groups=mesh['groups'=2,'gz'=16] {'gz'}, dimensions={0} | all-to-all | bytes 128 | tf_op jit(solution)/shard_map/all_to_all | solution.py:386
  163.2 0.6 reduce_sum.9
  (5 shorter events, 0.0 us)
Async XLA Ops:
  0.6 26.4 %copy-start = (s32[4,256,256]{2,1,0:T(8,128)S(1)}, s32[4,256,256]{2,1,0:T(8,128)}, u32[]{:S(2)}) copy-start(s32[4,256,256]{2,1,0:T(8,128)} %labels_ref.3) | copy-start | bytes 3145732
  26.3 9.7 %collective-permute-start.2 = (f32[1,256,256]{2,1,0:T(8,128)}, f32[1,256,256]{2,1,0:T(8,128)S(1)}, u32[]{:S(2)}, u32[]{:S(2)}) collective-permute-start(f32[1,256,256]{2,1,0:T(8,128)} %get-tuple-element.8), channel_id=1, source_target_pairs={{1,2},{3,4},{5,6},{7,8},{9,10},{11,12},{13,14},{2,1},{4,3},{6,5},{... | collective-permute-start | bytes 786440 | tf_op jit(solution)/shard_map/ppermute | solution.py:361
  27.0 5.3 %copy-start.1 = (f32[4,256,256]{2,1,0:T(8,128)S(1)}, f32[4,256,256]{2,1,0:T(8,128)}, u32[]{:S(2)}) copy-start(f32[4,256,256]{2,1,0:T(8,128)} %right_ref.3) | copy-start | bytes 3145732
  27.1 23.0 %collective-permute-start.3 = (s32[2,256,256]{2,1,0:T(8,128)S(1)}, s32[2,256,256]{2,1,0:T(8,128)S(1)}, u32[]{:S(2)}, u32[]{:S(2)}) collective-permute-start(s32[2,256,256]{2,1,0:T(8,128)S(1)} %get-tuple-element.15), channel_id=1, source_target_pairs={{0,1},{1,0},{2,3},{3,2},{4,5},{5,4},{6,7},{7,6},{8,9},{9,8},{10,11... | collective-permute-start | bytes 1572872 | tf_op jit(solution)/shard_map/ppermute | solution.py:345
  31.5 4.6 %copy-start.8 = (f32[1,256,256]{2,1,0:T(8,128)S(1)}, f32[1,256,256]{2,1,0:T(8,128)}, u32[]{:S(2)}) copy-start(f32[1,256,256]{2,1,0:T(8,128)} %get-tuple-element.9) | copy-start | bytes 786436
  31.5 18.6 %collective-permute-start = (s32[2,256,256]{2,1,0:T(8,128)S(1)}, s32[2,256,256]{2,1,0:T(8,128)S(1)}, u32[]{:S(2)}, u32[]{:S(2)}) collective-permute-start(s32[2,256,256]{2,1,0:T(8,128)S(1)} %get-tuple-element.16), channel_id=1, source_target_pairs={{1,2},{3,4},{5,6},{7,8},{9,10},{11,12},{13,14},{2,1},{4,3},{6,5},{... | collective-permute-start | bytes 1572872 | tf_op jit(solution)/shard_map/ppermute | solution.py:345
  32.4 17.7 %collective-permute-start.4 = (f32[2,256,256]{2,1,0:T(8,128)S(1)}, f32[2,256,256]{2,1,0:T(8,128)S(1)}, u32[]{:S(2)}, u32[]{:S(2)}) collective-permute-start(f32[2,256,256]{2,1,0:T(8,128)S(1)} %get-tuple-element.13), channel_id=1, source_target_pairs={{0,1},{1,0},{2,3},{3,2},{4,5},{5,4},{6,7},{7,6},{8,9},{9,8},{10,11... | collective-permute-start | bytes 1572872 | tf_op jit(solution)/shard_map/ppermute | solution.py:345
  35.3 14.8 %collective-permute-start.1 = (f32[2,256,256]{2,1,0:T(8,128)S(1)}, f32[2,256,256]{2,1,0:T(8,128)S(1)}, u32[]{:S(2)}, u32[]{:S(2)}) collective-permute-start(f32[2,256,256]{2,1,0:T(8,128)S(1)} %get-tuple-element.14), channel_id=1, source_target_pairs={{1,2},{3,4},{5,6},{7,8},{9,10},{11,12},{13,14},{2,1},{4,3},{6,5},{... | collective-permute-start | bytes 1572872 | tf_op jit(solution)/shard_map/ppermute | solution.py:345
  36.0 14.1 %copy-start.6 = (f32[1,256,256]{2,1,0:T(8,128)}, f32[1,256,256]{2,1,0:T(8,128)S(1)}, u32[]{:S(2)}) copy-start(f32[1,256,256]{2,1,0:T(8,128)S(1)} %collective-permute-done.2.direction_near_ref) | copy-start | bytes 786436
  36.1 14.1 %collective-permute-start.5 = (f32[1,256,256]{2,1,0:T(8,128)S(1)}, f32[1,256,256]{2,1,0:T(8,128)S(1)}, u32[]{:S(2)}, u32[]{:S(2)}) collective-permute-start(f32[1,256,256]{2,1,0:T(8,128)S(1)} %copy-done.8), channel_id=1, source_target_pairs={{0,1},{1,0},{2,3},{3,2},{4,5},{5,4},{6,7},{7,6},{8,9},{9,8},{10,11... | collective-permute-start | bytes 786440 | tf_op jit(solution)/shard_map/ppermute | solution.py:362
  50.1 0.7 copy-start.7
  50.1 0.9 copy-start.2
  50.1 1.1 copy-start.3
  50.2 1.2 copy-start.4
  51.3 0.8 copy-start.5

commit v2 on v0

v2 whole, which is shorter than its diff:
```python
import functools

import jax
import jax.numpy as jnp
from jax import lax
from jax.experimental import pallas as pl
from jax.experimental.pallas import tpu as pltpu
from jax.sharding import PartitionSpec as P

ITERS = 3
PHASES = 8
LANES = 128
SUB = 8
PAD = 8
BELOW = 8
RIM = 16
RIM_BELOW = 24
HALO = 2

steps = (
    (1, 0, 0),
    (0, 1, 0),
    (0, 0, 1),
    (1, 1, 0),
    (1, -1, 0),
    (1, 0, 1),
    (1, 0, -1),
    (0, 1, 1),
    (0, 1, -1),
)
cross = [d for d, step in enumerate(steps) if step[0]]
inplane = [d for d, step in enumerate(steps) if not step[0]]
sideways = [d for d, step in enumerate(steps) if step[2]]


def slots(directions):
    order = [(d, 0) for d in directions] + [(d, 1) for d in directions if steps[d][2]]
    return {key: k for k, key in enumerate(order)}


cross_slots, inplane_slots = slots(cross), slots(inplane)


def splat(value):
    return jnp.full((SUB, LANES), value, jnp.float32)


def chebyshev(bounds_ref):
    lower, upper = splat(bounds_ref[0]), splat(bounds_ref[1])
    centre = (upper + lower) / 2.0
    half = (upper - lower) / 2.0
    sigma = centre / half
    rho = 1.0 / sigma
    factors = []
    for _ in range(ITERS):
        rho_new = 1.0 / (2.0 * sigma - rho)
        factors.append((rho_new * rho, 2.0 * rho_new / half))
        rho = rho_new
    return 1.0 / centre, factors


def each_block(rows, body, carry=0, unroll=8):
    count = rows // SUB

    def step(k, carry):
        return body(pl.multiple_of(k * SUB, SUB), carry)

    carry = lax.fori_loop(0, count - count % unroll, step, carry, unroll=unroll)
    for k in range(count - count % unroll, count):
        carry = body(k * SUB, carry)
    return carry


def lane_shifted(values, dz, edge):
    lane = lax.broadcasted_iota(jnp.int32, (SUB, LANES), 1)
    turned = [pltpu.roll(value, LANES - 1 if dz == 1 else 1, 1) for value in values]
    if dz == 1:
        beyond = turned[1:] + [edge]
        return [jnp.where(lane == LANES - 1, b, t) for t, b in zip(turned, beyond)]
    beyond = [edge] + turned[:-1]
    return [jnp.where(lane == 0, b, t) for t, b in zip(turned, beyond)]


def put_field(field, plane, row, values):
    zero = splat(0.0)
    for variant, dz in ((0, 0), (1, 1), (2, -1)):
        shifted = lane_shifted(values, dz, zero) if dz else values
        for c, value in enumerate(shifted):
            field[plane, c, variant, pl.ds(row + PAD, SUB), :] = value


def field_rims(field, plane, tiles, rows):
    for variant in range(3):
        for c in range(tiles):
            field[plane, c, variant, pl.ds(0, PAD), :] = splat(0.0)
            field[plane, c, variant, pl.ds(rows + PAD, PAD), :] = splat(0.0)


def tile(ref, plane, c, row):
    return ref[plane, pl.ds(row, SUB), pl.ds(c * LANES, LANES)]


def put_tile(ref, plane, c, row, value):
    ref[plane, pl.ds(row, SUB), pl.ds(c * LANES, LANES)] = value


class Half:
    def __init__(self, table_ref, flip, refs, tiles, rows):
        self.refs, self.tiles, self.rows = refs, tiles, rows
        turn = jnp.where(splat(flip.astype(jnp.float32)) > 0.5, -0.5, 0.5)
        self.tables = []
        for phase in range(PHASES):
            k = [splat(table_ref[phase, column]) for column in range(7)]
            size = [jnp.abs(value) for value in k]
            self.tables.append(
                (
                    (0.5 * (k[0] - size[3] - size[4]), turn * k[3], turn * k[4]),
                    (0.5 * (k[1] - size[3] - size[5]), 0.5 * (k[2] - size[4] - size[5]), 0.5 * k[5], k[6]),
                )
            )
        for ref, slots_of in zip(refs, (cross_slots, inplane_slots)):
            for slot in range(ref.shape[0]):
                for k in range(len(slots_of)):
                    for c in range(tiles):
                        for start in (0, SUB, rows + RIM, rows + RIM + SUB):
                            ref[slot, c, k, pl.ds(start, SUB), :] = splat(0.0)

    def fill(self, slot, read, mask=None, reaction=None):
        for group in range(2 if reaction else 1):
            tables = [t[group] for t in self.tables]
            if mask is not None:
                tables = [[mask * value for value in t] for t in tables]
            ref, at = (self.refs[1], 0) if group else (self.refs[0], slot)
            places = inplane_slots if group else cross_slots

            def body(row, carry):
                found = {}
                for c in range(self.tiles):
                    label = read(c, row)
                    bits = [(label & (1 << b)) != 0 for b in range(3)]
                    looked = []
                    for column in range(len(tables[0])):
                        level = [t[column] for t in tables]
                        for bit in bits:
                            level = [jnp.where(bit, b, a) for a, b in zip(level[::2], level[1::2])]
                        looked.append(level[0])
                    if group == 0:
                        values = {0: looked[0]}
                        signed = zip((3, 5), looked[1:])
                    else:
                        values = {1: looked[0], 2: looked[1]}
                        signed = [(7, looked[2])]
                        reaction[0][reaction[1], c, pl.ds(row, SUB), :] = looked[3]
                    for d, value in signed:
                        values[d] = jnp.maximum(value, 0.0)
                        values[d + 1] = jnp.maximum(-value, 0.0)
                    for d, value in values.items():
                        ref[at, c, places[d, 0], pl.ds(row + RIM, SUB), :] = value
                        found.setdefault(d, []).append(value)
                for d, values in found.items():
                    if steps[d][2]:
                        for c, value in enumerate(lane_shifted(values, steps[d][2], splat(0.0))):
                            ref[at, c, places[d, 1], pl.ds(row + RIM, SUB), :] = value
                return carry

            each_block(self.rows, body)

    def link(self, slot, other, out, at):
        directions, places = (cross, cross_slots) if other is not None else (inplane, inplane_slots)
        ref = self.refs[0 if other is not None else 1]
        slot, other = (slot, other) if other is not None else (0, 0)

        def body(row, carry):
            for d in directions:
                dx, dy, dz = steps[d]
                near = pl.ds(row + RIM - PAD, SUB)
                far = pl.ds(row + RIM - PAD + dy, SUB)
                ahead = [ref[other, c, places[d, 1 if dz else 0], far, :] for c in range(self.tiles)]
                values = [ref[slot, c, places[d, 0], near, :] + ahead[c] for c in range(self.tiles)]
                for c, value in enumerate(values):
                    out[at, c, places[d, 0], pl.ds(row, SUB), :] = value
                if dz:
                    edge = ref[other, 0 if dz == 1 else self.tiles - 1, places[d, 0], far, :]
                    for c, value in enumerate(lane_shifted(values, -dz, edge)):
                        out[at, c, places[d, 1], pl.ds(row, SUB), :] = value
            return carry

        each_block(self.rows + 2 * PAD, body)


def apply_operator(field, cross_ref, inplane_ref, reaction_ref, planes, tiles, rows, use):
    for c in range(tiles):

        def body(row, carry):
            held = {}

            def value(q, dy, dz):
                key = (q, dy, dz)
                if key not in held:
                    held[key] = field[q + HALO, c, dz % 3, pl.ds(row + PAD + dy, SUB), :]
                return held[key]

            for q in planes:
                here = value(q, 0, 0)
                image = reaction_ref[q + 1, c, pl.ds(row, SUB), :] * here
                sums = [image, None, None]
                k = 0
                for d, (dx, dy, dz) in enumerate(steps):
                    places = cross_slots if dx else inplane_slots
                    ref, base = (cross_ref, HALO) if dx else (inplane_ref, 1)
                    for sign in (1, -1):
                        if sign == 1:
                            link = ref[q + base, c, places[d, 0], pl.ds(row + PAD, SUB), :]
                        else:
                            key = places[d, 1 if dz else 0]
                            link = ref[q + base - dx, c, key, pl.ds(row + PAD - dy, SUB), :]
                        term = link * (here - value(q + sign * dx, sign * dy, sign * dz))
                        sums[k % 3] = term if sums[k % 3] is None else sums[k % 3] + term
                        k += 1
                carry = use(q, c, row, sums[0] + (sums[1] + sums[2]), here, carry)
            return carry

        yield body


def run_operator(*arguments, carry=0):
    rows = arguments[6]
    for body in apply_operator(*arguments):
        carry = each_block(rows, body, carry, unroll=4)
    return carry


class Device:
    def __init__(self, shape):
        self.depth, self.rows, self.tiles = shape[0], shape[1], shape[2] // LANES
        self.place, self.count = lax.axis_index("gz"), lax.axis_size("gz")
        self.flip = self.place % 2
        joined = jnp.logical_and(self.place > 0, self.place < self.count - 1)
        self.joined = splat(joined.astype(jnp.float32))

    def own(self, q):
        return jnp.where(self.flip == 1, self.depth - 1 - q, q)

    def halo(self, q):
        far = q >= self.depth
        first = (q == self.depth) if far else (q == -1)
        turned = self.flip == (1 if far else 0)
        return jnp.where(turned, 1, 0) if first else jnp.where(turned, 0, 1)


def start_kernel(labels_hbm, right_hbm, table_ref, bounds_ref, *refs):
    labels_ref, first_ref, cross_ref, inplane_ref, reaction_ref, rest_ref, near_ref, far_ref = refs[:8]
    right_ref, sems, *halves = refs[8:]
    copies = [
        pltpu.make_async_copy(source, target, sems.at[k])
        for k, (source, target) in enumerate(((right_hbm, right_ref), (labels_hbm, labels_ref)))
    ]
    for copy in copies:
        copy.start()
    device = Device(labels_ref.shape)
    depth, rows, tiles = device.depth, device.rows, device.tiles
    inverse, factors = chebyshev(bounds_ref)
    half = Half(table_ref, device.flip, halves, tiles, rows)
    copies[0].wait()
    for q in range(depth):
        index = device.own(q)
        field_rims(first_ref, q + HALO, tiles, rows)

        def body(row, carry):
            values = [tile(right_ref, index, c, row) for c in range(tiles)]
            for c, value in enumerate(values):
                rest_ref[q + 1, c, pl.ds(row, SUB), :] = value
            put_field(first_ref, q + HALO, row, [value * inverse for value in values])
            return carry

        each_block(rows, body)
    copies[1].wait()
    for q in range(depth):
        index = device.own(q)
        half.fill(q % 2, lambda c, row: tile(labels_ref, index, c, row), None, (reaction_ref, q + 1))
        if q:
            half.link((q - 1) % 2, q % 2, cross_ref, q - 1 + HALO)
        half.link(q % 2, None, inplane_ref, q + 1)

    ahead, behind = factors[0]

    def use(q, c, row, image, here, carry):
        rest = rest_ref[q + 1, c, pl.ds(row, SUB), :] - image
        rest_ref[q + 1, c, pl.ds(row, SUB), :] = rest
        for plane, out in ((1, near_ref), (depth - 2, far_ref)):
            if q == plane:
                put_tile(out, 0, c, row, ahead * here + behind * rest)
        return carry

    run_operator(first_ref, cross_ref, inplane_ref, reaction_ref, range(1, depth - 1), tiles, rows, use)


def halo_links(device, half, labels_ref, near_labels_ref, far_labels_ref, cross_ref, inplane_ref, reaction_ref):
    depth = device.depth

    def own(q):
        index = device.own(q)
        return lambda c, row: tile(labels_ref, index, c, row)

    def halo(ref, q):
        index = device.halo(q)
        return lambda c, row: tile(ref, index, c, row)

    for inner, outer, furthest, ref in ((depth - 1, depth, depth + 1, far_labels_ref), (0, -1, -2, near_labels_ref)):
        mask = device.joined if outer < 0 else None
        half.fill(0, own(inner))
        half.fill(1, halo(ref, outer), mask, (reaction_ref, outer + 1))
        half.link(1, None, inplane_ref, outer + 1)
        if outer > 0:
            half.link(0, 1, cross_ref, inner + HALO)
            half.fill(0, halo(ref, furthest), mask)
            half.link(1, 0, cross_ref, outer + HALO)
        else:
            half.link(1, 0, cross_ref, outer + HALO)
            half.fill(0, halo(ref, furthest), mask)
            half.link(0, 1, cross_ref, furthest + HALO)


class Solve:
    def __init__(self, device, refs, factors, right):
        self.device, self.refs, self.factors, self.right = device, refs, factors, right

    def subtract(self, iteration, planes, last=None):
        device = self.device
        first_ref, second_ref, cross_ref, inplane_ref, reaction_ref, rest_ref, _ = self.refs
        field = second_ref if iteration == 1 else first_ref

        def use(q, c, row, image, here, carry):
            if iteration == 0 and not 0 <= q < device.depth:
                rest = self.right(q, c, row) - image
            else:
                rest = rest_ref[q + 1, c, pl.ds(row, SUB), :] - image
            if q < 0:
                rest = rest * device.joined
            rest_ref[q + 1, c, pl.ds(row, SUB), :] = rest
            return carry

        run_operator(
            field, cross_ref, inplane_ref, reaction_ref, planes, device.tiles, device.rows, last or use
        )

    def direct(self, iteration, planes):
        device = self.device
        first_ref, second_ref, _, _, _, rest_ref, sum_ref = self.refs
        old, new = (first_ref, second_ref) if iteration == 0 else (second_ref, first_ref)
        ahead, behind = self.factors[iteration]
        for q in planes:
            if iteration == 0:
                field_rims(new, q + HALO, device.tiles, device.rows)

            def body(row, carry):
                values = []
                for c in range(device.tiles):
                    here = old[q + HALO, c, 0, pl.ds(row + PAD, SUB), :]
                    value = ahead * here + behind * rest_ref[q + 1, c, pl.ds(row, SUB), :]
                    values.append(value)
                    if 0 <= q < device.depth:
                        before = here if iteration == 0 else sum_ref[q, c, pl.ds(row, SUB), :]
                        sum_ref[q, c, pl.ds(row, SUB), :] = before + value
                put_field(new, q + HALO, row, values)
                return carry

            each_block(device.rows, body)

    def receive(self, field, q, read):
        field_rims(field, q + HALO, self.device.tiles, self.device.rows)

        def body(row, carry):
            put_field(field, q + HALO, row, [read(c, row) for c in range(self.device.tiles)])
            return carry

        each_block(self.device.rows, body)


def middle_kernel(*refs):
    _, _, _, _, _, labels_ref, table_ref, bounds_ref = refs[:8]
    far_labels_ref, far_right_ref, far_second_ref, near_labels_ref = refs[8:12]
    first_ref, cross_ref, inplane_ref, reaction_ref, rest_ref, second_ref, sum_ref, *halves = refs[12:]
    device = Device(labels_ref.shape)
    depth = device.depth
    inverse, factors = chebyshev(bounds_ref)
    half = Half(table_ref, device.flip, halves, device.tiles, device.rows)
    halo_links(device, half, labels_ref, near_labels_ref, far_labels_ref, cross_ref, inplane_ref, reaction_ref)

    def right(q, c, row):
        return tile(far_right_ref, device.halo(q), c, row)

    solve = Solve(
        device, (first_ref, second_ref, cross_ref, inplane_ref, reaction_ref, rest_ref, sum_ref), factors, right
    )
    for q in (depth, depth + 1):
        index = device.halo(q)
        solve.receive(first_ref, q, lambda c, row: tile(far_right_ref, index, c, row) * inverse)
    solve.subtract(0, [depth - 1, depth])
    solve.direct(0, range(1, depth + 1))
    solve.receive(second_ref, depth + 1, lambda c, row: tile(far_second_ref, 0, c, row))
    solve.subtract(1, range(2, depth + 1))
    solve.direct(1, range(2, depth + 1))
    solve.subtract(2, range(3, depth))


def last_kernel(
    first_in,
    second_in,
    rest_in,
    sum_in,
    cross_ref,
    inplane_ref,
    reaction_ref,
    bounds_ref,
    near_right_ref,
    near_second_ref,
    first_ref,
    second_ref,
    rest_ref,
    sum_ref,
    solution_ref,
    residual_ref,
    squares_ref,
):
    device = Device(residual_ref.shape)
    depth, rows, tiles = device.depth, device.rows, device.tiles
    inverse, factors = chebyshev(bounds_ref)

    def right(q, c, row):
        return tile(near_right_ref, device.halo(q), c, row)

    refs = (first_ref, second_ref, cross_ref, inplane_ref, reaction_ref, rest_ref, sum_ref)
    solve = Solve(device, refs, factors, right)
    for q in (-1, -2):
        index = device.halo(q)
        solve.receive(first_ref, q, lambda c, row: tile(near_right_ref, index, c, row) * inverse)
    solve.subtract(0, [-1, 0])
    solve.direct(0, [-1, 0])
    solve.receive(second_ref, -2, lambda c, row: tile(near_second_ref, 0, c, row))
    solve.subtract(1, [-1, 0, 1])
    solve.direct(1, [-1, 0, 1])

    def use(q, c, row, image, here, carry):
        rest = rest_ref[q + 1, c, pl.ds(row, SUB), :] - image
        put_tile(residual_ref, device.own(q), c, row, rest)
        return carry + rest * rest

    planes = range(0, min(3, depth))
    total = run_operator(
        first_ref, cross_ref, inplane_ref, reaction_ref, planes, tiles, rows, use, carry=splat(0.0)
    )
    for c in range(tiles):

        def body(row, carry):
            for q in range(3, depth):
                rest = rest_ref[q + 1, c, pl.ds(row, SUB), :]
                put_tile(residual_ref, device.own(q), c, row, rest)
                carry = carry + rest * rest
            for q in range(depth):
                put_tile(solution_ref, device.own(q), c, row, sum_ref[q, c, pl.ds(row, SUB), :])
            return carry

        total = each_block(rows, body, total)
    squares_ref[...] = jnp.broadcast_to(jnp.sum(total), squares_ref.shape)


def per_device(labels, tensor_table, bounds, right_side):
    depth, rows, columns = labels.shape
    tiles = columns // LANES
    count = lax.axis_size("gz")
    odd = lax.axis_index("gz") % 2

    vmem = pl.BlockSpec(memory_space=pltpu.VMEM)
    smem = pl.BlockSpec(memory_space=pltpu.SMEM)
    hbm = pl.BlockSpec(memory_space=pltpu.HBM)

    def array(*shape):
        return jax.ShapeDtypeStruct(shape, jnp.float32)

    below = rows + PAD + BELOW
    first = array(depth + 2 * HALO, tiles, 3, below, LANES)
    cross_links = array(depth + 2 * HALO - 1, tiles, len(cross_slots), below, LANES)
    inplane_links = array(depth + 2, tiles, len(inplane_slots), below, LANES)
    reaction = array(depth + 2, tiles, rows, LANES)
    total = array(depth, tiles, rows, LANES)
    plane = array(1, rows, columns)
    halves = [
        pltpu.VMEM((count_, tiles, len(places), rows + RIM + RIM_BELOW, LANES), jnp.float32)
        for count_, places in ((2, cross_slots), (1, inplane_slots))
    ]

    def call(kernel, name, out_shape, in_specs, aliases, limit, cycles, scratch=()):
        return pl.pallas_call(
            kernel,
            out_shape=out_shape,
            in_specs=in_specs,
            out_specs=[vmem] * len(out_shape),
            scratch_shapes=list(scratch),
            input_output_aliases=aliases,
            compiler_params=pltpu.CompilerParams(vmem_limit_bytes=limit),
            cost_estimate=pl.CostEstimate(flops=cycles, bytes_accessed=1 << 20, transcendentals=0),
            name=name,
        )

    inside = [(i, i ^ 1) for i in range(count)]
    across = [(i, i + 1) for i in range(1, count - 1, 2)]
    across += [(j, i) for i, j in across]
    near_start = odd * (depth - HALO)
    far_start = (1 - odd) * (depth - HALO)

    def send(name, array, start, pairs):
        with jax.named_scope(name):
            return lax.ppermute(lax.dynamic_slice_in_dim(array, start, HALO, 0), "gz", pairs)

    near_labels = send("near_labels", labels, near_start, across)
    near_right = send("near_right", right_side, near_start, across)
    far_labels = send("far_labels", labels, far_start, inside)
    far_right = send("far_right", right_side, far_start, inside)

    state = (first, cross_links, inplane_links, reaction, reaction)
    own_labels, *state, near, far = call(
        start_kernel,
        "start",
        (jax.ShapeDtypeStruct(labels.shape, jnp.int32),) + state + (plane, plane),
        [hbm, hbm, smem, smem],
        {},
        9 << 20,
        10**8,
        [pltpu.VMEM(right_side.shape, jnp.float32), pltpu.SemaphoreType.DMA((2,))] + halves,
    )(labels, right_side, tensor_table, bounds)
    with jax.named_scope("near_second"):
        near_second = lax.ppermute(near, "gz", across)
    with jax.named_scope("far_second"):
        far_second = lax.ppermute(far, "gz", inside)

    outs = call(
        middle_kernel,
        "middle",
        tuple(array(*s.shape) for s in state) + (first, total),
        [vmem] * 6 + [smem, smem] + [vmem] * 4,
        {k: k for k in range(5)},
        7 << 20,
        10**8,
        halves,
    )(*state, own_labels, tensor_table, bounds, far_labels, far_right, far_second, near_labels)
    first, cross_links, inplane_links, reaction, rest, second, total = outs

    *_, solved, residual, squares = call(
        last_kernel,
        "last",
        tuple(array(*s.shape) for s in (first, second, rest, total))
        + (array(*right_side.shape), array(*right_side.shape), array(count, LANES)),
        [vmem] * 7 + [smem] + [vmem] * 2,
        {k: k for k in range(4)},
        6 << 20,
        10**8,
    )(first, second, rest, total, cross_links, inplane_links, reaction, bounds, near_right, near_second)
    gathered = lax.all_to_all(squares, "gz", 0, 0, tiled=True)
    return solved, residual, jnp.sqrt(jnp.sum(gathered[:, 0])).reshape(1)


def solution(mesh):
    whole = P(("groups", "gz"), None, None)
    return jax.shard_map(
        per_device,
        mesh=mesh,
        in_specs=(whole, P("groups", None), P("groups"), whole),
        out_specs=(whole, whole, P("groups")),
        check_vma=False,
    )
```

time: 197 us -> 73.4 us (0.37)
  other arithmetic: 113 us -> 0.6 us
  Pallas kernels: 0 us -> 39.4 us
  starting transfers between devices: 25.6 us -> 7.07 us
  blocking collectives: 34.3 us -> 15.8 us
  local copies, waits for them, and re-layouts: 12.7 us -> 7.02 us
  waiting for transfers between devices: 4.89 us -> 0.49 us
  between operations: 5.93 us -> 2.58 us
    pallas_call x0 -> x3, Pallas kernels: none -> 39.4 us  [the longest x1 16.4 us: per_device(): call(middle_kernel, 'middle', tuple((array(*s.shape) for s in state)) + (...]
    psum x1 -> x0, blocking collectives: 34.3 us -> none  [per_device(): squares = lax.psum(jnp.sum(residual * residual), 'gz')]
    add x3 -> x0, other arithmetic: 33.6 us -> none  [the longest x2 32.3 us: per_device(): new_factor * factor * direction + 2.0 * new_factor / spread * residual]
    select_n x4 -> x0, other arithmetic: 27.2 us -> none  [cell_values(): result = jnp.where(labels == phase, per_phase[phase], result)]
    unnamed x4 -> x0, other arithmetic: 27 us -> none
    ppermute x8 -> x6, starting transfers between devices: 25.6 us -> 7.07 us  [the longest x4 5.85 us: send(): lax.ppermute(lax.dynamic_slice_in_dim(array, start, HALO, 0), 'gz', pairs)]
    all_to_all x0 -> x1, blocking collectives: none -> 15.8 us  [per_device(): gathered = lax.all_to_all(squares, 'gz', 0, 0, tiled=True)]
    slice x11 -> x0, local copies, waits for them, and re-layouts: 10.2 us -> none  [the longest x4 4.85 us: extended_2(): lax.slice_in_dim(cells, cells.shape[dim] - width, cells.shape[dim], axis=...]
  transfers between devices with their start and end apart: 8 -> 6, of which waited for: 2 -> 1; matrix products, arithmetic and copies ran while one was open for 36% -> 2% of each run, Pallas kernels for 0% -> 39%
where the time goes in v2:
time: 73.4 us; the launch traced here: 73 us
  Pallas kernels  39.4 us (54%)
  blocking collectives  15.8 us (22%)
  starting transfers between devices  7.07 us (10%)
  local copies, waits for them, and re-layouts  7.02 us (10%)
  between operations  2.58 us (4%)
    pallas_call x1, Pallas kernels, per_device(): call(middle_kernel, 'middle', tuple((array(*s.shape) for s in state)) + (...  16.4 us
    all_to_all x1, blocking collectives, per_device(): gathered = lax.all_to_all(squares, 'gz', 0, 0, tiled=True)  15.8 us
    pallas_call x1, Pallas kernels, per_device(): call(start_kernel, 'start', (jax.ShapeDtypeStruct(labels.shape, jnp.int32...  12.2 us
    pallas_call x1, Pallas kernels, per_device(): call(last_kernel, 'last', tuple((array(*s.shape) for s in (first, second,...  10.8 us
    ppermute x4, starting transfers between devices, send(): lax.ppermute(lax.dynamic_slice_in_dim(array, start, HALO, 0), 'gz', pairs)  5.85 us
    unnamed x10, local copies, waits for them, and re-layouts  4.47 us
    dynamic_slice x2, local copies, waits for them, and re-layouts, send(): lax.dynamic_slice_in_dim(array, start, HALO, 0)  2.55 us
  transfers between devices with their start and end apart: 6, of which 1 were waited for; matrix products, arithmetic and copies ran while one was open for 2% of the time, Pallas kernels for 39%

profile of v2, /device:TPU:0, one launch (start us, length us, event | category | flops | bytes accessed | tf_op | source)
XLA Modules:
  0.0 73.0 jit_solution(11264963793086311177)
XLA Ops:
  0.7 1.3 %constant_dynamic-slice_fusion.1 = (s32[2,256,256]{2,1,0:T(8,128)S(1)}, s32[2,256,256]{2,1,0:T(8,128)S(1)}) fusion(s32[4,256,256]{2,1,0:T(8,128)} %labels_hbm.1, s32[]{:T(128)S(6)} %select_n.17, s32[]{:T(128)S(6)} %select_n.16), kind=kLoop, calls=%fused_computation.2 | loop fusion | bytes 2097160 | tf_op jit(solution)/shard_map/near_labels/dynamic_slice | solution.py:514
  1.9 0.7 collective-permute-start.3
  2.6 4.4 %collective-permute-start = (s32[2,256,256]{2,1,0:T(8,128)S(1)}, s32[2,256,256]{2,1,0:T(8,128)S(1)}, u32[]{:S(2)}, u32[]{:S(2)}) collective-permute-start(s32[2,256,256]{2,1,0:T(8,128)S(1)} %get-tuple-element.42), channel_id=1, source_target_pairs={{0,1},{1,0},{2,3},{3,2},{4,5},{5,4},{6,7},{7,6},{8,9},{9,8},{10,11... | collective-permute-start | bytes 1572872 | tf_op jit(solution)/shard_map/far_labels/ppermute | solution.py:514
  7.0 1.3 %constant_dynamic-slice_fusion = (f32[2,256,256]{2,1,0:T(8,128)S(1)}, f32[2,256,256]{2,1,0:T(8,128)S(1)}) fusion(f32[4,256,256]{2,1,0:T(8,128)} %right_hbm.1, s32[]{:T(128)S(6)} %select_n.17, s32[]{:T(128)S(6)} %select_n.16), kind=kLoop, calls=%fused_computation.1 | loop fusion | bytes 2097160 | tf_op jit(solution)/shard_map/near_right/dynamic_slice | solution.py:514
  8.3 0.1 collective-permute-start.1
  8.4 0.0 copy-start
  8.4 1.2 %copy-done = s32[4,256,256]{2,1,0:T(8,128)S(1)} copy-done((s32[4,256,256]{2,1,0:T(8,128)S(1)}, s32[4,256,256]{2,1,0:T(8,128)}, u32[]{:S(2)}) %copy-start) | copy-done | bytes 1048600
  9.6 0.0 copy-start.1
  9.6 1.2 %copy-done.1 = f32[4,256,256]{2,1,0:T(8,128)S(1)} copy-done((f32[4,256,256]{2,1,0:T(8,128)S(1)}, f32[4,256,256]{2,1,0:T(8,128)}, u32[]{:S(2)}) %copy-start.1) | copy-done | bytes 1048600
  10.8 0.0 copy-start.2
  10.8 0.7 copy-done.2
  11.5 0.0 copy-start.4
  11.5 0.7 copy-done.4
  12.2 12.2 %start.1 = (s32[4,256,256]{2,1,0:T(8,128)S(1)}, f32[8,2,3,272,128]{4,3,2,1,0:T(8,128)S(1)}, f32[7,2,7,272,128]{4,3,2,1,0:T(8,128)S(1)}, f32[6,2,7,272,128]{4,3,2...) custom-call(s32[4,256,256]{2,1,0:T(8,128)S(1)} %copy-done, ...), custom_call_target="tpu_custom_call" | custom-call | flops 100000000 | bytes 1048576 | tf_op jit(solution)/shard_map/start/pallas_call | solution.py:522
  24.4 0.6 collective-permute-start.2
  25.0 0.7 collective-permute-start.4
  25.7 0.5 collective-permute-done.2.refs_10_
  26.1 0.7 collective-permute-start.5
  26.8 0.0 collective-permute-done.3.refs_11_
  26.8 0.0 collective-permute-done.refs_8_
  26.8 0.0 collective-permute-done.1.refs_9_
  26.8 0.0 copy-start.3
  26.9 0.7 copy-done.3
  27.5 16.4 %middle.1 = (f32[8,2,3,272,128]{4,3,2,1,0:T(8,128)S(1)}, f32[7,2,7,272,128]{4,3,2,1,0:T(8,128)S(1)}, f32[6,2,7,272,128]{4,3,2,1,0:T(8,128)S(1)}, f32[6,2,256,128...) custom-call(f32[8,2,3,272,128]{4,3,2,1,0:T(8,128)S(1)} %get-tuple-el, ...), custom_call_target="tpu_custom_call", output_to_operand_aliasing={{0}: (0, {}), {1}: (1, {}), {2}: (2, {}), {3}: (3, {}), {4}... | custom-call | flops 100000000 | bytes 1048576 | tf_op jit(solution)/shard_map/middle/pallas_call | solution.py:537
  44.0 0.0 collective-permute-done.5.near_second_ref
  44.0 0.0 collective-permute-done.4.near_right_ref
  44.0 10.8 %last.1 = (f32[8,2,3,272,128]{4,3,2,1,0:T(8,128)S(1)}, f32[8,2,3,272,128]{4,3,2,1,0:T(8,128)S(1)}, f32[6,2,256,128]{3,2,1,0:T(8,128)S(1)}, f32[4,2,256,128]{3,2,...) custom-call(f32[8,2,3,272,128]{4,3,2,1,0:T(8,128)S(1)} %get-tuple-el, ...), custom_call_target="tpu_custom_call", output_to_operand_aliasing={{0}: (0, {}), {1}: (1, {}), {2}: (2, {}), {3}: (3, {})} | custom-call | flops 100000000 | bytes 1048576 | tf_op jit(solution)/shard_map/last/pallas_call | solution.py:549
  54.8 15.8 %all_to_all.12 = f32[16,1,128]{2,1,0:T(1,128)S(1)} all-to-all(f32[16,1,128]{2,1,0:T(1,128)S(1)} %bitcast.5), channel_id=1, replica_groups=mesh['groups'=2,'gz'=16] {'gz'}, dimensions={0} | all-to-all | bytes 16384 | tf_op jit(solution)/shard_map/all_to_all | solution.py:559
  70.6 0.6 slice_reduce_fusion
Async XLA Ops:
  1.9 24.9 %collective-permute-start.3 = (s32[2,256,256]{2,1,0:T(8,128)S(1)}, s32[2,256,256]{2,1,0:T(8,128)S(1)}, u32[]{:S(2)}, u32[]{:S(2)}) collective-permute-start(s32[2,256,256]{2,1,0:T(8,128)S(1)} %get-tuple-element.41), channel_id=1, source_target_pairs={{1,2},{3,4},{5,6},{7,8},{9,10},{11,12},{13,14},{2,1},{4,3},{6,5},{... | collective-permute-start | bytes 1572872 | tf_op jit(solution)/shard_map/near_labels/ppermute | solution.py:514
  2.6 24.2 %collective-permute-start = (s32[2,256,256]{2,1,0:T(8,128)S(1)}, s32[2,256,256]{2,1,0:T(8,128)S(1)}, u32[]{:S(2)}, u32[]{:S(2)}) collective-permute-start(s32[2,256,256]{2,1,0:T(8,128)S(1)} %get-tuple-element.42), channel_id=1, source_target_pairs={{0,1},{1,0},{2,3},{3,2},{4,5},{5,4},{6,7},{7,6},{8,9},{9,8},{10,11... | collective-permute-start | bytes 1572872 | tf_op jit(solution)/shard_map/far_labels/ppermute | solution.py:514
  8.3 18.5 %collective-permute-start.1 = (f32[2,256,256]{2,1,0:T(8,128)S(1)}, f32[2,256,256]{2,1,0:T(8,128)S(1)}, u32[]{:S(2)}, u32[]{:S(2)}) collective-permute-start(f32[2,256,256]{2,1,0:T(8,128)S(1)} %get-tuple-element.40), channel_id=1, source_target_pairs={{0,1},{1,0},{2,3},{3,2},{4,5},{5,4},{6,7},{7,6},{8,9},{9,8},{10,11... | collective-permute-start | bytes 1572872 | tf_op jit(solution)/shard_map/far_right/ppermute | solution.py:514
  8.4 1.2 %copy-start = (s32[4,256,256]{2,1,0:T(8,128)S(1)}, s32[4,256,256]{2,1,0:T(8,128)}, u32[]{:S(2)}) copy-start(s32[4,256,256]{2,1,0:T(8,128)} %labels_hbm.1) | copy-start | bytes 3145732
  9.6 1.2 %copy-start.1 = (f32[4,256,256]{2,1,0:T(8,128)S(1)}, f32[4,256,256]{2,1,0:T(8,128)}, u32[]{:S(2)}) copy-start(f32[4,256,256]{2,1,0:T(8,128)} %right_hbm.1) | copy-start | bytes 3145732
  10.8 0.7 copy-start.2
  11.5 0.7 copy-start.4
  24.4 1.7 %collective-permute-start.2 = (f32[1,256,256]{2,1,0:T(8,128)S(1)}, f32[1,256,256]{2,1,0:T(8,128)S(1)}, u32[]{:S(2)}, u32[]{:S(2)}) collective-permute-start(f32[1,256,256]{2,1,0:T(8,128)S(1)} %get-tuple-element.27), channel_id=1, source_target_pairs={{0,1},{1,0},{2,3},{3,2},{4,5},{5,4},{6,7},{7,6},{8,9},{9,8},{10,11... | collective-permute-start | bytes 786440 | tf_op jit(solution)/shard_map/far_second/ppermute | solution.py:535
  25.0 19.0 %collective-permute-start.4 = (f32[2,256,256]{2,1,0:T(8,128)S(1)}, f32[2,256,256]{2,1,0:T(8,128)S(1)}, u32[]{:S(2)}, u32[]{:S(2)}) collective-permute-start(f32[2,256,256]{2,1,0:T(8,128)S(1)} %get-tuple-element.39), channel_id=1, source_target_pairs={{1,2},{3,4},{5,6},{7,8},{9,10},{11,12},{13,14},{2,1},{4,3},{6,5},{... | collective-permute-start | bytes 1572872 | tf_op jit(solution)/shard_map/near_right/ppermute | solution.py:514
  26.1 17.9 %collective-permute-start.5 = (f32[1,256,256]{2,1,0:T(8,128)S(1)}, f32[1,256,256]{2,1,0:T(8,128)S(1)}, u32[]{:S(2)}, u32[]{:S(2)}) collective-permute-start(f32[1,256,256]{2,1,0:T(8,128)S(1)} %get-tuple-element.35), channel_id=1, source_target_pairs={{1,2},{3,4},{5,6},{7,8},{9,10},{11,12},{13,14},{2,1},{4,3},{6,5},{... | collective-permute-start | bytes 786440 | tf_op jit(solution)/shard_map/near_second/ppermute | solution.py:533
  26.8 0.7 copy-start.3

commit v3 on v2

v3 whole, which is shorter than its diff:
```python
import jax
import jax.numpy as jnp
from jax import lax
from jax.experimental import pallas as pl
from jax.experimental.pallas import tpu as pltpu
from jax.sharding import PartitionSpec as P


ITERS = 3
PHASES = 8
LANES = 128
SUB = 8
PAD = 8
BELOW = 8
RIM = 16
RIM_BELOW = 24
HALO = 2
LIMITS = (8, 8, 5, 5)

steps = (
    (1, 0, 0),
    (0, 1, 0),
    (0, 0, 1),
    (1, 1, 0),
    (1, -1, 0),
    (1, 0, 1),
    (1, 0, -1),
    (0, 1, 1),
    (0, 1, -1),
)
cross = [d for d, step in enumerate(steps) if step[0]]
inplane = [d for d, step in enumerate(steps) if not step[0]]


def slots(directions):
    order = [(d, 0) for d in directions] + [(d, 1) for d in directions if steps[d][2]]
    return {key: k for k, key in enumerate(order)}


cross_slots, inplane_slots = slots(cross), slots(inplane)


def splat(value):
    return jnp.full((SUB, LANES), value, jnp.float32)


def chebyshev(bounds_ref):
    lower, upper = splat(bounds_ref[0]), splat(bounds_ref[1])
    centre = (upper + lower) / 2.0
    half = (upper - lower) / 2.0
    sigma = centre / half
    rho = 1.0 / sigma
    factors = []
    for _ in range(ITERS):
        rho_new = 1.0 / (2.0 * sigma - rho)
        factors.append((rho_new * rho, 2.0 * rho_new / half))
        rho = rho_new
    return 1.0 / centre, factors


def each_block(rows, body, carry=0, unroll=None):
    count = rows // SUB
    unroll = min(unroll or 16, count)

    def step(k, carry):
        return body(pl.multiple_of(k * SUB, SUB), carry)

    carry = lax.fori_loop(0, count - count % unroll, step, carry, unroll=unroll)
    for k in range(count - count % unroll, count):
        carry = body(k * SUB, carry)
    return carry


def lane_shifted(values, dz, edge):
    lane = lax.broadcasted_iota(jnp.int32, (SUB, LANES), 1)
    turned = [pltpu.roll(value, LANES - 1 if dz == 1 else 1, 1) for value in values]
    if dz == 1:
        beyond = turned[1:] + [edge]
        return [jnp.where(lane == LANES - 1, b, t) for t, b in zip(turned, beyond)]
    beyond = [edge] + turned[:-1]
    return [jnp.where(lane == 0, b, t) for t, b in zip(turned, beyond)]


def put_field(field, plane, row, values):
    zero = splat(0.0)
    for variant, dz in ((0, 0), (1, 1), (2, -1)):
        shifted = lane_shifted(values, dz, zero) if dz else values
        for c, value in enumerate(shifted):
            field[plane, c, variant, pl.ds(row + PAD, SUB), :] = value


def field_rims(field, plane, tiles, rows):
    for variant in range(3):
        for c in range(tiles):
            field[plane, c, variant, pl.ds(0, PAD), :] = splat(0.0)
            field[plane, c, variant, pl.ds(rows + PAD, PAD), :] = splat(0.0)


def tile(ref, plane, c, row):
    return ref[plane, pl.ds(row, SUB), pl.ds(c * LANES, LANES)]


def put_tile(ref, plane, c, row, value):
    ref[plane, pl.ds(row, SUB), pl.ds(c * LANES, LANES)] = value


def put_tables(tables_ref, table_ref, flip):
    turn = jnp.where(splat(flip.astype(jnp.float32)) > 0.5, -0.5, 0.5)
    for phase in range(PHASES):
        k = [splat(table_ref[phase, column]) for column in range(7)]
        size = [jnp.abs(value) for value in k]
        values = (
            0.5 * (k[0] - size[3] - size[4]),
            turn * k[3],
            turn * k[4],
            0.5 * (k[1] - size[3] - size[5]),
            0.5 * (k[2] - size[4] - size[5]),
            0.5 * k[5],
            k[6],
        )
        for place, value in enumerate(values):
            tables_ref[phase, place] = value


def put_factors(factors_ref, bounds_ref):
    inverse, factors = chebyshev(bounds_ref)
    for k, value in enumerate([inverse] + [value for pair in factors for value in pair]):
        factors_ref[k] = value


def get_factors(factors_ref):
    pairs = [(factors_ref[1 + 2 * k], factors_ref[2 + 2 * k]) for k in range(ITERS)]
    return factors_ref[0], pairs


class Half:
    def __init__(self, tables_ref, refs, tiles, rows):
        self.refs, self.tiles, self.rows = refs, tiles, rows
        self.tables = [
            ([tables_ref[phase, k] for k in range(3)], [tables_ref[phase, k] for k in range(3, 7)])
            for phase in range(PHASES)
        ]
        for ref, slots_of in zip(refs, (cross_slots, inplane_slots)):
            for slot in range(ref.shape[0]):
                for k in range(len(slots_of)):
                    for c in range(tiles):
                        for start in (0, SUB, rows + RIM, rows + RIM + SUB):
                            ref[slot, c, k, pl.ds(start, SUB), :] = splat(0.0)

    def fill(self, slot, read, mask=None, reaction=None):
        for group in range(2 if reaction else 1):
            tables = [t[group] for t in self.tables]
            if mask is not None:
                tables = [[mask * value for value in t] for t in tables]
            ref, at = (self.refs[1], 0) if group else (self.refs[0], slot)
            places = inplane_slots if group else cross_slots

            def body(row, carry):
                found = {}
                for c in range(self.tiles):
                    label = read(c, row)
                    bits = [(label & (1 << b)) != 0 for b in range(3)]
                    looked = []
                    for column in range(len(tables[0])):
                        level = [t[column] for t in tables]
                        for bit in bits:
                            level = [jnp.where(bit, b, a) for a, b in zip(level[::2], level[1::2])]
                        looked.append(level[0])
                    if group == 0:
                        values = {0: looked[0]}
                        signed = zip((3, 5), looked[1:])
                    else:
                        values = {1: looked[0], 2: looked[1]}
                        signed = [(7, looked[2])]
                        reaction[0][reaction[1], c, pl.ds(row, SUB), :] = looked[3]
                    for d, value in signed:
                        values[d] = jnp.maximum(value, 0.0)
                        values[d + 1] = jnp.maximum(-value, 0.0)
                    for d, value in values.items():
                        ref[at, c, places[d, 0], pl.ds(row + RIM, SUB), :] = value
                        found.setdefault(d, []).append(value)
                for d, values in found.items():
                    if steps[d][2]:
                        for c, value in enumerate(lane_shifted(values, steps[d][2], splat(0.0))):
                            ref[at, c, places[d, 1], pl.ds(row + RIM, SUB), :] = value
                return carry

            each_block(self.rows, body)

    def link(self, slot, other, out, at):
        directions, places = (cross, cross_slots) if other is not None else (inplane, inplane_slots)
        ref = self.refs[0 if other is not None else 1]
        slot, other = (slot, other) if other is not None else (0, 0)

        def body(row, carry):
            for d in directions:
                _, dy, dz = steps[d]
                near = pl.ds(row + RIM - PAD, SUB)
                far = pl.ds(row + RIM - PAD + dy, SUB)
                ahead = [ref[other, c, places[d, 1 if dz else 0], far, :] for c in range(self.tiles)]
                values = [ref[slot, c, places[d, 0], near, :] + ahead[c] for c in range(self.tiles)]
                for c, value in enumerate(values):
                    out[at, c, places[d, 0], pl.ds(row, SUB), :] = value
                if dz:
                    edge = ref[other, 0 if dz == 1 else self.tiles - 1, places[d, 0], far, :]
                    for c, value in enumerate(lane_shifted(values, -dz, edge)):
                        out[at, c, places[d, 1], pl.ds(row, SUB), :] = value
            return carry

        each_block(self.rows + 2 * PAD, body)


def apply_operator(field, cross_ref, inplane_ref, reaction_ref, planes, tiles, rows, use, parts=None):
    whole = (-1, 0, 1)
    for c in range(tiles):

        def body(row, carry):
            held = {}

            def value(q, dy, dz):
                key = (q, dy, dz)
                if key not in held:
                    held[key] = field[q + HALO, c, dz % 3, pl.ds(row + PAD + dy, SUB), :]
                return held[key]

            for q in planes:
                here = value(q, 0, 0)
                wanted = (parts or {}).get(q, whole)
                sums = [reaction_ref[q + 1, c, pl.ds(row, SUB), :] * here] if 0 in wanted else []
                for d, (dx, dy, dz) in enumerate(steps):
                    places = cross_slots if dx else inplane_slots
                    ref, base = (cross_ref, HALO) if dx else (inplane_ref, 1)
                    for sign in (1, -1):
                        if sign * dx not in wanted:
                            continue
                        if sign == 1:
                            link = ref[q + base, c, places[d, 0], pl.ds(row + PAD, SUB), :]
                        else:
                            key = places[d, 1 if dz else 0]
                            link = ref[q + base - dx, c, key, pl.ds(row + PAD - dy, SUB), :]
                        term = link * (here - value(q + sign * dx, sign * dy, sign * dz))
                        sums = sums[1:] + [sums[0] + term] if len(sums) == 3 else sums + [term]
                carry = use(q, c, row, sums[0] + (sums[1] + sums[2]), here, carry)
            return carry

        yield body


def run_operator(*arguments, carry=0):
    rows = arguments[6]
    for body in apply_operator(*arguments):
        carry = each_block(rows, body, carry, unroll=4)
    return carry


class Device:
    def __init__(self, shape):
        self.depth, self.rows, self.tiles = shape[0], shape[1], shape[2] // LANES
        self.place, self.count = lax.axis_index("gz"), lax.axis_size("gz")
        self.flip = self.place % 2
        joined = jnp.logical_and(self.place > 0, self.place < self.count - 1)
        self.joined = splat(joined.astype(jnp.float32))

    def own(self, q):
        return jnp.where(self.flip == 1, self.depth - 1 - q, q)

    def sent(self, q):
        return jnp.where(self.flip == 1, 1 - q % HALO, q % HALO)

    def halo(self, q):
        far = q >= self.depth
        first = (q == self.depth) if far else (q == -1)
        turned = self.flip == (1 if far else 0)
        return jnp.where(turned, 1, 0) if first else jnp.where(turned, 0, 1)


class Solve:
    def __init__(self, device, refs, factors, right=None):
        self.device, self.refs, self.factors, self.right = device, refs, factors, right

    def subtract(self, iteration, planes, parts=None):
        device = self.device
        first_ref, second_ref, cross_ref, inplane_ref, reaction_ref, rest_ref, _ = self.refs
        field = second_ref if iteration == 1 else first_ref

        def use(q, c, row, image, here, carry):
            if iteration == 0 and not 0 <= q < device.depth:
                rest = self.right(q, c, row) - image
            else:
                rest = rest_ref[q + 1, c, pl.ds(row, SUB), :] - image
            if q < 0:
                rest = rest * device.joined
            rest_ref[q + 1, c, pl.ds(row, SUB), :] = rest
            return carry

        run_operator(
            field, cross_ref, inplane_ref, reaction_ref, planes, device.tiles, device.rows, use, parts
        )

    def direct(self, iteration, planes, copies={}):
        device = self.device
        first_ref, second_ref, _, _, _, rest_ref, sum_ref = self.refs
        old, new = (first_ref, second_ref) if iteration == 0 else (second_ref, first_ref)
        ahead, behind = self.factors[iteration]
        for q in planes:
            if q < 0:
                field_rims(new, q + HALO, device.tiles, device.rows)

            def body(row, carry):
                values = []
                for c in range(device.tiles):
                    here = old[q + HALO, c, 0, pl.ds(row + PAD, SUB), :]
                    value = ahead * here + behind * rest_ref[q + 1, c, pl.ds(row, SUB), :]
                    values.append(value)
                    if q in copies:
                        put_tile(copies[q], 0, c, row, value)
                    if 0 <= q < device.depth and sum_ref is not None:
                        before = here if iteration == 0 else sum_ref[q, c, pl.ds(row, SUB), :]
                        sum_ref[q, c, pl.ds(row, SUB), :] = before + value
                put_field(new, q + HALO, row, values)
                return carry

            each_block(device.rows, body)

    def receive(self, field, q, read):
        field_rims(field, q + HALO, self.device.tiles, self.device.rows)

        def body(row, carry):
            put_field(field, q + HALO, row, [read(c, row) for c in range(self.device.tiles)])
            return carry

        each_block(self.device.rows, body)


def start_kernel(*refs):
    near_labels_ref, near_right_ref, far_labels_ref, far_right_ref, beside_labels_ref, beside_right_ref = refs[:6]
    table_ref, bounds_ref, tables_ref, factors_ref = refs[6:10]
    first_ref, cross_ref, inplane_ref, reaction_ref, rest_ref, second_ref, sum_ref, near_ref, far_ref = refs[10:19]
    halves = refs[19:]
    device = Device((2 * HALO,) + near_labels_ref.shape[1:])
    depth, rows, tiles = device.depth, device.rows, device.tiles
    put_factors(factors_ref, bounds_ref)
    inverse, factors = get_factors(factors_ref)
    put_tables(tables_ref, table_ref, device.flip)
    half = Half(tables_ref, halves, tiles, rows)

    def read(q, near, far, beside):
        if q == depth:
            ref, index = beside, device.halo(q)
        else:
            ref, index = near if q < HALO else far, device.sent(q)
        return lambda c, row: tile(ref, index, c, row)

    for q in range(depth + 1):
        field_rims(first_ref, q + HALO, tiles, rows)
        field_rims(second_ref, q + HALO, tiles, rows)
        right = read(q, near_right_ref, far_right_ref, beside_right_ref)

        def body(row, carry):
            values = [right(c, row) for c in range(tiles)]
            if q < depth:
                for c, value in enumerate(values):
                    rest_ref[q + 1, c, pl.ds(row, SUB), :] = value
            put_field(first_ref, q + HALO, row, [value * inverse for value in values])
            return carry

        each_block(rows, body)
        labels = read(q, near_labels_ref, far_labels_ref, beside_labels_ref)
        half.fill(q % 2, labels, None, (reaction_ref, q + 1) if q < depth else None)
        if q:
            half.link((q - 1) % 2, q % 2, cross_ref, q - 1 + HALO)
        if q < depth:
            half.link(q % 2, None, inplane_ref, q + 1)

    solve = Solve(device, (first_ref, second_ref, cross_ref, inplane_ref, reaction_ref, rest_ref, sum_ref), factors)
    solve.subtract(0, range(1, depth))
    solve.direct(0, range(1, depth), {1: near_ref, depth - 1: far_ref})


def middle_kernel(*refs):
    tables_ref, factors_ref, sent_labels_ref, far_second_ref, near_labels_ref = refs[7:12]
    first_ref, cross_ref, inplane_ref, reaction_ref, rest_ref, second_ref, sum_ref, far_ref, *halves = refs[12:]
    device = Device((2 * HALO,) + near_labels_ref.shape[1:])
    depth = device.depth
    _, factors = get_factors(factors_ref)
    solve = Solve(device, (first_ref, second_ref, cross_ref, inplane_ref, reaction_ref, rest_ref, sum_ref), factors)
    solve.receive(second_ref, depth, lambda c, row: tile(far_second_ref, 0, c, row))
    solve.subtract(1, range(2, depth))
    solve.direct(1, range(2, depth), {depth - 1: far_ref})

    def labels(ref, index):
        return lambda c, row: tile(ref, index, c, row)

    half = Half(tables_ref, halves, device.tiles, device.rows)
    half.fill(0, labels(sent_labels_ref, device.sent(0)))
    half.fill(1, labels(near_labels_ref, device.halo(-1)), device.joined, (reaction_ref, 0))
    half.link(1, None, inplane_ref, 0)
    half.link(1, 0, cross_ref, HALO - 1)
    half.fill(0, labels(near_labels_ref, device.halo(-2)), device.joined)
    half.link(0, 1, cross_ref, HALO - 2)


def late_kernel(*refs):
    cross_ref, inplane_ref, reaction_ref, factors_ref, near_right_ref = refs[4:9]
    first_ref, second_ref, rest_ref, sum_ref, solution_ref = refs[9:]
    device = Device(solution_ref.shape)
    depth = device.depth
    inverse, factors = get_factors(factors_ref)

    def right(q, c, row):
        return tile(near_right_ref, device.halo(q), c, row)

    solve = Solve(
        device, (first_ref, second_ref, cross_ref, inplane_ref, reaction_ref, rest_ref, sum_ref), factors, right
    )
    for q in (-1, -2):
        index = device.halo(q)
        solve.receive(first_ref, q, lambda c, row: tile(near_right_ref, index, c, row) * inverse)
    solve.subtract(0, [-1, 0])
    solve.direct(0, [-1, 0])
    solve.subtract(1, [-1, 0, 1], parts={-1: (0, 1)})
    solve.direct(1, [0, 1])
    solve.subtract(2, range(depth), parts={0: (0, 1), depth - 1: (-1, 0)})
    for c in range(device.tiles):

        def body(row, carry):
            for q in range(depth):
                put_tile(solution_ref, device.own(q), c, row, sum_ref[q, c, pl.ds(row, SUB), :])
            return carry

        each_block(device.rows, body)


def last_kernel(*refs):
    cross_ref, inplane_ref, reaction_ref, factors_ref, near_second_ref, far_third_ref = refs[3:9]
    first_ref, second_ref, rest_ref, residual_ref, squares_ref = refs[9:]
    device = Device(residual_ref.shape)
    depth, rows, tiles = device.depth, device.rows, device.tiles
    _, factors = get_factors(factors_ref)
    solve = Solve(device, (first_ref, second_ref, cross_ref, inplane_ref, reaction_ref, rest_ref, None), factors)
    solve.receive(first_ref, depth, lambda c, row: tile(far_third_ref, 0, c, row))
    solve.receive(second_ref, -2, lambda c, row: tile(near_second_ref, 0, c, row))
    solve.subtract(1, [-1], parts={-1: (-1,)})
    solve.direct(1, [-1])

    def use(q, c, row, image, here, carry):
        for plane in [0] + list(range(1, depth - 1)) if q == 0 else [q]:
            rest = rest_ref[plane + 1, c, pl.ds(row, SUB), :]
            if plane == q:
                rest = rest - image
            put_tile(residual_ref, device.own(plane), c, row, rest)
            carry = carry + rest * rest
        return carry

    total = run_operator(
        first_ref,
        cross_ref,
        inplane_ref,
        reaction_ref,
        [0, depth - 1],
        tiles,
        rows,
        use,
        {0: (-1,), depth - 1: (1,)},
        carry=splat(0.0),
    )
    squares_ref[...] = jnp.broadcast_to(jnp.sum(total), squares_ref.shape)


def per_device(labels, tensor_table, bounds, right_side):
    depth, rows, columns = labels.shape
    if depth != 2 * HALO or columns % LANES or rows % SUB:
        raise ValueError("unsupported block")
    tiles = columns // LANES
    count = lax.axis_size("gz")
    odd = lax.axis_index("gz") % 2

    vmem = pl.BlockSpec(memory_space=pltpu.VMEM)
    smem = pl.BlockSpec(memory_space=pltpu.SMEM)

    def array(*shape):
        return jax.ShapeDtypeStruct(shape, jnp.float32)

    below = rows + PAD + BELOW
    field = array(depth + HALO + 1, tiles, 3, below, LANES)
    cross_links = array(depth + HALO, tiles, len(cross_slots), below, LANES)
    inplane_links = array(depth + 1, tiles, len(inplane_slots), below, LANES)
    reaction = rest = array(depth + 1, tiles, rows, LANES)
    total = array(depth, tiles, rows, LANES)
    plane = array(1, rows, columns)
    block = array(depth, rows, columns)
    tables, factors = array(PHASES, 7, SUB, LANES), array(1 + 2 * ITERS, SUB, LANES)
    halves = [
        pltpu.VMEM((planes, tiles, len(places), rows + RIM + RIM_BELOW, LANES), jnp.float32)
        for planes, places in ((2, cross_slots), (1, inplane_slots))
    ]

    def call(kernel, arguments, out_shape, aliased, limit, flops, scratch=(), scalars=0):
        return pl.pallas_call(
            kernel,
            out_shape=out_shape,
            in_specs=[vmem] * (len(arguments) - scalars) + [smem] * scalars,
            out_specs=[vmem] * len(out_shape),
            scratch_shapes=list(scratch),
            input_output_aliases={k: k for k in range(aliased)},
            compiler_params=pltpu.CompilerParams(vmem_limit_bytes=limit << 20),
            cost_estimate=pl.CostEstimate(flops=flops, bytes_accessed=1 << 20, transcendentals=0),
        )(*arguments)

    inside = [(i, i ^ 1) for i in range(count)]
    across = [(i, i + 1) for i in range(1, count - 1, 2)]
    across += [(j, i) for i, j in across]
    near_start = odd * (depth - HALO)
    far_start = (1 - odd) * (depth - HALO)

    def send(array, pairs):
        return lax.ppermute(array, "gz", pairs)

    def ends(array):
        return [lax.dynamic_slice_in_dim(array, start, HALO, 0) for start in (near_start, far_start)]

    my_labels, my_right = ends(labels), ends(right_side)
    near_labels = send(my_labels[0], across)
    near_right = send(my_right[0], across)
    far_labels = send(my_labels[1], inside)
    far_right = send(my_right[1], inside)

    tables, factors, *state, near, far = call(
        start_kernel,
        (my_labels[0], my_right[0], my_labels[1], my_right[1], far_labels, far_right, tensor_table, bounds),
        (tables, factors, field, cross_links, inplane_links, reaction, rest, field, total, plane, plane),
        0,
        LIMITS[0],
        10**8,
        halves,
        scalars=2,
    )
    near_second = send(near, across)
    far_second = send(far, inside)

    *state, far = call(
        middle_kernel,
        (*state, tables, factors, my_labels[0], far_second, near_labels),
        tuple(array(*s.shape) for s in state) + (plane,),
        7,
        LIMITS[1],
        10**8,
        halves,
    )
    far_third = send(far, inside)
    first, cross_links, inplane_links, reaction, rest, second, total = state
    links = (cross_links, inplane_links, reaction, factors)
    first, second, rest, _, solved = call(
        late_kernel,
        (first, second, rest, total, *links, near_right),
        (field, field, array(*rest.shape), array(*total.shape), block),
        4,
        LIMITS[2],
        10**8,
    )
    *_, residual, squares = call(
        last_kernel,
        (first, second, rest, *links, near_second, far_third),
        (field, field, array(*rest.shape), block, array(count, LANES)),
        3,
        LIMITS[3],
        10**8,
    )
    gathered = lax.all_to_all(squares, "gz", 0, 0, tiled=True)
    return solved, residual, jnp.sqrt(jnp.sum(gathered[:, 0])).reshape(1)


def solution(mesh):
    whole = P(("groups", "gz"), None, None)
    return jax.shard_map(
        per_device,
        mesh=mesh,
        in_specs=(whole, P("groups", None), P("groups"), whole),
        out_specs=(whole, whole, P("groups")),
        check_vma=False,
    )
```

time: 73.4 us -> 65.4 us (0.89)
  Pallas kernels: 39.4 us -> 27.3 us
  blocking collectives: 15.8 us -> 19.4 us
  local copies, waits for them, and re-layouts: 7.02 us -> 3.89 us
  starting transfers between devices: 7.07 us -> 10.2 us
    pallas_call x3 -> x4, Pallas kernels: 39.4 us -> 27.3 us  [call(): pl.pallas_call(kernel, out_shape=out_shape, in_specs=[vmem] * (len(argume...]
    all_to_all x1, blocking collectives: 15.8 us -> 19.4 us  [per_device(): gathered = lax.all_to_all(squares, 'gz', 0, 0, tiled=True)]
    unnamed x10 -> x4, local copies, waits for them, and re-layouts: 4.47 us -> 1.34 us
    ppermute x6 -> x7, starting transfers between devices: 7.07 us -> 10.2 us  [send(): return lax.ppermute(array, 'gz', pairs)]
  transfers between devices with their start and end apart: 6 -> 7, of which waited for: 1 -> 1; matrix products, arithmetic and copies ran while one was open for 2% -> 2% of each run, Pallas kernels for 39% -> 38%
where the time goes in v3:
time: 65.4 us; the launch traced here: 65.1 us
  Pallas kernels  27.3 us (42%)
  blocking collectives  19.4 us (30%)
  starting transfers between devices  10.2 us (16%)
  local copies, waits for them, and re-layouts  3.89 us (6%)
  between operations  2.56 us (4%)
  waiting for transfers between devices  1.2 us (2%)
    pallas_call x4, Pallas kernels, call(): pl.pallas_call(kernel, out_shape=out_shape, in_specs=[vmem] * (len(argume...  27.3 us
    all_to_all x1, blocking collectives, per_device(): gathered = lax.all_to_all(squares, 'gz', 0, 0, tiled=True)  19.4 us
    ppermute x7, starting transfers between devices, send(): return lax.ppermute(array, 'gz', pairs)  10.2 us
    dynamic_slice x2, local copies, waits for them, and re-layouts, ends(): lax.dynamic_slice_in_dim(array, start, HALO, 0)  2.55 us
    unnamed x4, local copies, waits for them, and re-layouts  1.34 us
  transfers between devices with their start and end apart: 7, of which 1 were waited for; matrix products, arithmetic and copies ran while one was open for 2% of the time, Pallas kernels for 38%

profile of v3, /device:TPU:0, one launch (start us, length us, event | category | flops | bytes accessed | tf_op | source)
XLA Modules:
  0.0 65.1 jit_solution(8529383057352911896)
XLA Ops:
  0.7 1.3 %constant_dynamic-slice_fusion.1 = (s32[2,256,256]{2,1,0:T(8,128)S(1)}, s32[2,256,256]{2,1,0:T(8,128)S(1)}) fusion(s32[4,256,256]{2,1,0:T(8,128)} %param.4, s32[]{:T(128)S(6)} %select_n.17, s32[]{:T(128)S(6)} %select_n.16), kind=kLoop, calls=%fused_computation.2 | loop fusion | bytes 2097160 | tf_op jit(solution)/shard_map/dynamic_slice | solution.py:520
  1.9 0.6 collective-permute-start
  2.5 1.3 %constant_dynamic-slice_fusion = (f32[2,256,256]{2,1,0:T(8,128)S(1)}, f32[2,256,256]{2,1,0:T(8,128)S(1)}) fusion(f32[4,256,256]{2,1,0:T(8,128)} %param.7, s32[]{:T(128)S(6)} %select_n.17, s32[]{:T(128)S(6)} %select_n.16), kind=kLoop, calls=%fused_computation.1 | loop fusion | bytes 2097160 | tf_op jit(solution)/shard_map/dynamic_slice | solution.py:520
  3.8 0.1 collective-permute-start.1
  3.9 0.7 %collective-permute-start.3 = (s32[2,256,256]{2,1,0:T(8,128)S(1)}, s32[2,256,256]{2,1,0:T(8,128)S(1)}, u32[]{:S(2)}, u32[]{:S(2)}) collective-permute-start(s32[2,256,256]{2,1,0:T(8,128)S(1)} %get-tuple-element.56.refs_0_.refs_9_), channel_id=1, source_target_pairs={{1,2},{3,4},{5,6},{7,8},{9,10},{11,12},{13,14},{2,1},{4,3},{6,5},{... | collective-permute-start | bytes 1572872 | tf_op jit(solution)/shard_map/ppermute | solution.py:517
  4.6 0.0 collective-permute-done.refs_4_
  4.6 1.2 %collective-permute-done.1.refs_5_ = f32[2,256,256]{2,1,0:T(8,128)S(1)} collective-permute-done((f32[2,256,256]{2,1,0:T(8,128)S(1)}, f32[2,256,256]{2,1,0:T(8,128)S(1)}, u32[]{:S(2)}, u32[]{:S(2)}) %collective-permute-start.1) | collective-permute-done | bytes 524320 | tf_op jit(solution)/shard_map/ppermute | solution.py:517
  5.7 0.0 copy-start
  5.8 0.7 %copy-done = f32[8,7]{1,0:T(8,128)S(1)} copy-done((f32[8,7]{1,0:T(8,128)S(1)}, f32[8,7]{1,0:T(8,128)}, u32[]{:S(2)}) %copy-start) | copy-done | bytes 248
  6.4 0.0 copy-start.1
  6.4 0.7 %copy-done.1 = f32[2]{0:T(128)S(1)} copy-done((f32[2]{0:T(128)S(1)}, f32[2]{0:T(128)}, u32[]{:S(2)}) %copy-start.1) | copy-done | bytes 32
  7.1 11.8 %shard_map.67 = (f32[8,7,8,128]{3,2,1,0:T(8,128)S(1)}, f32[7,8,128]{2,1,0:T(8,128)S(1)}, f32[7,2,3,272,128]{4,3,2,1,0:T(8,128)S(1)}, f32[6,2,7,272,128]{4,3,2,1,...) custom-call(s32[2,256,256]{2,1,0:T(8,128)S(1)} %get-tuple-element.56, ...), custom_call_target="tpu_custom_call" | custom-call | flops 100000000 | bytes 1048576 | tf_op jit(solution)/shard_map/pallas_call | solution.py:499
  18.9 3.2 %collective-permute-start.2 = (f32[1,256,256]{2,1,0:T(8,128)S(1)}, f32[1,256,256]{2,1,0:T(8,128)S(1)}, u32[]{:S(2)}, u32[]{:S(2)}) collective-permute-start(f32[1,256,256]{2,1,0:T(8,128)S(1)} %get-tuple-element.37), channel_id=1, source_target_pairs={{0,1},{1,0},{2,3},{3,2},{4,5},{5,4},{6,7},{7,6},{8,9},{9,8},{10,11... | collective-permute-start | bytes 786440 | tf_op jit(solution)/shard_map/ppermute | solution.py:517
  22.1 0.7 %collective-permute-start.4 = (f32[2,256,256]{2,1,0:T(8,128)S(1)}, f32[2,256,256]{2,1,0:T(8,128)S(1)}, u32[]{:S(2)}, u32[]{:S(2)}) collective-permute-start(f32[2,256,256]{2,1,0:T(8,128)S(1)} %get-tuple-element.54.refs_1_), channel_id=1, source_target_pairs={{1,2},{3,4},{5,6},{7,8},{9,10},{11,12},{13,14},{2,1},{4,3},{6,5},{... | collective-permute-start | bytes 1572872 | tf_op jit(solution)/shard_map/ppermute | solution.py:517
  22.8 0.7 %collective-permute-start.5 = (f32[1,256,256]{2,1,0:T(8,128)S(1)}, f32[1,256,256]{2,1,0:T(8,128)S(1)}, u32[]{:S(2)}, u32[]{:S(2)}) collective-permute-start(f32[1,256,256]{2,1,0:T(8,128)S(1)} %get-tuple-element.49), channel_id=1, source_target_pairs={{1,2},{3,4},{5,6},{7,8},{9,10},{11,12},{13,14},{2,1},{4,3},{6,5},{... | collective-permute-start | bytes 786440 | tf_op jit(solution)/shard_map/ppermute | solution.py:517
  23.5 0.0 collective-permute-done.3.refs_11_
  23.5 0.0 collective-permute-done.2.refs_10_
  23.5 5.0 %shard_map.68 = (f32[7,2,3,272,128]{4,3,2,1,0:T(8,128)S(1)}, f32[6,2,7,272,128]{4,3,2,1,0:T(8,128)S(1)}, f32[5,2,7,272,128]{4,3,2,1,0:T(8,128)S(1)}, f32[5,2,256...) custom-call(f32[7,2,3,272,128]{4,3,2,1,0:T(8,128)S(1)} %get-tuple-el, ...), custom_call_target="tpu_custom_call", output_to_operand_aliasing={{0}: (0, {}), {1}: (1, {}), {2}: (2, {}), {3}: (3, {}), {4}... | custom-call | flops 100000000 | bytes 1048576 | tf_op jit(solution)/shard_map/pallas_call | solution.py:499
  28.5 4.3 %collective-permute-start.6 = (f32[1,256,256]{2,1,0:T(8,128)S(1)}, f32[1,256,256]{2,1,0:T(8,128)S(1)}, u32[]{:S(2)}, u32[]{:S(2)}) collective-permute-start(f32[1,256,256]{2,1,0:T(8,128)S(1)} %get-tuple-element.50), channel_id=1, source_target_pairs={{0,1},{1,0},{2,3},{3,2},{4,5},{5,4},{6,7},{7,6},{8,9},{9,8},{10,11... | collective-permute-start | bytes 786440 | tf_op jit(solution)/shard_map/ppermute | solution.py:517
  32.8 0.0 collective-permute-done.4.refs_8_
  32.8 7.9 %shard_map.69 = (f32[7,2,3,272,128]{4,3,2,1,0:T(8,128)S(1)}, f32[7,2,3,272,128]{4,3,2,1,0:T(8,128)S(1)}, f32[5,2,256,128]{3,2,1,0:T(8,128)S(1)}, f32[4,2,256,128]{3,2,1,0:T(8,128)S(1)}, f32[4,256,256]{2,1,0:T(8,128)}) custom-call(f32[7,2,3,272,128]{4,3,2,1,0:T(8,128)S(1)} %get-tuple-element.3, ...), custom_call_target="tpu_custom_call", output_to_operand_aliasing={{0}: (0, {}), {1}: (1, {}), {2}: (2, {}), {3}: (3, {})} | custom-call | flops 100000000 | bytes 1048576 | tf_op jit(solution)/shard_map/pallas_call | solution.py:499
  40.7 0.0 collective-permute-done.5.refs_7_
  40.7 0.0 collective-permute-done.6.refs_8_
  40.7 2.6 %shard_map.70 = (f32[7,2,3,272,128]{4,3,2,1,0:T(8,128)S(1)}, f32[7,2,3,272,128]{4,3,2,1,0:T(8,128)S(1)}, f32[5,2,256,128]{3,2,1,0:T(8,128)S(1)}, f32[4,256,256]{2,1,0:T(8,128)}, f32[16,128]{1,0:T(8,128)S(1)}) custom-call(f32[7,2,3,272,128]{4,3,2,1,0:T(8,128)S(1)} %get-tuple-element.46.refs_0_, ...), custom_call_target="tpu_custom_call", output_to_operand_aliasing={{0}: (0, {}), {1}: (1, {}), {2}: (2, {})} | custom-call | flops 100000000 | bytes 1048576 | tf_op jit(solution)/shard_map/pallas_call | solution.py:499
  43.3 19.4 %all_to_all.12 = f32[16,1,128]{2,1,0:T(1,128)S(1)} all-to-all(f32[16,1,128]{2,1,0:T(1,128)S(1)} %bitcast.5), channel_id=1, replica_groups=mesh['groups'=2,'gz'=16] {'gz'}, dimensions={0} | all-to-all | bytes 16384 | tf_op jit(solution)/shard_map/all_to_all | solution.py:569
  62.7 0.6 slice_reduce_fusion
Async XLA Ops:
  1.9 2.6 %collective-permute-start = (s32[2,256,256]{2,1,0:T(8,128)S(1)}, s32[2,256,256]{2,1,0:T(8,128)S(1)}, u32[]{:S(2)}, u32[]{:S(2)}) collective-permute-start(s32[2,256,256]{2,1,0:T(8,128)S(1)} %get-tuple-element.55.refs_2_), channel_id=1, source_target_pairs={{0,1},{1,0},{2,3},{3,2},{4,5},{5,4},{6,7},{7,6},{8,9},{9,8},{10,11... | collective-permute-start | bytes 1572872 | tf_op jit(solution)/shard_map/ppermute | solution.py:517
  3.8 2.0 %collective-permute-start.1 = (f32[2,256,256]{2,1,0:T(8,128)S(1)}, f32[2,256,256]{2,1,0:T(8,128)S(1)}, u32[]{:S(2)}, u32[]{:S(2)}) collective-permute-start(f32[2,256,256]{2,1,0:T(8,128)S(1)} %get-tuple-element.53.refs_3_), channel_id=1, source_target_pairs={{0,1},{1,0},{2,3},{3,2},{4,5},{5,4},{6,7},{7,6},{8,9},{9,8},{10,11... | collective-permute-start | bytes 1572872 | tf_op jit(solution)/shard_map/ppermute | solution.py:517
  3.9 19.6 %collective-permute-start.3 = (s32[2,256,256]{2,1,0:T(8,128)S(1)}, s32[2,256,256]{2,1,0:T(8,128)S(1)}, u32[]{:S(2)}, u32[]{:S(2)}) collective-permute-start(s32[2,256,256]{2,1,0:T(8,128)S(1)} %get-tuple-element.56.refs_0_.refs_9_), channel_id=1, source_target_pairs={{1,2},{3,4},{5,6},{7,8},{9,10},{11,12},{13,14},{2,1},{4,3},{6,5},{... | collective-permute-start | bytes 1572872 | tf_op jit(solution)/shard_map/ppermute | solution.py:517
  5.7 0.7 %copy-start = (f32[8,7]{1,0:T(8,128)S(1)}, f32[8,7]{1,0:T(8,128)}, u32[]{:S(2)}) copy-start(f32[8,7]{1,0:T(8,128)} %refs_6_.1) | copy-start | bytes 676
  6.4 0.7 %copy-start.1 = (f32[2]{0:T(128)S(1)}, f32[2]{0:T(128)}, u32[]{:S(2)}) copy-start(f32[2]{0:T(128)} %refs_7_.1) | copy-start | bytes 28
  18.9 4.6 %collective-permute-start.2 = (f32[1,256,256]{2,1,0:T(8,128)S(1)}, f32[1,256,256]{2,1,0:T(8,128)S(1)}, u32[]{:S(2)}, u32[]{:S(2)}) collective-permute-start(f32[1,256,256]{2,1,0:T(8,128)S(1)} %get-tuple-element.37), channel_id=1, source_target_pairs={{0,1},{1,0},{2,3},{3,2},{4,5},{5,4},{6,7},{7,6},{8,9},{9,8},{10,11... | collective-permute-start | bytes 786440 | tf_op jit(solution)/shard_map/ppermute | solution.py:517
  22.1 10.7 %collective-permute-start.4 = (f32[2,256,256]{2,1,0:T(8,128)S(1)}, f32[2,256,256]{2,1,0:T(8,128)S(1)}, u32[]{:S(2)}, u32[]{:S(2)}) collective-permute-start(f32[2,256,256]{2,1,0:T(8,128)S(1)} %get-tuple-element.54.refs_1_), channel_id=1, source_target_pairs={{1,2},{3,4},{5,6},{7,8},{9,10},{11,12},{13,14},{2,1},{4,3},{6,5},{... | collective-permute-start | bytes 1572872 | tf_op jit(solution)/shard_map/ppermute | solution.py:517
  22.8 17.9 %collective-permute-start.5 = (f32[1,256,256]{2,1,0:T(8,128)S(1)}, f32[1,256,256]{2,1,0:T(8,128)S(1)}, u32[]{:S(2)}, u32[]{:S(2)}) collective-permute-start(f32[1,256,256]{2,1,0:T(8,128)S(1)} %get-tuple-element.49), channel_id=1, source_target_pairs={{1,2},{3,4},{5,6},{7,8},{9,10},{11,12},{13,14},{2,1},{4,3},{6,5},{... | collective-permute-start | bytes 786440 | tf_op jit(solution)/shard_map/ppermute | solution.py:517
  28.5 12.2 %collective-permute-start.6 = (f32[1,256,256]{2,1,0:T(8,128)S(1)}, f32[1,256,256]{2,1,0:T(8,128)S(1)}, u32[]{:S(2)}, u32[]{:S(2)}) collective-permute-start(f32[1,256,256]{2,1,0:T(8,128)S(1)} %get-tuple-element.50), channel_id=1, source_target_pairs={{0,1},{1,0},{2,3},{3,2},{4,5},{5,4},{6,7},{7,6},{8,9},{9,8},{10,11... | collective-permute-start | bytes 786440 | tf_op jit(solution)/shard_map/ppermute | solution.py:517

commit v4 on v3

--- a/solution.py
+++ b/solution.py
@@ -15,6 +15,7 @@
 RIM = 16
 RIM_BELOW = 24
 HALO = 2
+OPERATOR_UNROLL = 8
 LIMITS = (8, 8, 5, 5)
 
 steps = (
@@ -207,50 +208,46 @@
                         out[at, c, places[d, 1], pl.ds(row, SUB), :] = value
             return carry
 
-        each_block(self.rows + 2 * PAD, body)
-
-
-def apply_operator(field, cross_ref, inplane_ref, reaction_ref, planes, tiles, rows, use, parts=None):
-    whole = (-1, 0, 1)
-    for c in range(tiles):
-
-        def body(row, carry):
-            held = {}
-
-            def value(q, dy, dz):
-                key = (q, dy, dz)
-                if key not in held:
-                    held[key] = field[q + HALO, c, dz % 3, pl.ds(row + PAD + dy, SUB), :]
-                return held[key]
-
-            for q in planes:
-                here = value(q, 0, 0)
-                wanted = (parts or {}).get(q, whole)
-                sums = [reaction_ref[q + 1, c, pl.ds(row, SUB), :] * here] if 0 in wanted else []
-                for d, (dx, dy, dz) in enumerate(steps):
-                    places = cross_slots if dx else inplane_slots
-                    ref, base = (cross_ref, HALO) if dx else (inplane_ref, 1)
-                    for sign in (1, -1):
-                        if sign * dx not in wanted:
-                            continue
-                        if sign == 1:
-                            link = ref[q + base, c, places[d, 0], pl.ds(row + PAD, SUB), :]
-                        else:
-                            key = places[d, 1 if dz else 0]
-                            link = ref[q + base - dx, c, key, pl.ds(row + PAD - dy, SUB), :]
-                        term = link * (here - value(q + sign * dx, sign * dy, sign * dz))
-                        sums = sums[1:] + [sums[0] + term] if len(sums) == 3 else sums + [term]
-                carry = use(q, c, row, sums[0] + (sums[1] + sums[2]), here, carry)
-            return carry
-
-        yield body
-
-
-def run_operator(*arguments, carry=0):
-    rows = arguments[6]
-    for body in apply_operator(*arguments):
-        carry = each_block(rows, body, carry, unroll=4)
-    return carry
+        each_block(self.rows + 2 * PAD, body, unroll=17)
+
+
+def run_operator(field, links, planes, device, use, parts={}, carry=0):
+    cross_ref, inplane_ref, reaction_ref = links
+
+    def body(row, carry):
+        held = {}
+
+        def value(q, c, dy, dz):
+            key = (q, c, dy, dz)
+            if key not in held:
+                held[key] = field[q + HALO, c, dz % 3, pl.ds(row + PAD + dy, SUB), :]
+            return held[key]
+
+        def image(q, c):
+            here = value(q, c, 0, 0)
+            wanted = parts.get(q, (-1, 0, 1))
+            sums = [reaction_ref[q + 1, c, pl.ds(row, SUB), :] * here] if 0 in wanted else []
+            for d, (dx, dy, dz) in enumerate(steps):
+                places = cross_slots if dx else inplane_slots
+                ref, base = (cross_ref, HALO) if dx else (inplane_ref, 1)
+                for sign in (1, -1):
+                    if sign * dx not in wanted:
+                        continue
+                    if sign == 1:
+                        link = ref[q + base, c, places[d, 0], pl.ds(row + PAD, SUB), :]
+                    else:
+                        key = places[d, 1 if dz else 0]
+                        link = ref[q + base - dx, c, key, pl.ds(row + PAD - dy, SUB), :]
+                    term = link * (here - value(q + sign * dx, c, sign * dy, sign * dz))
+                    sums = sums[1:] + [sums[0] + term] if len(sums) == 3 else sums + [term]
+            return sums[0] + (sums[1] + sums[2])
+
+        for q in planes:
+            images = [image(q, c) for c in range(device.tiles)]
+            carry = use(q, row, images, [value(q, c, 0, 0) for c in range(device.tiles)], carry)
+        return carry
+
+    return each_block(device.rows, body, carry, unroll=OPERATOR_UNROLL)
 
 
 class Device:
@@ -276,51 +273,42 @@
 
 class Solve:
     def __init__(self, device, refs, factors, right=None):
-        self.device, self.refs, self.factors, self.right = device, refs, factors, right
-
-    def subtract(self, iteration, planes, parts=None):
-        device = self.device
-        first_ref, second_ref, cross_ref, inplane_ref, reaction_ref, rest_ref, _ = self.refs
-        field = second_ref if iteration == 1 else first_ref
-
-        def use(q, c, row, image, here, carry):
-            if iteration == 0 and not 0 <= q < device.depth:
-                rest = self.right(q, c, row) - image
-            else:
-                rest = rest_ref[q + 1, c, pl.ds(row, SUB), :] - image
-            if q < 0:
-                rest = rest * device.joined
-            rest_ref[q + 1, c, pl.ds(row, SUB), :] = rest
-            return carry
-
-        run_operator(
-            field, cross_ref, inplane_ref, reaction_ref, planes, device.tiles, device.rows, use, parts
-        )
-
-    def direct(self, iteration, planes, copies={}):
-        device = self.device
-        first_ref, second_ref, _, _, _, rest_ref, sum_ref = self.refs
-        old, new = (first_ref, second_ref) if iteration == 0 else (second_ref, first_ref)
+        self.device, self.factors, self.right = device, factors, right
+        self.first, self.second, *self.links, self.rest = refs
+
+    def advance(self, iteration, planes, direct=(), parts={}, copies={}, keep=None):
+        device, rest_ref = self.device, self.rest
+        old, new = (self.first, self.second) if iteration == 0 else (self.second, self.first)
         ahead, behind = self.factors[iteration]
-        for q in planes:
+        if iteration == 2:
+            old, new = new, old
+        for q in direct:
             if q < 0:
                 field_rims(new, q + HALO, device.tiles, device.rows)
 
-            def body(row, carry):
-                values = []
-                for c in range(device.tiles):
-                    here = old[q + HALO, c, 0, pl.ds(row + PAD, SUB), :]
-                    value = ahead * here + behind * rest_ref[q + 1, c, pl.ds(row, SUB), :]
-                    values.append(value)
-                    if q in copies:
-                        put_tile(copies[q], 0, c, row, value)
-                    if 0 <= q < device.depth and sum_ref is not None:
-                        before = here if iteration == 0 else sum_ref[q, c, pl.ds(row, SUB), :]
-                        sum_ref[q, c, pl.ds(row, SUB), :] = before + value
+        def use(q, row, images, here, carry):
+            block = pl.ds(row, SUB)
+            if self.right and iteration == 0 and q < 0:
+                before = [self.right(q, c, row) for c in range(device.tiles)]
+            else:
+                before = [rest_ref[q + 1, c, block, :] for c in range(device.tiles)]
+            rest = [b - image for b, image in zip(before, images)]
+            if q < 0:
+                rest = [device.joined * r for r in rest]
+            for c, r in enumerate(rest):
+                rest_ref[q + 1, c, block, :] = r
+            if q in direct:
+                values = [ahead * h + behind * r for h, r in zip(here, rest)]
+                if q in copies:
+                    for c, v in enumerate(values):
+                        put_tile(copies[q], 0, c, row, v)
+                if keep and 0 <= q:
+                    for c, (h, v) in enumerate(zip(here, values)):
+                        keep(q, c, row, new[q + HALO, c, 0, pl.ds(row + PAD, SUB), :] + h + v)
                 put_field(new, q + HALO, row, values)
-                return carry
-
-            each_block(device.rows, body)
+            return carry
+
+        run_operator(old, self.links, planes, device, use, parts)
 
     def receive(self, field, q, read):
         field_rims(field, q + HALO, self.device.tiles, self.device.rows)
@@ -335,8 +323,8 @@
 def start_kernel(*refs):
     near_labels_ref, near_right_ref, far_labels_ref, far_right_ref, beside_labels_ref, beside_right_ref = refs[:6]
     table_ref, bounds_ref, tables_ref, factors_ref = refs[6:10]
-    first_ref, cross_ref, inplane_ref, reaction_ref, rest_ref, second_ref, sum_ref, near_ref, far_ref = refs[10:19]
-    halves = refs[19:]
+    first_ref, cross_ref, inplane_ref, reaction_ref, rest_ref, second_ref, near_ref, far_ref = refs[10:18]
+    halves = refs[18:]
     device = Device((2 * HALO,) + near_labels_ref.shape[1:])
     depth, rows, tiles = device.depth, device.rows, device.tiles
     put_factors(factors_ref, bounds_ref)
@@ -372,21 +360,23 @@
         if q < depth:
             half.link(q % 2, None, inplane_ref, q + 1)
 
-    solve = Solve(device, (first_ref, second_ref, cross_ref, inplane_ref, reaction_ref, rest_ref, sum_ref), factors)
-    solve.subtract(0, range(1, depth))
-    solve.direct(0, range(1, depth), {1: near_ref, depth - 1: far_ref})
+    solve = Solve(device, (first_ref, second_ref, cross_ref, inplane_ref, reaction_ref, rest_ref), factors)
+    solve.advance(0, range(1, depth), range(1, depth), copies={1: near_ref, depth - 1: far_ref})
 
 
 def middle_kernel(*refs):
-    tables_ref, factors_ref, sent_labels_ref, far_second_ref, near_labels_ref = refs[7:12]
-    first_ref, cross_ref, inplane_ref, reaction_ref, rest_ref, second_ref, sum_ref, far_ref, *halves = refs[12:]
+    tables_ref, factors_ref, sent_labels_ref, far_second_ref, near_labels_ref = refs[6:11]
+    first_ref, cross_ref, inplane_ref, reaction_ref, rest_ref, second_ref, far_ref, sum_ref, *halves = refs[11:]
     device = Device((2 * HALO,) + near_labels_ref.shape[1:])
     depth = device.depth
     _, factors = get_factors(factors_ref)
-    solve = Solve(device, (first_ref, second_ref, cross_ref, inplane_ref, reaction_ref, rest_ref, sum_ref), factors)
+    solve = Solve(device, (first_ref, second_ref, cross_ref, inplane_ref, reaction_ref, rest_ref), factors)
     solve.receive(second_ref, depth, lambda c, row: tile(far_second_ref, 0, c, row))
-    solve.subtract(1, range(2, depth))
-    solve.direct(1, range(2, depth), {depth - 1: far_ref})
+
+    def keep(q, c, row, value):
+        put_tile(sum_ref, q - HALO, c, row, value)
+
+    solve.advance(1, range(HALO, depth), range(HALO, depth), copies={depth - 1: far_ref}, keep=keep)
 
     def labels(ref, index):
         return lambda c, row: tile(ref, index, c, row)
@@ -401,70 +391,83 @@
 
 
 def late_kernel(*refs):
-    cross_ref, inplane_ref, reaction_ref, factors_ref, near_right_ref = refs[4:9]
-    first_ref, second_ref, rest_ref, sum_ref, solution_ref = refs[9:]
+    *links, factors_ref, near_right_ref, sum_ref = refs[3:9]
+    first_ref, second_ref, rest_ref, solution_ref, ready_ref, sems = refs[9:]
     device = Device(solution_ref.shape)
     depth = device.depth
     inverse, factors = get_factors(factors_ref)
+    copies = [
+        pltpu.make_async_copy(
+            ready_ref.at[q] if q < HALO else sum_ref.at[q - HALO], solution_ref.at[device.own(q)], sems.at[q]
+        )
+        for q in range(depth)
+    ]
+    for copy in copies[HALO:]:
+        copy.start()
 
     def right(q, c, row):
         return tile(near_right_ref, device.halo(q), c, row)
 
-    solve = Solve(
-        device, (first_ref, second_ref, cross_ref, inplane_ref, reaction_ref, rest_ref, sum_ref), factors, right
-    )
+    def keep(q, c, row, value):
+        put_tile(ready_ref, q, c, row, value)
+
+    solve = Solve(device, (first_ref, second_ref, *links, rest_ref), factors, right)
     for q in (-1, -2):
         index = device.halo(q)
         solve.receive(first_ref, q, lambda c, row: tile(near_right_ref, index, c, row) * inverse)
-    solve.subtract(0, [-1, 0])
-    solve.direct(0, [-1, 0])
-    solve.subtract(1, [-1, 0, 1], parts={-1: (0, 1)})
-    solve.direct(1, [0, 1])
-    solve.subtract(2, range(depth), parts={0: (0, 1), depth - 1: (-1, 0)})
-    for c in range(device.tiles):
-
-        def body(row, carry):
-            for q in range(depth):
-                put_tile(solution_ref, device.own(q), c, row, sum_ref[q, c, pl.ds(row, SUB), :])
-            return carry
-
-        each_block(device.rows, body)
+    solve.advance(0, [-1, 0], [-1, 0])
+    solve.advance(1, [-1, 0, 1], [0, 1], parts={-1: (0, 1)}, keep=keep)
+    for copy in copies[:HALO]:
+        copy.start()
+    solve.advance(2, range(depth), parts={0: (0, 1), depth - 1: (-1, 0)})
+    for copy in copies:
+        copy.wait()
 
 
 def last_kernel(*refs):
-    cross_ref, inplane_ref, reaction_ref, factors_ref, near_second_ref, far_third_ref = refs[3:9]
-    first_ref, second_ref, rest_ref, residual_ref, squares_ref = refs[9:]
+    *links, factors_ref, near_second_ref, far_third_ref = refs[3:9]
+    first_ref, second_ref, rest_ref, residual_ref, squares_ref, sems = refs[9:]
     device = Device(residual_ref.shape)
-    depth, rows, tiles = device.depth, device.rows, device.tiles
+    depth = device.depth
+    copies = {
+        q: [
+            pltpu.make_async_copy(
+                rest_ref.at[q + 1, c],
+                residual_ref.at[device.own(q), :, pl.ds(c * LANES, LANES)],
+                sems.at[q, c],
+            )
+            for c in range(device.tiles)
+        ]
+        for q in range(depth)
+    }
+    for q in range(1, depth - 1):
+        for copy in copies[q]:
+            copy.start()
     _, factors = get_factors(factors_ref)
-    solve = Solve(device, (first_ref, second_ref, cross_ref, inplane_ref, reaction_ref, rest_ref, None), factors)
+    solve = Solve(device, (first_ref, second_ref, *links, rest_ref), factors)
     solve.receive(first_ref, depth, lambda c, row: tile(far_third_ref, 0, c, row))
     solve.receive(second_ref, -2, lambda c, row: tile(near_second_ref, 0, c, row))
-    solve.subtract(1, [-1], parts={-1: (-1,)})
-    solve.direct(1, [-1])
-
-    def use(q, c, row, image, here, carry):
-        for plane in [0] + list(range(1, depth - 1)) if q == 0 else [q]:
-            rest = rest_ref[plane + 1, c, pl.ds(row, SUB), :]
-            if plane == q:
-                rest = rest - image
-            put_tile(residual_ref, device.own(plane), c, row, rest)
-            carry = carry + rest * rest
+    solve.advance(1, [-1], [-1], parts={-1: (-1,)})
+
+    def use(q, row, images, here, carry):
+        for c, image in enumerate(images):
+            for plane in range(depth - 1) if q == 0 else [q]:
+                rest = rest_ref[plane + 1, c, pl.ds(row, SUB), :]
+                if plane == q:
+                    rest = rest - image
+                    rest_ref[plane + 1, c, pl.ds(row, SUB), :] = rest
+                carry = carry + rest * rest
         return carry
 
-    total = run_operator(
-        first_ref,
-        cross_ref,
-        inplane_ref,
-        reaction_ref,
-        [0, depth - 1],
-        tiles,
-        rows,
-        use,
-        {0: (-1,), depth - 1: (1,)},
-        carry=splat(0.0),
-    )
+    ends = {0: (-1,), depth - 1: (1,)}
+    total = run_operator(first_ref, links, list(ends), device, use, ends, splat(0.0))
+    for q in ends:
+        for copy in copies[q]:
+            copy.start()
     squares_ref[...] = jnp.broadcast_to(jnp.sum(total), squares_ref.shape)
+    for q in range(depth):
+        for copy in copies[q]:
+            copy.wait()
 
 
 def per_device(labels, tensor_table, bounds, right_side):
@@ -477,6 +480,7 @@
 
     vmem = pl.BlockSpec(memory_space=pltpu.VMEM)
     smem = pl.BlockSpec(memory_space=pltpu.SMEM)
+    hbm = pl.BlockSpec(memory_space=pltpu.HBM)
 
     def array(*shape):
         return jax.ShapeDtypeStruct(shape, jnp.float32)
@@ -486,7 +490,7 @@
     cross_links = array(depth + HALO, tiles, len(cross_slots), below, LANES)
     inplane_links = array(depth + 1, tiles, len(inplane_slots), below, LANES)
     reaction = rest = array(depth + 1, tiles, rows, LANES)
-    total = array(depth, tiles, rows, LANES)
+    inner = array(depth - HALO, rows, columns)
     plane = array(1, rows, columns)
     block = array(depth, rows, columns)
     tables, factors = array(PHASES, 7, SUB, LANES), array(1 + 2 * ITERS, SUB, LANES)
@@ -495,12 +499,12 @@
         for planes, places in ((2, cross_slots), (1, inplane_slots))
     ]
 
-    def call(kernel, arguments, out_shape, aliased, limit, flops, scratch=(), scalars=0):
+    def call(kernel, arguments, out_shape, aliased, limit, flops, scratch=(), smem_count=0, kept=None):
         return pl.pallas_call(
             kernel,
             out_shape=out_shape,
-            in_specs=[vmem] * (len(arguments) - scalars) + [smem] * scalars,
-            out_specs=[vmem] * len(out_shape),
+            in_specs=[vmem] * (len(arguments) - smem_count) + [smem] * smem_count,
+            out_specs=[hbm if k == kept else vmem for k in range(len(out_shape))],
             scratch_shapes=list(scratch),
             input_output_aliases={k: k for k in range(aliased)},
             compiler_params=pltpu.CompilerParams(vmem_limit_bytes=limit << 20),
@@ -528,35 +532,37 @@
     tables, factors, *state, near, far = call(
         start_kernel,
         (my_labels[0], my_right[0], my_labels[1], my_right[1], far_labels, far_right, tensor_table, bounds),
-        (tables, factors, field, cross_links, inplane_links, reaction, rest, field, total, plane, plane),
+        (tables, factors, field, cross_links, inplane_links, reaction, rest, field, plane, plane),
         0,
         LIMITS[0],
         10**8,
         halves,
-        scalars=2,
+        smem_count=2,
     )
+    far_second = send(far, inside)
     near_second = send(near, across)
-    far_second = send(far, inside)
-
-    *state, far = call(
+
+    *state, far, summed = call(
         middle_kernel,
         (*state, tables, factors, my_labels[0], far_second, near_labels),
-        tuple(array(*s.shape) for s in state) + (plane,),
-        7,
+        tuple(array(*s.shape) for s in state) + (plane, inner),
+        6,
         LIMITS[1],
         10**8,
         halves,
     )
     far_third = send(far, inside)
-    first, cross_links, inplane_links, reaction, rest, second, total = state
+    first, cross_links, inplane_links, reaction, rest, second = state
     links = (cross_links, inplane_links, reaction, factors)
-    first, second, rest, _, solved = call(
+    first, second, rest, solved = call(
         late_kernel,
-        (first, second, rest, total, *links, near_right),
-        (field, field, array(*rest.shape), array(*total.shape), block),
-        4,
+        (first, second, rest, *links, near_right, summed),
+        (field, field, array(*rest.shape), block),
+        3,
         LIMITS[2],
         10**8,
+        [pltpu.VMEM((HALO, rows, columns), jnp.float32), pltpu.SemaphoreType.DMA((depth,))],
+        kept=3,
     )
     *_, residual, squares = call(
         last_kernel,
@@ -565,6 +571,8 @@
         3,
         LIMITS[3],
         10**8,
+        [pltpu.SemaphoreType.DMA((depth, tiles))],
+        kept=3,
     )
     gathered = lax.all_to_all(squares, "gz", 0, 0, tiled=True)
     return solved, residual, jnp.sqrt(jnp.sum(gathered[:, 0])).reshape(1)

time: 65.4 us -> 62 us (0.948)
  Pallas kernels: 27.3 us -> 23.3 us
    pallas_call x4, Pallas kernels: 27.3 us -> 23.3 us  [call(): pl.pallas_call(kernel, out_shape=out_shape, in_specs=[vmem] * (len(argume...]
  transfers between devices with their start and end apart: 7 -> 7, of which waited for: 1 -> 1; matrix products, arithmetic and copies ran while one was open for 2% -> 2% of each run, Pallas kernels for 38% -> 34%
where the time goes in v4:
time: 62 us; the launch traced here: 61.7 us
  Pallas kernels  23.3 us (38%)
  blocking collectives  19.9 us (32%)
  starting transfers between devices  10.2 us (16%)
  local copies, waits for them, and re-layouts  3.89 us (6%)
  between operations  2.58 us (4%)
  waiting for transfers between devices  1.2 us (2%)
    pallas_call x4, Pallas kernels, call(): pl.pallas_call(kernel, out_shape=out_shape, in_specs=[vmem] * (len(argume...  23.3 us
    all_to_all x1, blocking collectives, per_device(): gathered = lax.all_to_all(squares, 'gz', 0, 0, tiled=True)  19.9 us
    ppermute x7, starting transfers between devices, send(): return lax.ppermute(array, 'gz', pairs)  10.2 us
    dynamic_slice x2, local copies, waits for them, and re-layouts, ends(): lax.dynamic_slice_in_dim(array, start, HALO, 0)  2.55 us
    unnamed x4, local copies, waits for them, and re-layouts  1.34 us
  transfers between devices with their start and end apart: 7, of which 1 were waited for; matrix products, arithmetic and copies ran while one was open for 2% of the time, Pallas kernels for 34%

profile of v4, /device:TPU:0, one launch (start us, length us, event | category | flops | bytes accessed | tf_op | source)
XLA Modules:
  0.0 61.7 jit_solution(1068380397246863178)
XLA Ops:
  0.7 1.3 %constant_dynamic-slice_fusion.1 = (s32[2,256,256]{2,1,0:T(8,128)S(1)}, s32[2,256,256]{2,1,0:T(8,128)S(1)}) fusion(s32[4,256,256]{2,1,0:T(8,128)} %param.4, s32[]{:T(128)S(6)} %select_n.17, s32[]{:T(128)S(6)} %select_n.16), kind=kLoop, calls=%fused_computation.2 | loop fusion | bytes 2097160 | tf_op jit(solution)/shard_map/dynamic_slice | solution.py:524
  1.9 0.6 collective-permute-start
  2.5 1.3 %constant_dynamic-slice_fusion = (f32[2,256,256]{2,1,0:T(8,128)S(1)}, f32[2,256,256]{2,1,0:T(8,128)S(1)}) fusion(f32[4,256,256]{2,1,0:T(8,128)} %param.7, s32[]{:T(128)S(6)} %select_n.17, s32[]{:T(128)S(6)} %select_n.16), kind=kLoop, calls=%fused_computation.1 | loop fusion | bytes 2097160 | tf_op jit(solution)/shard_map/dynamic_slice | solution.py:524
  3.8 0.1 collective-permute-start.1
  3.9 0.7 %collective-permute-start.3 = (s32[2,256,256]{2,1,0:T(8,128)S(1)}, s32[2,256,256]{2,1,0:T(8,128)S(1)}, u32[]{:S(2)}, u32[]{:S(2)}) collective-permute-start(s32[2,256,256]{2,1,0:T(8,128)S(1)} %get-tuple-element.54.refs_0_.refs_8_), channel_id=1, source_target_pairs={{1,2},{3,4},{5,6},{7,8},{9,10},{11,12},{13,14},{2,1},{4,3},{6,5},{... | collective-permute-start | bytes 1572872 | tf_op jit(solution)/shard_map/ppermute | solution.py:521
  4.6 0.0 collective-permute-done.refs_4_
  4.6 1.2 %collective-permute-done.1.refs_5_ = f32[2,256,256]{2,1,0:T(8,128)S(1)} collective-permute-done((f32[2,256,256]{2,1,0:T(8,128)S(1)}, f32[2,256,256]{2,1,0:T(8,128)S(1)}, u32[]{:S(2)}, u32[]{:S(2)}) %collective-permute-start.1) | collective-permute-done | bytes 524320 | tf_op jit(solution)/shard_map/ppermute | solution.py:521
  5.7 0.0 copy-start
  5.8 0.7 %copy-done = f32[8,7]{1,0:T(8,128)S(1)} copy-done((f32[8,7]{1,0:T(8,128)S(1)}, f32[8,7]{1,0:T(8,128)}, u32[]{:S(2)}) %copy-start) | copy-done | bytes 248
  6.4 0.0 copy-start.1
  6.4 0.7 %copy-done.1 = f32[2]{0:T(128)S(1)} copy-done((f32[2]{0:T(128)S(1)}, f32[2]{0:T(128)}, u32[]{:S(2)}) %copy-start.1) | copy-done | bytes 32
  7.1 10.8 %shard_map.67 = (f32[8,7,8,128]{3,2,1,0:T(8,128)S(1)}, f32[7,8,128]{2,1,0:T(8,128)S(1)}, f32[7,2,3,272,128]{4,3,2,1,0:T(8,128)S(1)}, f32[6,2,7,272,128]{4,3,2,1,...) custom-call(s32[2,256,256]{2,1,0:T(8,128)S(1)} %get-tuple-element.54, ...), custom_call_target="tpu_custom_call" | custom-call | flops 100000000 | bytes 1048576 | tf_op jit(solution)/shard_map/pallas_call | solution.py:503
  17.9 3.2 %collective-permute-start.2 = (f32[1,256,256]{2,1,0:T(8,128)S(1)}, f32[1,256,256]{2,1,0:T(8,128)S(1)}, u32[]{:S(2)}, u32[]{:S(2)}) collective-permute-start(f32[1,256,256]{2,1,0:T(8,128)S(1)} %get-tuple-element.35), channel_id=1, source_target_pairs={{0,1},{1,0},{2,3},{3,2},{4,5},{5,4},{6,7},{7,6},{8,9},{9,8},{10,11... | collective-permute-start | bytes 786440 | tf_op jit(solution)/shard_map/ppermute | solution.py:521
  21.1 0.7 %collective-permute-start.4 = (f32[2,256,256]{2,1,0:T(8,128)S(1)}, f32[2,256,256]{2,1,0:T(8,128)S(1)}, u32[]{:S(2)}, u32[]{:S(2)}) collective-permute-start(f32[2,256,256]{2,1,0:T(8,128)S(1)} %get-tuple-element.52.refs_1_), channel_id=1, source_target_pairs={{1,2},{3,4},{5,6},{7,8},{9,10},{11,12},{13,14},{2,1},{4,3},{6,5},{... | collective-permute-start | bytes 1572872 | tf_op jit(solution)/shard_map/ppermute | solution.py:521
  21.8 0.7 %collective-permute-start.5 = (f32[1,256,256]{2,1,0:T(8,128)S(1)}, f32[1,256,256]{2,1,0:T(8,128)S(1)}, u32[]{:S(2)}, u32[]{:S(2)}) collective-permute-start(f32[1,256,256]{2,1,0:T(8,128)S(1)} %get-tuple-element.47), channel_id=1, source_target_pairs={{1,2},{3,4},{5,6},{7,8},{9,10},{11,12},{13,14},{2,1},{4,3},{6,5},{... | collective-permute-start | bytes 786440 | tf_op jit(solution)/shard_map/ppermute | solution.py:521
  22.4 0.0 collective-permute-done.3.refs_10_
  22.4 0.0 collective-permute-done.2.refs_9_
  22.5 4.5 %shard_map.68 = (f32[7,2,3,272,128]{4,3,2,1,0:T(8,128)S(1)}, f32[6,2,7,272,128]{4,3,2,1,0:T(8,128)S(1)}, f32[5,2,7,272,128]{4,3,2,1,0:T(8,128)S(1)}, f32[5,2,256...) custom-call(f32[7,2,3,272,128]{4,3,2,1,0:T(8,128)S(1)} %get-tuple-el, ...), custom_call_target="tpu_custom_call", output_to_operand_aliasing={{0}: (0, {}), {1}: (1, {}), {2}: (2, {}), {3}: (3, {}), {4}... | custom-call | flops 100000000 | bytes 1048576 | tf_op jit(solution)/shard_map/pallas_call | solution.py:503
  26.9 4.3 %collective-permute-start.6 = (f32[1,256,256]{2,1,0:T(8,128)S(1)}, f32[1,256,256]{2,1,0:T(8,128)S(1)}, u32[]{:S(2)}, u32[]{:S(2)}) collective-permute-start(f32[1,256,256]{2,1,0:T(8,128)S(1)} %get-tuple-element.48), channel_id=1, source_target_pairs={{0,1},{1,0},{2,3},{3,2},{4,5},{5,4},{6,7},{7,6},{8,9},{9,8},{10,11... | collective-permute-start | bytes 786440 | tf_op jit(solution)/shard_map/ppermute | solution.py:521
  31.2 0.0 collective-permute-done.4.refs_7_
  31.2 5.7 %shard_map.69 = (f32[7,2,3,272,128]{4,3,2,1,0:T(8,128)S(1)}, f32[7,2,3,272,128]{4,3,2,1,0:T(8,128)S(1)}, f32[5,2,256,128]{3,2,1,0:T(8,128)S(1)}, f32[4,256,256]{2,1,0:T(8,128)}) custom-call(f32[7,2,3,272,128]{4,3,2,1,0:T(8,128)S(1)} %get-tuple-element.36.refs_0_, ...), custom_call_target="tpu_custom_call", output_to_operand_aliasing={{0}: (0, {}), {1}: (1, {}), {2}: (2, {})} | custom-call | flops 100000000 | bytes 1048576 | tf_op jit(solution)/shard_map/pallas_call | solution.py:503
  37.0 0.0 collective-permute-done.5.refs_7_
  37.0 0.0 collective-permute-done.6.refs_8_
  37.0 2.3 %shard_map.70 = (f32[7,2,3,272,128]{4,3,2,1,0:T(8,128)S(1)}, f32[7,2,3,272,128]{4,3,2,1,0:T(8,128)S(1)}, f32[5,2,256,128]{3,2,1,0:T(8,128)S(1)}, f32[4,256,256]{2,1,0:T(8,128)}, f32[16,128]{1,0:T(8,128)S(1)}) custom-call(f32[7,2,3,272,128]{4,3,2,1,0:T(8,128)S(1)} %get-tuple-element.44.refs_0_, ...), custom_call_target="tpu_custom_call", output_to_operand_aliasing={{0}: (0, {}), {1}: (1, {}), {2}: (2, {})} | custom-call | flops 100000000 | bytes 1048576 | tf_op jit(solution)/shard_map/pallas_call | solution.py:503
  39.3 19.9 %all_to_all.12 = f32[16,1,128]{2,1,0:T(1,128)S(1)} all-to-all(f32[16,1,128]{2,1,0:T(1,128)S(1)} %bitcast.5), channel_id=1, replica_groups=mesh['groups'=2,'gz'=16] {'gz'}, dimensions={0} | all-to-all | bytes 16384 | tf_op jit(solution)/shard_map/all_to_all | solution.py:577
  59.2 0.6 slice_reduce_fusion
Async XLA Ops:
  1.9 2.6 %collective-permute-start = (s32[2,256,256]{2,1,0:T(8,128)S(1)}, s32[2,256,256]{2,1,0:T(8,128)S(1)}, u32[]{:S(2)}, u32[]{:S(2)}) collective-permute-start(s32[2,256,256]{2,1,0:T(8,128)S(1)} %get-tuple-element.53.refs_2_), channel_id=1, source_target_pairs={{0,1},{1,0},{2,3},{3,2},{4,5},{5,4},{6,7},{7,6},{8,9},{9,8},{10,11... | collective-permute-start | bytes 1572872 | tf_op jit(solution)/shard_map/ppermute | solution.py:521
  3.8 2.0 %collective-permute-start.1 = (f32[2,256,256]{2,1,0:T(8,128)S(1)}, f32[2,256,256]{2,1,0:T(8,128)S(1)}, u32[]{:S(2)}, u32[]{:S(2)}) collective-permute-start(f32[2,256,256]{2,1,0:T(8,128)S(1)} %get-tuple-element.51.refs_3_), channel_id=1, source_target_pairs={{0,1},{1,0},{2,3},{3,2},{4,5},{5,4},{6,7},{7,6},{8,9},{9,8},{10,11... | collective-permute-start | bytes 1572872 | tf_op jit(solution)/shard_map/ppermute | solution.py:521
  3.9 18.6 %collective-permute-start.3 = (s32[2,256,256]{2,1,0:T(8,128)S(1)}, s32[2,256,256]{2,1,0:T(8,128)S(1)}, u32[]{:S(2)}, u32[]{:S(2)}) collective-permute-start(s32[2,256,256]{2,1,0:T(8,128)S(1)} %get-tuple-element.54.refs_0_.refs_8_), channel_id=1, source_target_pairs={{1,2},{3,4},{5,6},{7,8},{9,10},{11,12},{13,14},{2,1},{4,3},{6,5},{... | collective-permute-start | bytes 1572872 | tf_op jit(solution)/shard_map/ppermute | solution.py:521
  5.7 0.7 %copy-start = (f32[8,7]{1,0:T(8,128)S(1)}, f32[8,7]{1,0:T(8,128)}, u32[]{:S(2)}) copy-start(f32[8,7]{1,0:T(8,128)} %refs_6_.1) | copy-start | bytes 676
  6.4 0.7 %copy-start.1 = (f32[2]{0:T(128)S(1)}, f32[2]{0:T(128)}, u32[]{:S(2)}) copy-start(f32[2]{0:T(128)} %refs_7_.1) | copy-start | bytes 28
  17.9 4.6 %collective-permute-start.2 = (f32[1,256,256]{2,1,0:T(8,128)S(1)}, f32[1,256,256]{2,1,0:T(8,128)S(1)}, u32[]{:S(2)}, u32[]{:S(2)}) collective-permute-start(f32[1,256,256]{2,1,0:T(8,128)S(1)} %get-tuple-element.35), channel_id=1, source_target_pairs={{0,1},{1,0},{2,3},{3,2},{4,5},{5,4},{6,7},{7,6},{8,9},{9,8},{10,11... | collective-permute-start | bytes 786440 | tf_op jit(solution)/shard_map/ppermute | solution.py:521
  21.1 10.2 %collective-permute-start.4 = (f32[2,256,256]{2,1,0:T(8,128)S(1)}, f32[2,256,256]{2,1,0:T(8,128)S(1)}, u32[]{:S(2)}, u32[]{:S(2)}) collective-permute-start(f32[2,256,256]{2,1,0:T(8,128)S(1)} %get-tuple-element.52.refs_1_), channel_id=1, source_target_pairs={{1,2},{3,4},{5,6},{7,8},{9,10},{11,12},{13,14},{2,1},{4,3},{6,5},{... | collective-permute-start | bytes 1572872 | tf_op jit(solution)/shard_map/ppermute | solution.py:521
  21.8 15.2 %collective-permute-start.5 = (f32[1,256,256]{2,1,0:T(8,128)S(1)}, f32[1,256,256]{2,1,0:T(8,128)S(1)}, u32[]{:S(2)}, u32[]{:S(2)}) collective-permute-start(f32[1,256,256]{2,1,0:T(8,128)S(1)} %get-tuple-element.47), channel_id=1, source_target_pairs={{1,2},{3,4},{5,6},{7,8},{9,10},{11,12},{13,14},{2,1},{4,3},{6,5},{... | collective-permute-start | bytes 786440 | tf_op jit(solution)/shard_map/ppermute | solution.py:521
  26.9 10.0 %collective-permute-start.6 = (f32[1,256,256]{2,1,0:T(8,128)S(1)}, f32[1,256,256]{2,1,0:T(8,128)S(1)}, u32[]{:S(2)}, u32[]{:S(2)}) collective-permute-start(f32[1,256,256]{2,1,0:T(8,128)S(1)} %get-tuple-element.48), channel_id=1, source_target_pairs={{0,1},{1,0},{2,3},{3,2},{4,5},{5,4},{6,7},{7,6},{8,9},{9,8},{10,11... | collective-permute-start | bytes 786440 | tf_op jit(solution)/shard_map/ppermute | solution.py:521

commit v5 on v4

--- a/solution.py
+++ b/solution.py
@@ -15,8 +15,8 @@
 RIM = 16
 RIM_BELOW = 24
 HALO = 2
-OPERATOR_UNROLL = 8
-LIMITS = (8, 8, 5, 5)
+OPERATOR_UNROLL = 16
+LIMITS = (9, 9, 6, 6)
 
 steps = (
     (1, 0, 0),
@@ -61,7 +61,7 @@
 
 def each_block(rows, body, carry=0, unroll=None):
     count = rows // SUB
-    unroll = min(unroll or 16, count)
+    unroll = min(unroll or 32, count)
 
     def step(k, carry):
         return body(pl.multiple_of(k * SUB, SUB), carry)
@@ -361,7 +361,7 @@
             half.link(q % 2, None, inplane_ref, q + 1)
 
     solve = Solve(device, (first_ref, second_ref, cross_ref, inplane_ref, reaction_ref, rest_ref), factors)
-    solve.advance(0, range(1, depth), range(1, depth), copies={1: near_ref, depth - 1: far_ref})
+    solve.advance(0, range(depth), range(1, depth), parts={0: (0, 1)}, copies={1: near_ref, depth - 1: far_ref})
 
 
 def middle_kernel(*refs):
@@ -376,7 +376,15 @@
     def keep(q, c, row, value):
         put_tile(sum_ref, q - HALO, c, row, value)
 
-    solve.advance(1, range(HALO, depth), range(HALO, depth), copies={depth - 1: far_ref}, keep=keep)
+    solve.advance(
+        1,
+        range(1, depth),
+        range(HALO, depth),
+        parts={1: (0, 1)},
+        copies={depth - 1: far_ref},
+        keep=keep,
+    )
+    solve.advance(2, range(HALO, depth), parts={HALO: (0, 1), depth - 1: (-1, 0)})
 
     def labels(ref, index):
         return lambda c, row: tile(ref, index, c, row)
@@ -415,11 +423,11 @@
     for q in (-1, -2):
         index = device.halo(q)
         solve.receive(first_ref, q, lambda c, row: tile(near_right_ref, index, c, row) * inverse)
-    solve.advance(0, [-1, 0], [-1, 0])
-    solve.advance(1, [-1, 0, 1], [0, 1], parts={-1: (0, 1)}, keep=keep)
+    solve.advance(0, [-1, 0], [-1, 0], parts={0: (-1,)})
+    solve.advance(1, [-1, 0, 1], [0, 1], parts={-1: (0, 1), 1: (-1,)}, keep=keep)
     for copy in copies[:HALO]:
         copy.start()
-    solve.advance(2, range(depth), parts={0: (0, 1), depth - 1: (-1, 0)})
+    solve.advance(2, range(HALO + 1), parts={0: (0, 1), HALO: (-1,)})
     for copy in copies:
         copy.wait()
 

time: 62 us -> 57.8 us (0.932)
  Pallas kernels: 23.3 us -> 19.7 us
  blocking collectives: 19.9 us -> 19.2 us
    pallas_call x4, Pallas kernels: 23.3 us -> 19.7 us  [call(): pl.pallas_call(kernel, out_shape=out_shape, in_specs=[vmem] * (len(argume...]
    all_to_all x1, blocking collectives: 19.9 us -> 19.2 us  [per_device(): gathered = lax.all_to_all(squares, 'gz', 0, 0, tiled=True)]
  transfers between devices with their start and end apart: 7 -> 7, of which waited for: 1 -> 1; matrix products, arithmetic and copies ran while one was open for 2% -> 2% of each run, Pallas kernels for 34% -> 31%
where the time goes in v5:
time: 57.8 us; the launch traced here: 57.5 us
  Pallas kernels  19.7 us (34%)
  blocking collectives  19.2 us (33%)
  starting transfers between devices  10.4 us (18%)
  local copies, waits for them, and re-layouts  3.89 us (7%)
  between operations  2.58 us (4%)
  waiting for transfers between devices  1.2 us (2%)
  other arithmetic  0.6 us (1%)
    pallas_call x4, Pallas kernels, call(): pl.pallas_call(kernel, out_shape=out_shape, in_specs=[vmem] * (len(argume...  19.7 us
    all_to_all x1, blocking collectives, per_device(): gathered = lax.all_to_all(squares, 'gz', 0, 0, tiled=True)  19.2 us
    ppermute x7, starting transfers between devices, send(): return lax.ppermute(array, 'gz', pairs)  10.4 us
    dynamic_slice x2, local copies, waits for them, and re-layouts, ends(): lax.dynamic_slice_in_dim(array, start, HALO, 0)  2.55 us
    unnamed x4, local copies, waits for them, and re-layouts  1.34 us
    ppermute x7, waiting for transfers between devices, send(): return lax.ppermute(array, 'gz', pairs)  1.2 us
  transfers between devices with their start and end apart: 7, of which 1 were waited for; matrix products, arithmetic and copies ran while one was open for 2% of the time, Pallas kernels for 31%

profile of v5, /device:TPU:0, one launch (start us, length us, event | category | flops | bytes accessed | tf_op | source)
XLA Modules:
  0.0 57.5 jit_solution(9319478547795420639)
XLA Ops:
  0.7 1.3 %constant_dynamic-slice_fusion.1 = (s32[2,256,256]{2,1,0:T(8,128)S(1)}, s32[2,256,256]{2,1,0:T(8,128)S(1)}) fusion(s32[4,256,256]{2,1,0:T(8,128)} %param.4, s32[]{:T(128)S(6)} %select_n.17, s32[]{:T(128)S(6)} %select_n.16), kind=kLoop, calls=%fused_computation.2 | loop fusion | bytes 2097160 | tf_op jit(solution)/shard_map/dynamic_slice | solution.py:532
  1.9 0.6 collective-permute-start
  2.5 1.3 %constant_dynamic-slice_fusion = (f32[2,256,256]{2,1,0:T(8,128)S(1)}, f32[2,256,256]{2,1,0:T(8,128)S(1)}) fusion(f32[4,256,256]{2,1,0:T(8,128)} %param.7, s32[]{:T(128)S(6)} %select_n.17, s32[]{:T(128)S(6)} %select_n.16), kind=kLoop, calls=%fused_computation.1 | loop fusion | bytes 2097160 | tf_op jit(solution)/shard_map/dynamic_slice | solution.py:532
  3.8 0.1 collective-permute-start.1
  3.9 0.7 %collective-permute-start.3 = (s32[2,256,256]{2,1,0:T(8,128)S(1)}, s32[2,256,256]{2,1,0:T(8,128)S(1)}, u32[]{:S(2)}, u32[]{:S(2)}) collective-permute-start(s32[2,256,256]{2,1,0:T(8,128)S(1)} %get-tuple-element.54.refs_0_.refs_8_), channel_id=1, source_target_pairs={{1,2},{3,4},{5,6},{7,8},{9,10},{11,12},{13,14},{2,1},{4,3},{6,5},{... | collective-permute-start | bytes 1572872 | tf_op jit(solution)/shard_map/ppermute | solution.py:529
  4.6 0.0 collective-permute-done.refs_4_
  4.6 1.2 %collective-permute-done.1.refs_5_ = f32[2,256,256]{2,1,0:T(8,128)S(1)} collective-permute-done((f32[2,256,256]{2,1,0:T(8,128)S(1)}, f32[2,256,256]{2,1,0:T(8,128)S(1)}, u32[]{:S(2)}, u32[]{:S(2)}) %collective-permute-start.1) | collective-permute-done | bytes 524320 | tf_op jit(solution)/shard_map/ppermute | solution.py:529
  5.7 0.0 copy-start
  5.8 0.7 %copy-done = f32[8,7]{1,0:T(8,128)S(1)} copy-done((f32[8,7]{1,0:T(8,128)S(1)}, f32[8,7]{1,0:T(8,128)}, u32[]{:S(2)}) %copy-start) | copy-done | bytes 248
  6.4 0.0 copy-start.1
  6.4 0.7 %copy-done.1 = f32[2]{0:T(128)S(1)} copy-done((f32[2]{0:T(128)S(1)}, f32[2]{0:T(128)}, u32[]{:S(2)}) %copy-start.1) | copy-done | bytes 32
  7.1 9.0 %shard_map.67 = (f32[8,7,8,128]{3,2,1,0:T(8,128)S(1)}, f32[7,8,128]{2,1,0:T(8,128)S(1)}, f32[7,2,3,272,128]{4,3,2,1,0:T(8,128)S(1)}, f32[6,2,7,272,128]{4,3,2,1,...) custom-call(s32[2,256,256]{2,1,0:T(8,128)S(1)} %get-tuple-element.54, ...), custom_call_target="tpu_custom_call" | custom-call | flops 100000000 | bytes 1048576 | tf_op jit(solution)/shard_map/pallas_call | solution.py:511
  16.1 3.2 %collective-permute-start.2 = (f32[1,256,256]{2,1,0:T(8,128)S(1)}, f32[1,256,256]{2,1,0:T(8,128)S(1)}, u32[]{:S(2)}, u32[]{:S(2)}) collective-permute-start(f32[1,256,256]{2,1,0:T(8,128)S(1)} %get-tuple-element.35), channel_id=1, source_target_pairs={{0,1},{1,0},{2,3},{3,2},{4,5},{5,4},{6,7},{7,6},{8,9},{9,8},{10,11... | collective-permute-start | bytes 786440 | tf_op jit(solution)/shard_map/ppermute | solution.py:529
  19.3 0.7 %collective-permute-start.4 = (f32[2,256,256]{2,1,0:T(8,128)S(1)}, f32[2,256,256]{2,1,0:T(8,128)S(1)}, u32[]{:S(2)}, u32[]{:S(2)}) collective-permute-start(f32[2,256,256]{2,1,0:T(8,128)S(1)} %get-tuple-element.52.refs_1_), channel_id=1, source_target_pairs={{1,2},{3,4},{5,6},{7,8},{9,10},{11,12},{13,14},{2,1},{4,3},{6,5},{... | collective-permute-start | bytes 1572872 | tf_op jit(solution)/shard_map/ppermute | solution.py:529
  20.0 0.9 %collective-permute-start.5 = (f32[1,256,256]{2,1,0:T(8,128)S(1)}, f32[1,256,256]{2,1,0:T(8,128)S(1)}, u32[]{:S(2)}, u32[]{:S(2)}) collective-permute-start(f32[1,256,256]{2,1,0:T(8,128)S(1)} %get-tuple-element.47), channel_id=1, source_target_pairs={{1,2},{3,4},{5,6},{7,8},{9,10},{11,12},{13,14},{2,1},{4,3},{6,5},{... | collective-permute-start | bytes 786440 | tf_op jit(solution)/shard_map/ppermute | solution.py:529
  20.9 0.0 collective-permute-done.3.refs_10_
  20.9 0.0 collective-permute-done.2.refs_9_
  20.9 5.0 %shard_map.68 = (f32[7,2,3,272,128]{4,3,2,1,0:T(8,128)S(1)}, f32[6,2,7,272,128]{4,3,2,1,0:T(8,128)S(1)}, f32[5,2,7,272,128]{4,3,2,1,0:T(8,128)S(1)}, f32[5,2,256...) custom-call(f32[7,2,3,272,128]{4,3,2,1,0:T(8,128)S(1)} %get-tuple-el, ...), custom_call_target="tpu_custom_call", output_to_operand_aliasing={{0}: (0, {}), {1}: (1, {}), {2}: (2, {}), {3}: (3, {}), {4}... | custom-call | flops 100000000 | bytes 1048576 | tf_op jit(solution)/shard_map/pallas_call | solution.py:511
  25.9 4.3 %collective-permute-start.6 = (f32[1,256,256]{2,1,0:T(8,128)S(1)}, f32[1,256,256]{2,1,0:T(8,128)S(1)}, u32[]{:S(2)}, u32[]{:S(2)}) collective-permute-start(f32[1,256,256]{2,1,0:T(8,128)S(1)} %get-tuple-element.48), channel_id=1, source_target_pairs={{0,1},{1,0},{2,3},{3,2},{4,5},{5,4},{6,7},{7,6},{8,9},{9,8},{10,11... | collective-permute-start | bytes 786440 | tf_op jit(solution)/shard_map/ppermute | solution.py:529
  30.2 0.0 collective-permute-done.4.refs_7_
  30.2 3.7 %shard_map.69 = (f32[7,2,3,272,128]{4,3,2,1,0:T(8,128)S(1)}, f32[7,2,3,272,128]{4,3,2,1,0:T(8,128)S(1)}, f32[5,2,256,128]{3,2,1,0:T(8,128)S(1)}, f32[4,256,256]{2,1,0:T(8,128)}) custom-call(f32[7,2,3,272,128]{4,3,2,1,0:T(8,128)S(1)} %get-tuple-element.36.refs_0_, ...), custom_call_target="tpu_custom_call", output_to_operand_aliasing={{0}: (0, {}), {1}: (1, {}), {2}: (2, {})} | custom-call | flops 100000000 | bytes 1048576 | tf_op jit(solution)/shard_map/pallas_call | solution.py:511
  33.9 0.0 collective-permute-done.5.refs_7_
  33.9 0.0 collective-permute-done.6.refs_8_
  34.0 2.0 %shard_map.70 = (f32[7,2,3,272,128]{4,3,2,1,0:T(8,128)S(1)}, f32[7,2,3,272,128]{4,3,2,1,0:T(8,128)S(1)}, f32[5,2,256,128]{3,2,1,0:T(8,128)S(1)}, f32[4,256,256]{2,1,0:T(8,128)}, f32[16,128]{1,0:T(8,128)S(1)}) custom-call(f32[7,2,3,272,128]{4,3,2,1,0:T(8,128)S(1)} %get-tuple-element.44.refs_0_, ...), custom_call_target="tpu_custom_call", output_to_operand_aliasing={{0}: (0, {}), {1}: (1, {}), {2}: (2, {})} | custom-call | flops 100000000 | bytes 1048576 | tf_op jit(solution)/shard_map/pallas_call | solution.py:511
  35.9 19.2 %all_to_all.12 = f32[16,1,128]{2,1,0:T(1,128)S(1)} all-to-all(f32[16,1,128]{2,1,0:T(1,128)S(1)} %bitcast.5), channel_id=1, replica_groups=mesh['groups'=2,'gz'=16] {'gz'}, dimensions={0} | all-to-all | bytes 16384 | tf_op jit(solution)/shard_map/all_to_all | solution.py:585
  55.1 0.6 %slice_reduce_fusion = f32[]{:T(128)} fusion(f32[16,128]{1,0:T(8,128)S(1)} %bitcast.6), kind=kLoop, calls=%fused_computation | loop fusion | flops 15 | bytes 68 | tf_op jit(solution)/shard_map/reduce_sum | solution.py:586
Async XLA Ops:
  1.9 2.6 %collective-permute-start = (s32[2,256,256]{2,1,0:T(8,128)S(1)}, s32[2,256,256]{2,1,0:T(8,128)S(1)}, u32[]{:S(2)}, u32[]{:S(2)}) collective-permute-start(s32[2,256,256]{2,1,0:T(8,128)S(1)} %get-tuple-element.53.refs_2_), channel_id=1, source_target_pairs={{0,1},{1,0},{2,3},{3,2},{4,5},{5,4},{6,7},{7,6},{8,9},{9,8},{10,11... | collective-permute-start | bytes 1572872 | tf_op jit(solution)/shard_map/ppermute | solution.py:529
  3.8 2.0 %collective-permute-start.1 = (f32[2,256,256]{2,1,0:T(8,128)S(1)}, f32[2,256,256]{2,1,0:T(8,128)S(1)}, u32[]{:S(2)}, u32[]{:S(2)}) collective-permute-start(f32[2,256,256]{2,1,0:T(8,128)S(1)} %get-tuple-element.51.refs_3_), channel_id=1, source_target_pairs={{0,1},{1,0},{2,3},{3,2},{4,5},{5,4},{6,7},{7,6},{8,9},{9,8},{10,11... | collective-permute-start | bytes 1572872 | tf_op jit(solution)/shard_map/ppermute | solution.py:529
  3.9 17.0 %collective-permute-start.3 = (s32[2,256,256]{2,1,0:T(8,128)S(1)}, s32[2,256,256]{2,1,0:T(8,128)S(1)}, u32[]{:S(2)}, u32[]{:S(2)}) collective-permute-start(s32[2,256,256]{2,1,0:T(8,128)S(1)} %get-tuple-element.54.refs_0_.refs_8_), channel_id=1, source_target_pairs={{1,2},{3,4},{5,6},{7,8},{9,10},{11,12},{13,14},{2,1},{4,3},{6,5},{... | collective-permute-start | bytes 1572872 | tf_op jit(solution)/shard_map/ppermute | solution.py:529
  5.7 0.7 %copy-start = (f32[8,7]{1,0:T(8,128)S(1)}, f32[8,7]{1,0:T(8,128)}, u32[]{:S(2)}) copy-start(f32[8,7]{1,0:T(8,128)} %refs_6_.1) | copy-start | bytes 676
  6.4 0.7 %copy-start.1 = (f32[2]{0:T(128)S(1)}, f32[2]{0:T(128)}, u32[]{:S(2)}) copy-start(f32[2]{0:T(128)} %refs_7_.1) | copy-start | bytes 28
  16.1 4.8 %collective-permute-start.2 = (f32[1,256,256]{2,1,0:T(8,128)S(1)}, f32[1,256,256]{2,1,0:T(8,128)S(1)}, u32[]{:S(2)}, u32[]{:S(2)}) collective-permute-start(f32[1,256,256]{2,1,0:T(8,128)S(1)} %get-tuple-element.35), channel_id=1, source_target_pairs={{0,1},{1,0},{2,3},{3,2},{4,5},{5,4},{6,7},{7,6},{8,9},{9,8},{10,11... | collective-permute-start | bytes 786440 | tf_op jit(solution)/shard_map/ppermute | solution.py:529
  19.3 10.9 %collective-permute-start.4 = (f32[2,256,256]{2,1,0:T(8,128)S(1)}, f32[2,256,256]{2,1,0:T(8,128)S(1)}, u32[]{:S(2)}, u32[]{:S(2)}) collective-permute-start(f32[2,256,256]{2,1,0:T(8,128)S(1)} %get-tuple-element.52.refs_1_), channel_id=1, source_target_pairs={{1,2},{3,4},{5,6},{7,8},{9,10},{11,12},{13,14},{2,1},{4,3},{6,5},{... | collective-permute-start | bytes 1572872 | tf_op jit(solution)/shard_map/ppermute | solution.py:529
  20.0 14.0 %collective-permute-start.5 = (f32[1,256,256]{2,1,0:T(8,128)S(1)}, f32[1,256,256]{2,1,0:T(8,128)S(1)}, u32[]{:S(2)}, u32[]{:S(2)}) collective-permute-start(f32[1,256,256]{2,1,0:T(8,128)S(1)} %get-tuple-element.47), channel_id=1, source_target_pairs={{1,2},{3,4},{5,6},{7,8},{9,10},{11,12},{13,14},{2,1},{4,3},{6,5},{... | collective-permute-start | bytes 786440 | tf_op jit(solution)/shard_map/ppermute | solution.py:529
  25.9 8.1 %collective-permute-start.6 = (f32[1,256,256]{2,1,0:T(8,128)S(1)}, f32[1,256,256]{2,1,0:T(8,128)S(1)}, u32[]{:S(2)}, u32[]{:S(2)}) collective-permute-start(f32[1,256,256]{2,1,0:T(8,128)S(1)} %get-tuple-element.48), channel_id=1, source_target_pairs={{0,1},{1,0},{2,3},{3,2},{4,5},{5,4},{6,7},{7,6},{8,9},{9,8},{10,11... | collective-permute-start | bytes 786440 | tf_op jit(solution)/shard_map/ppermute | solution.py:529

commit v6 on v4

--- a/solution.py
+++ b/solution.py
@@ -15,8 +15,8 @@
 RIM = 16
 RIM_BELOW = 24
 HALO = 2
-OPERATOR_UNROLL = 8
-LIMITS = (8, 8, 5, 5)
+OPERATOR_UNROLL = 16
+LIMITS = (9, 5, 5, 5)
 
 steps = (
     (1, 0, 0),
@@ -61,7 +61,7 @@
 
 def each_block(rows, body, carry=0, unroll=None):
     count = rows // SUB
-    unroll = min(unroll or 16, count)
+    unroll = min(unroll or 32, count)
 
     def step(k, carry):
         return body(pl.multiple_of(k * SUB, SUB), carry)
@@ -99,6 +99,10 @@
 
 def tile(ref, plane, c, row):
     return ref[plane, pl.ds(row, SUB), pl.ds(c * LANES, LANES)]
+
+
+def label_of(ref):
+    return lambda c, row: tile(ref, 0, c, row).astype(jnp.int32)
 
 
 def put_tile(ref, plane, c, row, value):
@@ -135,14 +139,14 @@
 
 
 class Half:
-    def __init__(self, tables_ref, refs, tiles, rows):
+    def __init__(self, tables_ref, refs, tiles, rows, clean=True):
         self.refs, self.tiles, self.rows = refs, tiles, rows
         self.tables = [
             ([tables_ref[phase, k] for k in range(3)], [tables_ref[phase, k] for k in range(3, 7)])
             for phase in range(PHASES)
         ]
         for ref, slots_of in zip(refs, (cross_slots, inplane_slots)):
-            for slot in range(ref.shape[0]):
+            for slot in range(ref.shape[0] if clean else 0):
                 for k in range(len(slots_of)):
                     for c in range(tiles):
                         for start in (0, SUB, rows + RIM, rows + RIM + SUB):
@@ -261,15 +265,6 @@
     def own(self, q):
         return jnp.where(self.flip == 1, self.depth - 1 - q, q)
 
-    def sent(self, q):
-        return jnp.where(self.flip == 1, 1 - q % HALO, q % HALO)
-
-    def halo(self, q):
-        far = q >= self.depth
-        first = (q == self.depth) if far else (q == -1)
-        turned = self.flip == (1 if far else 0)
-        return jnp.where(turned, 1, 0) if first else jnp.where(turned, 0, 1)
-
 
 class Solve:
     def __init__(self, device, refs, factors, right=None):
@@ -321,31 +316,22 @@
 
 
 def start_kernel(*refs):
-    near_labels_ref, near_right_ref, far_labels_ref, far_right_ref, beside_labels_ref, beside_right_ref = refs[:6]
-    table_ref, bounds_ref, tables_ref, factors_ref = refs[6:10]
-    first_ref, cross_ref, inplane_ref, reaction_ref, rest_ref, second_ref, near_ref, far_ref = refs[10:18]
-    halves = refs[18:]
-    device = Device((2 * HALO,) + near_labels_ref.shape[1:])
+    *pairs, table_ref, bounds_ref, tables_ref, factors_ref = refs[:9]
+    first_ref, cross_ref, inplane_ref, reaction_ref, rest_ref, second_ref, near_ref, far_ref = refs[9:17]
+    halves = refs[17:]
+    device = Device((len(pairs) - 1,) + pairs[0].shape[1:])
     depth, rows, tiles = device.depth, device.rows, device.tiles
     put_factors(factors_ref, bounds_ref)
     inverse, factors = get_factors(factors_ref)
     put_tables(tables_ref, table_ref, device.flip)
     half = Half(tables_ref, halves, tiles, rows)
 
-    def read(q, near, far, beside):
-        if q == depth:
-            ref, index = beside, device.halo(q)
-        else:
-            ref, index = near if q < HALO else far, device.sent(q)
-        return lambda c, row: tile(ref, index, c, row)
-
-    for q in range(depth + 1):
+    for q, pair_ref in enumerate(pairs):
         field_rims(first_ref, q + HALO, tiles, rows)
         field_rims(second_ref, q + HALO, tiles, rows)
-        right = read(q, near_right_ref, far_right_ref, beside_right_ref)
 
         def body(row, carry):
-            values = [right(c, row) for c in range(tiles)]
+            values = [tile(pair_ref, 1, c, row) for c in range(tiles)]
             if q < depth:
                 for c, value in enumerate(values):
                     rest_ref[q + 1, c, pl.ds(row, SUB), :] = value
@@ -353,73 +339,69 @@
             return carry
 
         each_block(rows, body)
-        labels = read(q, near_labels_ref, far_labels_ref, beside_labels_ref)
-        half.fill(q % 2, labels, None, (reaction_ref, q + 1) if q < depth else None)
+        half.fill(q % 2, label_of(pair_ref), None, (reaction_ref, q + 1) if q < depth else None)
         if q:
             half.link((q - 1) % 2, q % 2, cross_ref, q - 1 + HALO)
         if q < depth:
             half.link(q % 2, None, inplane_ref, q + 1)
 
     solve = Solve(device, (first_ref, second_ref, cross_ref, inplane_ref, reaction_ref, rest_ref), factors)
-    solve.advance(0, range(1, depth), range(1, depth), copies={1: near_ref, depth - 1: far_ref})
+    solve.advance(0, range(depth), range(1, depth), parts={0: (0, 1)}, copies={1: near_ref, depth - 1: far_ref})
 
 
 def middle_kernel(*refs):
-    tables_ref, factors_ref, sent_labels_ref, far_second_ref, near_labels_ref = refs[6:11]
+    tables_ref, factors_ref, own_ref, far_second_ref, near_ref = refs[6:11]
     first_ref, cross_ref, inplane_ref, reaction_ref, rest_ref, second_ref, far_ref, sum_ref, *halves = refs[11:]
-    device = Device((2 * HALO,) + near_labels_ref.shape[1:])
-    depth = device.depth
-    _, factors = get_factors(factors_ref)
-    solve = Solve(device, (first_ref, second_ref, cross_ref, inplane_ref, reaction_ref, rest_ref), factors)
-    solve.receive(second_ref, depth, lambda c, row: tile(far_second_ref, 0, c, row))
-
-    def keep(q, c, row, value):
-        put_tile(sum_ref, q - HALO, c, row, value)
-
-    solve.advance(1, range(HALO, depth), range(HALO, depth), copies={depth - 1: far_ref}, keep=keep)
-
-    def labels(ref, index):
-        return lambda c, row: tile(ref, index, c, row)
-
+    depth = rest_ref.shape[0] - 1
+    device = Device((depth,) + near_ref.shape[1:])
+    inverse, factors = get_factors(factors_ref)
     half = Half(tables_ref, halves, device.tiles, device.rows)
-    half.fill(0, labels(sent_labels_ref, device.sent(0)))
-    half.fill(1, labels(near_labels_ref, device.halo(-1)), device.joined, (reaction_ref, 0))
+    half.fill(0, label_of(own_ref))
+    half.fill(1, label_of(near_ref), device.joined, (reaction_ref, 0))
     half.link(1, None, inplane_ref, 0)
     half.link(1, 0, cross_ref, HALO - 1)
-    half.fill(0, labels(near_labels_ref, device.halo(-2)), device.joined)
-    half.link(0, 1, cross_ref, HALO - 2)
+
+    def right(q, c, row):
+        return tile(near_ref, 1, c, row)
+
+    def keep(q, c, row, value):
+        put_tile(sum_ref, q - 1, c, row, value)
+
+    solve = Solve(device, (first_ref, second_ref, cross_ref, inplane_ref, reaction_ref, rest_ref), factors, right)
+    solve.receive(first_ref, -1, lambda c, row: tile(near_ref, 1, c, row) * inverse)
+    solve.advance(0, [-1, 0], [0], parts={-1: (0, 1), 0: (-1,)})
+    solve.receive(second_ref, depth, lambda c, row: tile(far_second_ref, 0, c, row))
+    solve.advance(1, range(depth), range(1, depth), parts={0: (0, 1)}, copies={depth - 1: far_ref}, keep=keep)
+    solve.advance(2, range(1, depth), parts={1: (0, 1), depth - 1: (-1, 0)})
 
 
 def late_kernel(*refs):
-    *links, factors_ref, near_right_ref, sum_ref = refs[3:9]
-    first_ref, second_ref, rest_ref, solution_ref, ready_ref, sems = refs[9:]
+    inplane_ref, reaction_ref, factors_ref, tables_ref, near_ref, sum_ref = refs[5:11]
+    first_ref, second_ref, rest_ref, cross_ref, half_ref, solution_ref, ready_ref, sems = refs[11:]
     device = Device(solution_ref.shape)
     depth = device.depth
     inverse, factors = get_factors(factors_ref)
     copies = [
         pltpu.make_async_copy(
-            ready_ref.at[q] if q < HALO else sum_ref.at[q - HALO], solution_ref.at[device.own(q)], sems.at[q]
+            sum_ref.at[q - 1] if q else ready_ref.at[0], solution_ref.at[device.own(q)], sems.at[q]
         )
         for q in range(depth)
     ]
-    for copy in copies[HALO:]:
+    for copy in copies[1:]:
         copy.start()
-
-    def right(q, c, row):
-        return tile(near_right_ref, device.halo(q), c, row)
+    half = Half(tables_ref, (half_ref,), device.tiles, device.rows, clean=False)
+    half.fill(0, label_of(near_ref), device.joined)
+    half.link(0, 1, cross_ref, HALO - 2)
 
     def keep(q, c, row, value):
         put_tile(ready_ref, q, c, row, value)
 
-    solve = Solve(device, (first_ref, second_ref, *links, rest_ref), factors, right)
-    for q in (-1, -2):
-        index = device.halo(q)
-        solve.receive(first_ref, q, lambda c, row: tile(near_right_ref, index, c, row) * inverse)
-    solve.advance(0, [-1, 0], [-1, 0])
-    solve.advance(1, [-1, 0, 1], [0, 1], parts={-1: (0, 1)}, keep=keep)
-    for copy in copies[:HALO]:
-        copy.start()
-    solve.advance(2, range(depth), parts={0: (0, 1), depth - 1: (-1, 0)})
+    solve = Solve(device, (first_ref, second_ref, cross_ref, inplane_ref, reaction_ref, rest_ref), factors)
+    solve.receive(first_ref, -2, lambda c, row: tile(near_ref, 1, c, row) * inverse)
+    solve.advance(0, [-1], [-1], parts={-1: (-1,)})
+    solve.advance(1, [-1, 0], [0], parts={-1: (0, 1), 0: (-1,)}, keep=keep)
+    copies[0].start()
+    solve.advance(2, [0, 1], parts={0: (0, 1), 1: (-1,)})
     for copy in copies:
         copy.wait()
 
@@ -490,7 +472,7 @@
     cross_links = array(depth + HALO, tiles, len(cross_slots), below, LANES)
     inplane_links = array(depth + 1, tiles, len(inplane_slots), below, LANES)
     reaction = rest = array(depth + 1, tiles, rows, LANES)
-    inner = array(depth - HALO, rows, columns)
+    inner = array(depth - 1, rows, columns)
     plane = array(1, rows, columns)
     block = array(depth, rows, columns)
     tables, factors = array(PHASES, 7, SUB, LANES), array(1 + 2 * ITERS, SUB, LANES)
@@ -514,24 +496,25 @@
     inside = [(i, i ^ 1) for i in range(count)]
     across = [(i, i + 1) for i in range(1, count - 1, 2)]
     across += [(j, i) for i, j in across]
-    near_start = odd * (depth - HALO)
-    far_start = (1 - odd) * (depth - HALO)
 
     def send(array, pairs):
         return lax.ppermute(array, "gz", pairs)
 
-    def ends(array):
-        return [lax.dynamic_slice_in_dim(array, start, HALO, 0) for start in (near_start, far_start)]
-
-    my_labels, my_right = ends(labels), ends(right_side)
-    near_labels = send(my_labels[0], across)
-    near_right = send(my_right[0], across)
-    far_labels = send(my_labels[1], inside)
-    far_right = send(my_right[1], inside)
+    def pair(q, labels, right_side):
+        index = jnp.where(odd == 1, depth - 1 - q, q)
+        own_labels = lax.dynamic_slice_in_dim(labels, index, 1, 0).astype(jnp.float32)
+        return jnp.concatenate([own_labels, lax.dynamic_slice_in_dim(right_side, index, 1, 0)], 0)
+
+    mine = [pair(0, labels, right_side)]
+    mine[0], *later = lax.optimization_barrier((mine[0], labels, right_side))
+    mine += [pair(q, *later) for q in range(1, depth)]
+    near_first = send(mine[0], across)
+    far_first = send(mine[-1], inside)
+    near_next = send(mine[1], across)
 
     tables, factors, *state, near, far = call(
         start_kernel,
-        (my_labels[0], my_right[0], my_labels[1], my_right[1], far_labels, far_right, tensor_table, bounds),
+        (*mine, far_first, tensor_table, bounds),
         (tables, factors, field, cross_links, inplane_links, reaction, rest, field, plane, plane),
         0,
         LIMITS[0],
@@ -542,28 +525,28 @@
     far_second = send(far, inside)
     near_second = send(near, across)
 
-    *state, far, summed = call(
+    *state, far, summed, half = call(
         middle_kernel,
-        (*state, tables, factors, my_labels[0], far_second, near_labels),
-        tuple(array(*s.shape) for s in state) + (plane, inner),
+        (*state, tables, factors, mine[0], far_second, near_first),
+        tuple(array(*s.shape) for s in state) + (plane, inner, array(*halves[0].shape)),
         6,
         LIMITS[1],
         10**8,
-        halves,
+        halves[1:],
     )
     far_third = send(far, inside)
     first, cross_links, inplane_links, reaction, rest, second = state
-    links = (cross_links, inplane_links, reaction, factors)
-    first, second, rest, solved = call(
+    first, second, rest, cross_links, _, solved = call(
         late_kernel,
-        (first, second, rest, *links, near_right, summed),
-        (field, field, array(*rest.shape), block),
-        3,
+        (first, second, rest, cross_links, half, inplane_links, reaction, factors, tables, near_next, summed),
+        (field, field, array(*rest.shape), array(*cross_links.shape), array(*half.shape), block),
+        5,
         LIMITS[2],
         10**8,
-        [pltpu.VMEM((HALO, rows, columns), jnp.float32), pltpu.SemaphoreType.DMA((depth,))],
-        kept=3,
+        [pltpu.VMEM((1, rows, columns), jnp.float32), pltpu.SemaphoreType.DMA((depth,))],
+        kept=5,
     )
+    links = (cross_links, inplane_links, reaction, factors)
     *_, residual, squares = call(
         last_kernel,
         (first, second, rest, *links, near_second, far_third),

time: 62 us -> 56.2 us (0.906)
  blocking collectives: 19.9 us -> 15.4 us
  Pallas kernels: 23.3 us -> 19.5 us
  starting transfers between devices: 10.2 us -> 13 us
  other arithmetic: 0.6 us -> 2.89 us
  local copies, waits for them, and re-layouts: 3.89 us -> 2.15 us
  waiting for transfers between devices: 1.2 us -> 0.36 us
    all_to_all x1, blocking collectives: 19.9 us -> 15.4 us  [per_device(): gathered = lax.all_to_all(squares, 'gz', 0, 0, tiled=True)]
    pallas_call x4, Pallas kernels: 23.3 us -> 19.5 us  [call(): pl.pallas_call(kernel, out_shape=out_shape, in_specs=[vmem] * (len(argume...]
    ppermute x7 -> x6, starting transfers between devices: 10.2 us -> 13 us  [send(): return lax.ppermute(array, 'gz', pairs)]
    convert_element_type x0 -> x2, other arithmetic: none -> 2.14 us  [pair(): lax.dynamic_slice_in_dim(labels, index, 1, 0).astype(jnp.float32)]
    unnamed x4, local copies, waits for them, and re-layouts: 1.34 us -> 0.01 us
    ppermute x7 -> x6, waiting for transfers between devices: 1.2 us -> 0.36 us  [send(): return lax.ppermute(array, 'gz', pairs)]
  transfers between devices with their start and end apart: 7 -> 6, of which waited for: 1 -> 2; matrix products, arithmetic and copies ran while one was open for 2% -> 0% of each run, Pallas kernels for 34% -> 32%
where the time goes in v6:
time: 56.2 us; the launch traced here: 55.9 us
  Pallas kernels  19.5 us (35%)
  blocking collectives  15.4 us (27%)
  starting transfers between devices  13 us (23%)
  other arithmetic  2.89 us (5%)
  between operations  2.61 us (5%)
  local copies, waits for them, and re-layouts  2.15 us (4%)
    pallas_call x4, Pallas kernels, call(): pl.pallas_call(kernel, out_shape=out_shape, in_specs=[vmem] * (len(argume...  19.5 us
    all_to_all x1, blocking collectives, per_device(): gathered = lax.all_to_all(squares, 'gz', 0, 0, tiled=True)  15.4 us
    ppermute x6, starting transfers between devices, send(): return lax.ppermute(array, 'gz', pairs)  13 us
    convert_element_type x2, other arithmetic, pair(): lax.dynamic_slice_in_dim(labels, index, 1, 0).astype(jnp.float32)  2.14 us
    dynamic_slice x2, local copies, waits for them, and re-layouts, pair(): lax.dynamic_slice_in_dim(right_side, index, 1, 0)  2.14 us
  transfers between devices with their start and end apart: 6, of which 2 were waited for; matrix products, arithmetic and copies ran while one was open for 0% of the time, Pallas kernels for 32%

profile of v6, /device:TPU:0, one launch (start us, length us, event | category | flops | bytes accessed | tf_op | source)
XLA Modules:
  0.0 55.9 jit_solution(1078703868278982625)
XLA Ops:
  0.6 0.0 copy-start.1
  0.6 0.0 copy-start
  0.7 1.0 %dynamic-slice_convert_fusion.3 = f32[1,256,256]{2,1,0:T(8,128)S(1)} fusion(s32[4,256,256]{2,1,0:T(8,128)} %param.4, s32[]{:T(128)S(6)} %select_n.29), kind=kLoop, calls=%fused_computation.7 | loop fusion | flops 65536 | bytes 524292 | tf_op jit(solution)/shard_map/convert_element_type | solution.py:505
  1.6 1.0 %constant_dynamic-slice_fusion.3 = f32[1,256,256]{2,1,0:T(8,128)S(1)} fusion(f32[4,256,256]{2,1,0:T(8,128)} %param.7, s32[]{:T(128)S(6)} %select_n.29), kind=kLoop, calls=%fused_computation.12 | loop fusion | bytes 524292 | tf_op jit(solution)/shard_map/dynamic_slice | solution.py:506
  2.7 1.2 %dynamic-slice_convert_fusion = (f32[1,256,256]{2,1,0:T(8,128)S(1)}, f32[1,256,256]{2,1,0:T(8,128)S(1)}, f32[1,256,256]{2,1,0:T(8,128)S(1)}) fusion(s32[4,256,256]{2,1,0:T(8,128)} %param.4, s32[]{:T(128)S(6)} %select_n.32, s32[]{:T(128)S(6)} %select_n.31, s32[]{:T(128)S(6)} %select_n.30), kind=kLoop, calls=%fused_computation.4 | loop fusion | flops 196608 | bytes 1572876 | tf_op jit(solution)/shard_map/convert_element_type | solution.py:505
  3.8 1.2 %constant_dynamic-slice_fusion = (f32[1,256,256]{2,1,0:T(8,128)S(1)}, f32[1,256,256]{2,1,0:T(8,128)S(1)}, f32[1,256,256]{2,1,0:T(8,128)S(1)}) fusion(f32[4,256,256]{2,1,0:T(8,128)} %param.7, s32[]{:T(128)S(6)} %select_n.32, s32[]{:T(128)S(6)} %select_n.31, s32[]{:T(128)S(6)} %select_n.30), kind=kLoop, calls=%fused_computation.9 | loop fusion | bytes 1572876 | tf_op jit(solution)/shard_map/dynamic_slice | solution.py:506
  5.1 0.6 collective-permute-start
  5.6 0.7 %collective-permute-start.2 = (f32[2,256,256]{2,1,0:T(8,128)S(1)}, f32[2,256,256]{2,1,0:T(8,128)S(1)}, u32[]{:S(2)}, u32[]{:S(2)}) collective-permute-start(f32[2,256,256]{2,1,0:T(8,128)S(1)} %pad_maximum_fusion.refs_0_.refs_8_), channel_id=1, source_target_pairs={{1,2},{3,4},{5,6},{7,8},{9,10},{11,12},{13,14},{2,1},{4,3},{6,5},{... | collective-permute-start | bytes 1572872 | tf_op jit(solution)/shard_map/ppermute | solution.py:501
  6.4 0.7 %collective-permute-start.3 = (f32[2,256,256]{2,1,0:T(8,128)S(1)}, f32[2,256,256]{2,1,0:T(8,128)S(1)}, u32[]{:S(2)}, u32[]{:S(2)}) collective-permute-start(f32[2,256,256]{2,1,0:T(8,128)S(1)} %pad_maximum_fusion.1.refs_1_), channel_id=1, source_target_pairs={{1,2},{3,4},{5,6},{7,8},{9,10},{11,12},{13,14},{2,1},{4,3},{6,5},{... | collective-permute-start | bytes 1572872 | tf_op jit(solution)/shard_map/ppermute | solution.py:501
  7.1 0.1 collective-permute-done.refs_4_
  7.2 0.0 copy-done.1
  7.2 0.0 copy-done
  7.2 9.0 %shard_map.67 = (f32[8,7,8,128]{3,2,1,0:T(8,128)S(1)}, f32[7,8,128]{2,1,0:T(8,128)S(1)}, f32[7,2,3,272,128]{4,3,2,1,0:T(8,128)S(1)}, f32[6,2,7,272,128]{4,3,2,1,...) custom-call(f32[2,256,256]{2,1,0:T(8,128)S(1)} %pad_maximum_fusion.r, ...), custom_call_target="tpu_custom_call" | custom-call | flops 100000000 | bytes 1048576 | tf_op jit(solution)/shard_map/pallas_call | solution.py:485
  16.2 5.1 %collective-permute-start.1 = (f32[1,256,256]{2,1,0:T(8,128)S(1)}, f32[1,256,256]{2,1,0:T(8,128)S(1)}, u32[]{:S(2)}, u32[]{:S(2)}) collective-permute-start(f32[1,256,256]{2,1,0:T(8,128)S(1)} %get-tuple-element.43), channel_id=1, source_target_pairs={{0,1},{1,0},{2,3},{3,2},{4,5},{5,4},{6,7},{7,6},{8,9},{9,8},{10,11... | collective-permute-start | bytes 786440 | tf_op jit(solution)/shard_map/ppermute | solution.py:501
  21.3 0.8 %collective-permute-start.4 = (f32[1,256,256]{2,1,0:T(8,128)S(1)}, f32[1,256,256]{2,1,0:T(8,128)S(1)}, u32[]{:S(2)}, u32[]{:S(2)}) collective-permute-start(f32[1,256,256]{2,1,0:T(8,128)S(1)} %get-tuple-element.57), channel_id=1, source_target_pairs={{1,2},{3,4},{5,6},{7,8},{9,10},{11,12},{13,14},{2,1},{4,3},{6,5},{... | collective-permute-start | bytes 786440 | tf_op jit(solution)/shard_map/ppermute | solution.py:501
  22.1 0.0 collective-permute-done.2.refs_10_
  22.2 0.3 collective-permute-done.1.refs_9_
  22.5 6.0 %shard_map.68 = (f32[7,2,3,272,128]{4,3,2,1,0:T(8,128)S(1)}, f32[6,2,7,272,128]{4,3,2,1,0:T(8,128)S(1)}, f32[5,2,7,272,128]{4,3,2,1,0:T(8,128)S(1)}, f32[5,2,256...) custom-call(f32[7,2,3,272,128]{4,3,2,1,0:T(8,128)S(1)} %get-tuple-el, ...), custom_call_target="tpu_custom_call", output_to_operand_aliasing={{0}: (0, {}), {1}: (1, {}), {2}: (2, {}), {3}: (3, {}), {4}... | custom-call | flops 100000000 | bytes 1048576 | tf_op jit(solution)/shard_map/pallas_call | solution.py:485
  28.5 5.1 %collective-permute-start.5 = (f32[1,256,256]{2,1,0:T(8,128)S(1)}, f32[1,256,256]{2,1,0:T(8,128)S(1)}, u32[]{:S(2)}, u32[]{:S(2)}) collective-permute-start(f32[1,256,256]{2,1,0:T(8,128)S(1)} %get-tuple-element.58), channel_id=1, source_target_pairs={{0,1},{1,0},{2,3},{3,2},{4,5},{5,4},{6,7},{7,6},{8,9},{9,8},{10,11... | collective-permute-start | bytes 786440 | tf_op jit(solution)/shard_map/ppermute | solution.py:501
  33.6 0.0 collective-permute-done.3.refs_9_
  33.6 2.6 %shard_map.69 = (f32[7,2,3,272,128]{4,3,2,1,0:T(8,128)S(1)}, f32[7,2,3,272,128]{4,3,2,1,0:T(8,128)S(1)}, f32[5,2,256,128]{3,2,1,0:T(8,128)S(1)}, f32[6,2,7,272,1...) custom-call(f32[7,2,3,272,128]{4,3,2,1,0:T(8,128)S(1)} %get-tuple-el, ...), custom_call_target="tpu_custom_call", output_to_operand_aliasing={{0}: (0, {}), {1}: (1, {}), {2}: (2, {}), {3}: (3, {}), {4}... | custom-call | flops 100000000 | bytes 1048576 | tf_op jit(solution)/shard_map/pallas_call | solution.py:485
  36.2 0.0 collective-permute-done.4.refs_7_
  36.2 0.0 collective-permute-done.5.refs_8_
  36.2 1.9 %shard_map.70 = (f32[7,2,3,272,128]{4,3,2,1,0:T(8,128)S(1)}, f32[7,2,3,272,128]{4,3,2,1,0:T(8,128)S(1)}, f32[5,2,256,128]{3,2,1,0:T(8,128)S(1)}, f32[4,256,256]{2,1,0:T(8,128)}, f32[16,128]{1,0:T(8,128)S(1)}) custom-call(f32[7,2,3,272,128]{4,3,2,1,0:T(8,128)S(1)} %get-tuple-element.53.refs_0_, ...), custom_call_target="tpu_custom_call", output_to_operand_aliasing={{0}: (0, {}), {1}: (1, {}), {2}: (2, {})} | custom-call | flops 100000000 | bytes 1048576 | tf_op jit(solution)/shard_map/pallas_call | solution.py:485
  38.1 15.4 %all_to_all.12 = f32[16,1,128]{2,1,0:T(1,128)S(1)} all-to-all(f32[16,1,128]{2,1,0:T(1,128)S(1)} %bitcast.5), channel_id=1, replica_groups=mesh['groups'=2,'gz'=16] {'gz'}, dimensions={0} | all-to-all | bytes 16384 | tf_op jit(solution)/shard_map/all_to_all | solution.py:560
  53.4 0.6 %slice_reduce_fusion = f32[]{:T(128)} fusion(f32[16,128]{1,0:T(8,128)S(1)} %bitcast.6), kind=kLoop, calls=%fused_computation.8 | loop fusion | flops 15 | bytes 68 | tf_op jit(solution)/shard_map/reduce_sum | solution.py:561
  (4 shorter events, 0.1 us)
Async XLA Ops:
  0.6 6.5 %copy-start.1 = (f32[2]{0:T(128)S(1)}, f32[2]{0:T(128)}, u32[]{:S(2)}) copy-start(f32[2]{0:T(128)} %refs_6_.1) | copy-start | bytes 28
  0.6 6.5 %copy-start = (f32[8,7]{1,0:T(8,128)S(1)}, f32[8,7]{1,0:T(8,128)}, u32[]{:S(2)}) copy-start(f32[8,7]{1,0:T(8,128)} %refs_5_.1) | copy-start | bytes 676
  5.1 2.1 %collective-permute-start = (f32[2,256,256]{2,1,0:T(8,128)S(1)}, f32[2,256,256]{2,1,0:T(8,128)S(1)}, u32[]{:S(2)}, u32[]{:S(2)}) collective-permute-start(f32[2,256,256]{2,1,0:T(8,128)S(1)} %pad_maximum_fusion.3.refs_3_), channel_id=1, source_target_pairs={{0,1},{1,0},{2,3},{3,2},{4,5},{5,4},{6,7},{7,6},{8,9},{9,8},{10,11... | collective-permute-start | bytes 1572872 | tf_op jit(solution)/shard_map/ppermute | solution.py:501
  5.6 16.5 %collective-permute-start.2 = (f32[2,256,256]{2,1,0:T(8,128)S(1)}, f32[2,256,256]{2,1,0:T(8,128)S(1)}, u32[]{:S(2)}, u32[]{:S(2)}) collective-permute-start(f32[2,256,256]{2,1,0:T(8,128)S(1)} %pad_maximum_fusion.refs_0_.refs_8_), channel_id=1, source_target_pairs={{1,2},{3,4},{5,6},{7,8},{9,10},{11,12},{13,14},{2,1},{4,3},{6,5},{... | collective-permute-start | bytes 1572872 | tf_op jit(solution)/shard_map/ppermute | solution.py:501
  6.4 27.3 %collective-permute-start.3 = (f32[2,256,256]{2,1,0:T(8,128)S(1)}, f32[2,256,256]{2,1,0:T(8,128)S(1)}, u32[]{:S(2)}, u32[]{:S(2)}) collective-permute-start(f32[2,256,256]{2,1,0:T(8,128)S(1)} %pad_maximum_fusion.1.refs_1_), channel_id=1, source_target_pairs={{1,2},{3,4},{5,6},{7,8},{9,10},{11,12},{13,14},{2,1},{4,3},{6,5},{... | collective-permute-start | bytes 1572872 | tf_op jit(solution)/shard_map/ppermute | solution.py:501
  16.2 6.3 %collective-permute-start.1 = (f32[1,256,256]{2,1,0:T(8,128)S(1)}, f32[1,256,256]{2,1,0:T(8,128)S(1)}, u32[]{:S(2)}, u32[]{:S(2)}) collective-permute-start(f32[1,256,256]{2,1,0:T(8,128)S(1)} %get-tuple-element.43), channel_id=1, source_target_pairs={{0,1},{1,0},{2,3},{3,2},{4,5},{5,4},{6,7},{7,6},{8,9},{9,8},{10,11... | collective-permute-start | bytes 786440 | tf_op jit(solution)/shard_map/ppermute | solution.py:501
  21.3 14.9 %collective-permute-start.4 = (f32[1,256,256]{2,1,0:T(8,128)S(1)}, f32[1,256,256]{2,1,0:T(8,128)S(1)}, u32[]{:S(2)}, u32[]{:S(2)}) collective-permute-start(f32[1,256,256]{2,1,0:T(8,128)S(1)} %get-tuple-element.57), channel_id=1, source_target_pairs={{1,2},{3,4},{5,6},{7,8},{9,10},{11,12},{13,14},{2,1},{4,3},{6,5},{... | collective-permute-start | bytes 786440 | tf_op jit(solution)/shard_map/ppermute | solution.py:501
  28.5 7.7 %collective-permute-start.5 = (f32[1,256,256]{2,1,0:T(8,128)S(1)}, f32[1,256,256]{2,1,0:T(8,128)S(1)}, u32[]{:S(2)}, u32[]{:S(2)}) collective-permute-start(f32[1,256,256]{2,1,0:T(8,128)S(1)} %get-tuple-element.58), channel_id=1, source_target_pairs={{0,1},{1,0},{2,3},{3,2},{4,5},{5,4},{6,7},{7,6},{8,9},{9,8},{10,11... | collective-permute-start | bytes 786440 | tf_op jit(solution)/shard_map/ppermute | solution.py:501

commit v7 on v6

--- a/solution.py
+++ b/solution.py
@@ -317,8 +317,8 @@
 
 def start_kernel(*refs):
     *pairs, table_ref, bounds_ref, tables_ref, factors_ref = refs[:9]
-    first_ref, cross_ref, inplane_ref, reaction_ref, rest_ref, second_ref, near_ref, far_ref = refs[9:17]
-    halves = refs[17:]
+    first_ref, cross_ref, inplane_ref, reaction_ref, rest_ref, second_ref, near_ref, far_ref, own_ref = refs[9:18]
+    halves = refs[18:]
     device = Device((len(pairs) - 1,) + pairs[0].shape[1:])
     depth, rows, tiles = device.depth, device.rows, device.tiles
     put_factors(factors_ref, bounds_ref)
@@ -332,6 +332,9 @@
 
         def body(row, carry):
             values = [tile(pair_ref, 1, c, row) for c in range(tiles)]
+            if q == 0:
+                for c in range(tiles):
+                    put_tile(own_ref, 0, c, row, tile(pair_ref, 0, c, row))
             if q < depth:
                 for c, value in enumerate(values):
                     rest_ref[q + 1, c, pl.ds(row, SUB), :] = value
@@ -512,10 +515,10 @@
     far_first = send(mine[-1], inside)
     near_next = send(mine[1], across)
 
-    tables, factors, *state, near, far = call(
+    tables, factors, *state, near, far, own_labels = call(
         start_kernel,
         (*mine, far_first, tensor_table, bounds),
-        (tables, factors, field, cross_links, inplane_links, reaction, rest, field, plane, plane),
+        (tables, factors, field, cross_links, inplane_links, reaction, rest, field, plane, plane, plane),
         0,
         LIMITS[0],
         10**8,
@@ -527,7 +530,7 @@
 
     *state, far, summed, half = call(
         middle_kernel,
-        (*state, tables, factors, mine[0], far_second, near_first),
+        (*state, tables, factors, own_labels, far_second, near_first),
         tuple(array(*s.shape) for s in state) + (plane, inner, array(*halves[0].shape)),
         6,
         LIMITS[1],

time: 56.2 us -> 56.9 us (1.012)
  blocking collectives: 15.4 us -> 18.4 us
  starting transfers between devices: 13 us -> 10.3 us
    all_to_all x1, blocking collectives: 15.4 us -> 18.4 us  [per_device(): gathered = lax.all_to_all(squares, 'gz', 0, 0, tiled=True)]
    ppermute x6, starting transfers between devices: 13 us -> 10.3 us  [send(): return lax.ppermute(array, 'gz', pairs)]
  transfers between devices with their start and end apart: 6 -> 6, of which waited for: 2 -> 1; matrix products, arithmetic and copies ran while one was open for 0% -> 0% of each run, Pallas kernels for 32% -> 31%
where the time goes in v7:
time: 56.9 us; the launch traced here: 56.6 us
  Pallas kernels  19.5 us (34%)
  blocking collectives  18.4 us (32%)
  starting transfers between devices  10.3 us (18%)
  other arithmetic  2.89 us (5%)
  between operations  2.61 us (5%)
  local copies, waits for them, and re-layouts  2.15 us (4%)
  waiting for transfers between devices  0.77 us (1%)
    pallas_call x4, Pallas kernels, call(): pl.pallas_call(kernel, out_shape=out_shape, in_specs=[vmem] * (len(argume...  19.5 us
    all_to_all x1, blocking collectives, per_device(): gathered = lax.all_to_all(squares, 'gz', 0, 0, tiled=True)  18.4 us
    ppermute x6, starting transfers between devices, send(): return lax.ppermute(array, 'gz', pairs)  10.3 us
    convert_element_type x2, other arithmetic, pair(): lax.dynamic_slice_in_dim(labels, index, 1, 0).astype(jnp.float32)  2.14 us
    dynamic_slice x2, local copies, waits for them, and re-layouts, pair(): lax.dynamic_slice_in_dim(right_side, index, 1, 0)  2.14 us
  transfers between devices with their start and end apart: 6, of which 1 were waited for; matrix products, arithmetic and copies ran while one was open for 0% of the time, Pallas kernels for 31%

profile of v7, /device:TPU:0, one launch (start us, length us, event | category | flops | bytes accessed | tf_op | source)
XLA Modules:
  0.0 56.6 jit_solution(7948453977758068240)
XLA Ops:
  0.6 0.0 copy-start.1
  0.6 0.0 copy-start
  0.7 1.0 %dynamic-slice_convert_fusion.3 = f32[1,256,256]{2,1,0:T(8,128)S(1)} fusion(s32[4,256,256]{2,1,0:T(8,128)} %param.4, s32[]{:T(128)S(6)} %select_n.29), kind=kLoop, calls=%fused_computation.7 | loop fusion | flops 65536 | bytes 524292 | tf_op jit(solution)/shard_map/convert_element_type | solution.py:508
  1.6 1.0 %constant_dynamic-slice_fusion.3 = f32[1,256,256]{2,1,0:T(8,128)S(1)} fusion(f32[4,256,256]{2,1,0:T(8,128)} %param.7, s32[]{:T(128)S(6)} %select_n.29), kind=kLoop, calls=%fused_computation.12 | loop fusion | bytes 524292 | tf_op jit(solution)/shard_map/dynamic_slice | solution.py:509
  2.7 1.2 %dynamic-slice_convert_fusion = (f32[1,256,256]{2,1,0:T(8,128)S(1)}, f32[1,256,256]{2,1,0:T(8,128)S(1)}, f32[1,256,256]{2,1,0:T(8,128)S(1)}) fusion(s32[4,256,256]{2,1,0:T(8,128)} %param.4, s32[]{:T(128)S(6)} %select_n.32, s32[]{:T(128)S(6)} %select_n.31, s32[]{:T(128)S(6)} %select_n.30), kind=kLoop, calls=%fused_computation.4 | loop fusion | flops 196608 | bytes 1572876 | tf_op jit(solution)/shard_map/convert_element_type | solution.py:508
  3.8 1.2 %constant_dynamic-slice_fusion = (f32[1,256,256]{2,1,0:T(8,128)S(1)}, f32[1,256,256]{2,1,0:T(8,128)S(1)}, f32[1,256,256]{2,1,0:T(8,128)S(1)}) fusion(f32[4,256,256]{2,1,0:T(8,128)} %param.7, s32[]{:T(128)S(6)} %select_n.32, s32[]{:T(128)S(6)} %select_n.31, s32[]{:T(128)S(6)} %select_n.30), kind=kLoop, calls=%fused_computation.9 | loop fusion | bytes 1572876 | tf_op jit(solution)/shard_map/dynamic_slice | solution.py:509
  5.1 0.6 collective-permute-start
  5.6 0.7 %collective-permute-start.2 = (f32[2,256,256]{2,1,0:T(8,128)S(1)}, f32[2,256,256]{2,1,0:T(8,128)S(1)}, u32[]{:S(2)}, u32[]{:S(2)}) collective-permute-start(f32[2,256,256]{2,1,0:T(8,128)S(1)} %pad_maximum_fusion.refs_0_), channel_id=1, source_target_pairs={{1,2},{3,4},{5,6},{7,8},{9,10},{11,12},{13,14},{2,1},{4,3},{6,5},{... | collective-permute-start | bytes 1572872 | tf_op jit(solution)/shard_map/ppermute | solution.py:504
  6.4 0.8 %collective-permute-done.refs_4_ = f32[2,256,256]{2,1,0:T(8,128)S(1)} collective-permute-done((f32[2,256,256]{2,1,0:T(8,128)S(1)}, f32[2,256,256]{2,1,0:T(8,128)S(1)}, u32[]{:S(2)}, u32[]{:S(2)}) %collective-permute-start) | collective-permute-done | bytes 524320 | tf_op jit(solution)/shard_map/ppermute | solution.py:504
  7.2 0.0 copy-done.1
  7.2 0.0 copy-done
  7.2 9.0 %shard_map.67 = (f32[8,7,8,128]{3,2,1,0:T(8,128)S(1)}, f32[7,8,128]{2,1,0:T(8,128)S(1)}, f32[7,2,3,272,128]{4,3,2,1,0:T(8,128)S(1)}, f32[6,2,7,272,128]{4,3,2,1,...) custom-call(f32[2,256,256]{2,1,0:T(8,128)S(1)} %pad_maximum_fusion.r, ...), custom_call_target="tpu_custom_call" | custom-call | flops 100000000 | bytes 1048576 | tf_op jit(solution)/shard_map/pallas_call | solution.py:488
  16.2 3.2 %collective-permute-start.1 = (f32[1,256,256]{2,1,0:T(8,128)S(1)}, f32[1,256,256]{2,1,0:T(8,128)S(1)}, u32[]{:S(2)}, u32[]{:S(2)}) collective-permute-start(f32[1,256,256]{2,1,0:T(8,128)S(1)} %get-tuple-element.45), channel_id=1, source_target_pairs={{0,1},{1,0},{2,3},{3,2},{4,5},{5,4},{6,7},{7,6},{8,9},{9,8},{10,11... | collective-permute-start | bytes 786440 | tf_op jit(solution)/shard_map/ppermute | solution.py:504
  19.4 0.7 %collective-permute-start.3 = (f32[2,256,256]{2,1,0:T(8,128)S(1)}, f32[2,256,256]{2,1,0:T(8,128)S(1)}, u32[]{:S(2)}, u32[]{:S(2)}) collective-permute-start(f32[2,256,256]{2,1,0:T(8,128)S(1)} %pad_maximum_fusion.1.refs_1_), channel_id=1, source_target_pairs={{1,2},{3,4},{5,6},{7,8},{9,10},{11,12},{13,14},{2,1},{4,3},{6,5},{... | collective-permute-start | bytes 1572872 | tf_op jit(solution)/shard_map/ppermute | solution.py:504
  20.1 0.9 %collective-permute-start.4 = (f32[1,256,256]{2,1,0:T(8,128)S(1)}, f32[1,256,256]{2,1,0:T(8,128)S(1)}, u32[]{:S(2)}, u32[]{:S(2)}) collective-permute-start(f32[1,256,256]{2,1,0:T(8,128)S(1)} %get-tuple-element.59), channel_id=1, source_target_pairs={{1,2},{3,4},{5,6},{7,8},{9,10},{11,12},{13,14},{2,1},{4,3},{6,5},{... | collective-permute-start | bytes 786440 | tf_op jit(solution)/shard_map/ppermute | solution.py:504
  20.9 0.0 collective-permute-done.2.refs_10_
  21.0 0.0 collective-permute-done.1.refs_9_
  21.0 6.0 %shard_map.68 = (f32[7,2,3,272,128]{4,3,2,1,0:T(8,128)S(1)}, f32[6,2,7,272,128]{4,3,2,1,0:T(8,128)S(1)}, f32[5,2,7,272,128]{4,3,2,1,0:T(8,128)S(1)}, f32[5,2,256...) custom-call(f32[7,2,3,272,128]{4,3,2,1,0:T(8,128)S(1)} %get-tuple-el, ...), custom_call_target="tpu_custom_call", output_to_operand_aliasing={{0}: (0, {}), {1}: (1, {}), {2}: (2, {}), {3}: (3, {}), {4}... | custom-call | flops 100000000 | bytes 1048576 | tf_op jit(solution)/shard_map/pallas_call | solution.py:488
  27.0 4.3 %collective-permute-start.5 = (f32[1,256,256]{2,1,0:T(8,128)S(1)}, f32[1,256,256]{2,1,0:T(8,128)S(1)}, u32[]{:S(2)}, u32[]{:S(2)}) collective-permute-start(f32[1,256,256]{2,1,0:T(8,128)S(1)} %get-tuple-element.60), channel_id=1, source_target_pairs={{0,1},{1,0},{2,3},{3,2},{4,5},{5,4},{6,7},{7,6},{8,9},{9,8},{10,11... | collective-permute-start | bytes 786440 | tf_op jit(solution)/shard_map/ppermute | solution.py:504
  31.3 0.0 collective-permute-done.3.refs_9_
  31.3 2.6 %shard_map.69 = (f32[7,2,3,272,128]{4,3,2,1,0:T(8,128)S(1)}, f32[7,2,3,272,128]{4,3,2,1,0:T(8,128)S(1)}, f32[5,2,256,128]{3,2,1,0:T(8,128)S(1)}, f32[6,2,7,272,1...) custom-call(f32[7,2,3,272,128]{4,3,2,1,0:T(8,128)S(1)} %get-tuple-el, ...), custom_call_target="tpu_custom_call", output_to_operand_aliasing={{0}: (0, {}), {1}: (1, {}), {2}: (2, {}), {3}: (3, {}), {4}... | custom-call | flops 100000000 | bytes 1048576 | tf_op jit(solution)/shard_map/pallas_call | solution.py:488
  33.9 0.0 collective-permute-done.4.refs_7_
  33.9 0.0 collective-permute-done.5.refs_8_
  33.9 1.9 %shard_map.70 = (f32[7,2,3,272,128]{4,3,2,1,0:T(8,128)S(1)}, f32[7,2,3,272,128]{4,3,2,1,0:T(8,128)S(1)}, f32[5,2,256,128]{3,2,1,0:T(8,128)S(1)}, f32[4,256,256]{2,1,0:T(8,128)}, f32[16,128]{1,0:T(8,128)S(1)}) custom-call(f32[7,2,3,272,128]{4,3,2,1,0:T(8,128)S(1)} %get-tuple-element.55.refs_0_, ...), custom_call_target="tpu_custom_call", output_to_operand_aliasing={{0}: (0, {}), {1}: (1, {}), {2}: (2, {})} | custom-call | flops 100000000 | bytes 1048576 | tf_op jit(solution)/shard_map/pallas_call | solution.py:488
  35.8 18.4 %all_to_all.12 = f32[16,1,128]{2,1,0:T(1,128)S(1)} all-to-all(f32[16,1,128]{2,1,0:T(1,128)S(1)} %bitcast.5), channel_id=1, replica_groups=mesh['groups'=2,'gz'=16] {'gz'}, dimensions={0} | all-to-all | bytes 16384 | tf_op jit(solution)/shard_map/all_to_all | solution.py:563
  54.2 0.6 %slice_reduce_fusion = f32[]{:T(128)} fusion(f32[16,128]{1,0:T(8,128)S(1)} %bitcast.6), kind=kLoop, calls=%fused_computation.8 | loop fusion | flops 15 | bytes 68 | tf_op jit(solution)/shard_map/reduce_sum | solution.py:564
  (4 shorter events, 0.1 us)
Async XLA Ops:
  0.6 6.5 %copy-start.1 = (f32[2]{0:T(128)S(1)}, f32[2]{0:T(128)}, u32[]{:S(2)}) copy-start(f32[2]{0:T(128)} %refs_6_.1) | copy-start | bytes 28
  0.6 6.5 %copy-start = (f32[8,7]{1,0:T(8,128)S(1)}, f32[8,7]{1,0:T(8,128)}, u32[]{:S(2)}) copy-start(f32[8,7]{1,0:T(8,128)} %refs_5_.1) | copy-start | bytes 676
  5.1 2.1 %collective-permute-start = (f32[2,256,256]{2,1,0:T(8,128)S(1)}, f32[2,256,256]{2,1,0:T(8,128)S(1)}, u32[]{:S(2)}, u32[]{:S(2)}) collective-permute-start(f32[2,256,256]{2,1,0:T(8,128)S(1)} %pad_maximum_fusion.3.refs_3_), channel_id=1, source_target_pairs={{0,1},{1,0},{2,3},{3,2},{4,5},{5,4},{6,7},{7,6},{8,9},{9,8},{10,11... | collective-permute-start | bytes 1572872 | tf_op jit(solution)/shard_map/ppermute | solution.py:504
  5.6 15.3 %collective-permute-start.2 = (f32[2,256,256]{2,1,0:T(8,128)S(1)}, f32[2,256,256]{2,1,0:T(8,128)S(1)}, u32[]{:S(2)}, u32[]{:S(2)}) collective-permute-start(f32[2,256,256]{2,1,0:T(8,128)S(1)} %pad_maximum_fusion.refs_0_), channel_id=1, source_target_pairs={{1,2},{3,4},{5,6},{7,8},{9,10},{11,12},{13,14},{2,1},{4,3},{6,5},{... | collective-permute-start | bytes 1572872 | tf_op jit(solution)/shard_map/ppermute | solution.py:504
  16.2 4.8 %collective-permute-start.1 = (f32[1,256,256]{2,1,0:T(8,128)S(1)}, f32[1,256,256]{2,1,0:T(8,128)S(1)}, u32[]{:S(2)}, u32[]{:S(2)}) collective-permute-start(f32[1,256,256]{2,1,0:T(8,128)S(1)} %get-tuple-element.45), channel_id=1, source_target_pairs={{0,1},{1,0},{2,3},{3,2},{4,5},{5,4},{6,7},{7,6},{8,9},{9,8},{10,11... | collective-permute-start | bytes 786440 | tf_op jit(solution)/shard_map/ppermute | solution.py:504
  19.4 11.9 %collective-permute-start.3 = (f32[2,256,256]{2,1,0:T(8,128)S(1)}, f32[2,256,256]{2,1,0:T(8,128)S(1)}, u32[]{:S(2)}, u32[]{:S(2)}) collective-permute-start(f32[2,256,256]{2,1,0:T(8,128)S(1)} %pad_maximum_fusion.1.refs_1_), channel_id=1, source_target_pairs={{1,2},{3,4},{5,6},{7,8},{9,10},{11,12},{13,14},{2,1},{4,3},{6,5},{... | collective-permute-start | bytes 1572872 | tf_op jit(solution)/shard_map/ppermute | solution.py:504
  20.1 13.8 %collective-permute-start.4 = (f32[1,256,256]{2,1,0:T(8,128)S(1)}, f32[1,256,256]{2,1,0:T(8,128)S(1)}, u32[]{:S(2)}, u32[]{:S(2)}) collective-permute-start(f32[1,256,256]{2,1,0:T(8,128)S(1)} %get-tuple-element.59), channel_id=1, source_target_pairs={{1,2},{3,4},{5,6},{7,8},{9,10},{11,12},{13,14},{2,1},{4,3},{6,5},{... | collective-permute-start | bytes 786440 | tf_op jit(solution)/shard_map/ppermute | solution.py:504
  27.0 6.9 %collective-permute-start.5 = (f32[1,256,256]{2,1,0:T(8,128)S(1)}, f32[1,256,256]{2,1,0:T(8,128)S(1)}, u32[]{:S(2)}, u32[]{:S(2)}) collective-permute-start(f32[1,256,256]{2,1,0:T(8,128)S(1)} %get-tuple-element.60), channel_id=1, source_target_pairs={{0,1},{1,0},{2,3},{3,2},{4,5},{5,4},{6,7},{7,6},{8,9},{9,8},{10,11... | collective-permute-start | bytes 786440 | tf_op jit(solution)/shard_map/ppermute | solution.py:504
